TPU v7x, 8 devices: a whole 2x2x1 slice. The times are simulated.
8 devices in a mesh: tp: 2 (over z, y), dp: 4 (over x, core).
Axes of the slice: x: 2, y: 2, z: 1, core: 2. Of those that a mesh axis runs over, the one named last changes fastest.
Arguments:
- x_in: bfloat16 [128, 256, 2048], P('dp')
- dy_in: bfloat16 [128, 256, 2048], P('dp')
- positions: int32 [128, 256], P('dp')
- g_attn: bfloat16 [2048], replicated
- q_gain: bfloat16 [128], replicated
- k_gain: bfloat16 [128], replicated
- w_q: bfloat16 [2048, 2048], P(None, 'tp')
- w_k: bfloat16 [2048, 1024], P(None, 'tp')
- w_v: bfloat16 [2048, 1024], P(None, 'tp')
- w_o: bfloat16 [2048, 2048], P('tp')
Outputs:
- output 1: bfloat16 [128, 256, 2048], P('dp')
- output 2: bfloat16 [128, 256, 2048], P('dp')
- output 3: float32 [2048, 2048], P(None, 'tp')
- output 4: float32 [2048, 1024], P(None, 'tp')
- output 5: float32 [2048, 1024], P(None, 'tp')
- output 6: float32 [2048, 2048], P('tp')
- output 7: float32 [128], replicated
- output 8: float32 [128], replicated
- output 9: float32 [2048], replicated
All inputs are finite; a program needn't handle non-finite values.
Results may differ from a plain program's by a relative error of at most 0.0199202.
Values sent between devices are 32-bit elements.
A program may use at most 1 GiB of HBM per device.

v0:
```python
import jax
import jax.numpy as jnp
from jax import lax
from jax.sharding import PartitionSpec as P

EPS = 1e-6
ROPE_THETA = 1000000.0


def rope_tables(positions, head_dim):
    inv_freq = ROPE_THETA ** (-jnp.arange(0, head_dim, 2, dtype=jnp.float32) / head_dim)
    angles = positions.astype(jnp.float32)[:, :, None, None] * inv_freq
    return jnp.cos(angles), jnp.sin(angles)


def head_norm_rope(t_proj, weight, cos_tab, sin_tab):
    t_f32 = t_proj.astype(jnp.float32)
    t_hat = t_f32 * lax.rsqrt(jnp.mean(t_f32 * t_f32, axis=-1, keepdims=True) + EPS)
    scaled = t_hat * weight
    half_dim = scaled.shape[-1] // 2
    low_half = scaled[..., :half_dim]
    high_half = scaled[..., half_dim:]
    return jnp.concatenate([low_half * cos_tab - high_half * sin_tab, high_half * cos_tab + low_half * sin_tab], axis=-1)


def attention_pair(q_rot, k_rot, v_proj, d_out):
    n_batch, n_seq, n_kv, head_dim = k_rot.shape
    group_size = q_rot.shape[2] // n_kv
    q_grp = q_rot.reshape(n_batch, n_seq, n_kv, group_size, head_dim)
    do_grp = d_out.reshape(n_batch, n_seq, n_kv, group_size, head_dim)
    att_scale = head_dim ** -0.5
    scores = jnp.einsum("bqkgd,bskd->bkgqs", q_grp, k_rot, preferred_element_type=jnp.float32) * att_scale
    causal = jnp.arange(n_seq)[:, None] >= jnp.arange(n_seq)[None, :]
    attn_prob = jax.nn.softmax(jnp.where(causal, scores, -jnp.inf), axis=-1)
    prob_bf = attn_prob.astype(jnp.bfloat16)
    attn_out = jnp.einsum("bkgqs,bskd->bqkgd", prob_bf, v_proj, preferred_element_type=jnp.float32).astype(jnp.bfloat16)
    d_val = jnp.einsum("bkgqs,bqkgd->bskd", prob_bf, do_grp, preferred_element_type=jnp.float32).astype(jnp.bfloat16)
    d_prob = jnp.einsum("bqkgd,bskd->bkgqs", do_grp, v_proj, preferred_element_type=jnp.float32)
    d_score = (attn_prob * (d_prob - jnp.sum(d_prob * attn_prob, axis=-1, keepdims=True)) * att_scale).astype(jnp.bfloat16)
    d_query = jnp.einsum("bkgqs,bskd->bqkgd", d_score, k_rot, preferred_element_type=jnp.float32).astype(jnp.bfloat16)
    d_key = jnp.einsum("bkgqs,bqkgd->bskd", d_score, q_grp, preferred_element_type=jnp.float32).astype(jnp.bfloat16)
    return attn_out.reshape(q_rot.shape), d_query.reshape(q_rot.shape), d_key, d_val


def solution(mesh):
    tok_spec = P("dp", None, None)
    col_spec = P(None, "tp")
    row_spec = P("tp", None)

    def per_device(x_in, dy_in, positions, g_attn, q_gain, k_gain, w_q, w_k, w_v, w_o):
        n_batch, n_seq, n_dim = x_in.shape
        head_dim = q_gain.shape[0]
        n_heads = w_q.shape[1] // head_dim
        n_kv = w_k.shape[1] // head_dim
        x_f32 = x_in.astype(jnp.float32).reshape(-1, n_dim)
        inv_rms = lax.rsqrt(jnp.mean(x_f32 * x_f32, axis=-1, keepdims=True) + EPS)
        x_hat = x_f32 * inv_rms
        normed = (x_hat * g_attn.astype(jnp.float32)).astype(jnp.bfloat16)
        q_raw = jnp.dot(normed, w_q, preferred_element_type=jnp.float32).astype(jnp.bfloat16).reshape(n_batch, n_seq, n_heads, head_dim)
        k_raw = jnp.dot(normed, w_k, preferred_element_type=jnp.float32).astype(jnp.bfloat16).reshape(n_batch, n_seq, n_kv, head_dim)
        v_proj = jnp.dot(normed, w_v, preferred_element_type=jnp.float32).astype(jnp.bfloat16).reshape(n_batch, n_seq, n_kv, head_dim)
        cos_tab, sin_tab = rope_tables(positions, head_dim)
        q_rot, q_pull = jax.vjp(lambda t_proj, weight: head_norm_rope(t_proj, weight, cos_tab, sin_tab), q_raw, q_gain.astype(jnp.float32))
        k_rot, k_pull = jax.vjp(lambda t_proj, weight: head_norm_rope(t_proj, weight, cos_tab, sin_tab), k_raw, k_gain.astype(jnp.float32))
        dy_flat = dy_in.reshape(-1, n_dim)
        d_out = jnp.einsum("td,id->ti", dy_flat, w_o, preferred_element_type=jnp.float32).astype(jnp.bfloat16).reshape(n_batch, n_seq, n_heads, head_dim)
        attn_out, dq_rot, dk_rot, dv_proj = attention_pair(q_rot.astype(jnp.bfloat16), k_rot.astype(jnp.bfloat16), v_proj, d_out)
        o_flat = attn_out.reshape(-1, n_heads * head_dim)
        attn_sum = lax.psum(jnp.dot(o_flat, w_o, preferred_element_type=jnp.float32), "tp")
        y_out = (x_f32 + attn_sum).astype(jnp.bfloat16).reshape(x_in.shape)
        dw_o = lax.psum(jnp.einsum("ti,td->id", o_flat, dy_flat, preferred_element_type=jnp.float32), "dp")
        dq_raw, dq_part = q_pull(dq_rot.astype(jnp.float32))
        dk_raw, dk_part = k_pull(dk_rot.astype(jnp.float32))
        dq_flat = dq_raw.reshape(-1, n_heads * head_dim)
        dk_flat = dk_raw.reshape(-1, n_kv * head_dim)
        dv_flat = dv_proj.reshape(-1, n_kv * head_dim)
        dw_q = lax.psum(jnp.einsum("td,ti->di", normed, dq_flat, preferred_element_type=jnp.float32), "dp")
        dw_k = lax.psum(jnp.einsum("td,ti->di", normed, dk_flat, preferred_element_type=jnp.float32), "dp")
        dw_v = lax.psum(jnp.einsum("td,ti->di", normed, dv_flat, preferred_element_type=jnp.float32), "dp")
        d_part = (jnp.einsum("ti,di->td", dq_flat, w_q, preferred_element_type=jnp.float32) + jnp.einsum("ti,di->td", dk_flat, w_k, preferred_element_type=jnp.float32) + jnp.einsum("ti,di->td", dv_flat, w_v, preferred_element_type=jnp.float32))
        d_normed = lax.psum(d_part, "tp")
        dq_gain = lax.psum(dq_part, ("tp", "dp"))
        dk_gain = lax.psum(dk_part, ("tp", "dp"))
        dg_attn = lax.psum(jnp.sum(d_normed * x_hat, axis=0), "dp")
        d_scaled = d_normed * g_attn.astype(jnp.float32)
        dx_f32 = dy_flat.astype(jnp.float32) + inv_rms * (d_scaled - x_hat * jnp.mean(d_scaled * x_hat, axis=-1, keepdims=True))
        dx_out = dx_f32.astype(jnp.bfloat16).reshape(x_in.shape)
        return y_out, dx_out, dw_q, dw_k, dw_v, dw_o, dq_gain, dk_gain, dg_attn

    return jax.shard_map(per_device, mesh=mesh, in_specs=(tok_spec, tok_spec, P("dp", None), P(), P(), P(), col_spec, col_spec, col_spec, row_spec), out_specs=(tok_spec, tok_spec, col_spec, col_spec, col_spec, row_spec, P(), P(), P()), check_vma=False)
```

profile of v0, /device:TPU:0, one launch (start us, length us, event | category | flops | bytes accessed | tf_op | source)
XLA Modules:
  0.0 4689.9 jit_solution(6548603238023140127)
XLA Ops:
  25.0 40.7 convolution_convert_fusion
  93.1 40.6 copy.159
  238.2 42.6 convert_bitcast_fusion
  413.3 36.1 subtract_convert_fusion
  473.5 31.4 fusion.46
  504.9 49.8 %fusion.63 = (f32[32,4,2,256]{3,2,1,0:T(2,128)S(1)}, f32[32,4,2,256,256]{3,4,2,1,0:T(8,128)}) fusion(pred[256,256]{0,1:T(8,128)(4,1)S(1)} %copy-done.19, bf16[32,256,4,64]{3,1,2,0:T(8,128)(2,1)} %get-tuple-element.32, bf16[32,256,4,64]{3,1,2,0:T(8,128)(2,1)} %get-tuple-element.31, bf16[32,256,4,2,64]{4,1,3,2,0:T(8,128)(2,1)} %bitcast.218, ...), kind=kOutput, calls=%fused_computation.110 | convolution fusion | flops 4412407808 | bytes 92602368 | tf_op jit(solution)/shard_map/sub | solution.py:34
  554.7 97.2 %convert_bitcast_fusion.1 = f32[32,256,4,128]{3,1,2,0:T(8,128)} fusion(f32[32,4,256,256,2]{3,2,4,1,0:T(8,128)} %fusion.46, bf16[32,256,4,2,64]{4,1,3,2,0:T(8,128)(2,1)} %bitcast.219, bf16[32,256,4,2,64]{4,1,3,2,0:T(8,128)(2,1)} %bitcast.217, f32[32,4,2,256,256]{3,4,2,1,0:T(8,128)} %get-tuple-element.38, f32[32,4,2,256]{3,2,1,0:T(2,128)S(1)} %get-tuple-element.37), kind=kOutput, calls=%fused_computation.61 | convolution fusion | flops 4454416384 | bytes 168034304 | tf_op jit(solution)/shard_map/bkgqs,bqkgd->bskd/dot_general | solution.py:41
  651.9 98.7 %convert_convert_fusion = f32[32,4,128,2,256]{4,2,3,1,0:T(8,128)} fusion(f32[32,4,256,256,2]{3,2,4,1,0:T(8,128)} %fusion.46, bf16[32,256,4,64]{3,1,2,0:T(8,128)(2,1)} %get-tuple-element.32, bf16[32,256,4,64]{3,1,2,0:T(8,128)(2,1)} %get-tuple-element.31, f32[32,4,2,256,256]{3,4,2,1,0:T(8,128)} %get-tuple-element.38, f32[32,4,2,256]{3,2,1,0:T(2,128)S(1)} %get-tuple-element.37), kind=kOutput, calls=%fused_computation.67 | convolution fusion | flops 4446027776 | bytes 176422912 | tf_op jit(solution)/shard_map/bkgqs,bskd->bqkgd/dot_general | solution.py:40
  750.6 30.2 fusion.44
  976.0 46.3 multiply_add_fusion.1
  1022.3 128.9 %multiply_reduce_fusion = (f32[128]{0:T(128)}, f32[32,256,8]{2,1,0:T(8,128)}) fusion(f32[32,256,8]{2,1,0:T(8,128)} %copy.137, f32[32,256,8,64]{3,2,1,0:T(8,128)} %get-tuple-element.22, f32[32,256,8,64]{3,2,1,0:T(8,128)} %get-tuple-element.21, f32[128]{0:T(128)S(1)} %copy-done.21, f32[32,256,8,128]{3,2,1,0:T(8,128)} %bitcast.197), kind=kLoop, calls=%fused_computation.39 | loop fusion | flops 58654592 | bytes 67634176 | tf_op jit(solution)/shard_map/transpose(jvp())/reduce_sum | solution.py:19
  1156.7 29.2 fusion.65
  1185.9 31.3 fusion.66
  1217.2 39.6 fusion.21
  1256.8 73.0 %add_add_fusion = f32[8192,2048]{1,0:T(8,128)} fusion(f32[8192,2048]{1,0:T(8,128)} %fusion.66, f32[8192,2048]{1,0:T(8,128)} %fusion.65, bf16[2048,1024]{1,0:T(8,128)(2,1)} %param.16, bf16[1024,8,8,128]{3,2,1,0:T(8,128)(2,1)} %bitcast.212), kind=kOutput, calls=%fused_computation.27 | convolution fusion | flops 34393292800 | bytes 222298112 | tf_op jit(solution)/shard_map/ti,di->td/dot_general | solution.py:80
  1330.8 30.9 convert_bitcast_fusion.2
  1391.3 44.0 fusion.64
  1459.3 44.0 fusion.32
  1553.4 43.7 fusion.69
  1623.5 1162.2 %all-reduce.12.cloned.1.call-done = f32[8192,2048]{1,0:T(8,128)} async-done(((f32[8192,2048]{1,0:T(8,128)}), f32[8192,2048]{1,0:T(8,128)}) %all-reduce.12.cloned.1.call-update) | async-done | bytes 67108880 | tf_op jit(solution)/shard_map/psum | solution.py:81
  2785.7 31.1 fusion.15
  2824.5 1417.4 %all-reduce.10.cloned.1.call-done = f32[8192,2048]{1,0:T(8,128)} async-done(((f32[8192,2048]{1,0:T(8,128)}), f32[8192,2048]{1,0:T(8,128)}) %all-reduce.10.cloned.1.call-update) | async-done | bytes 67108880 | tf_op jit(solution)/shard_map/psum | solution.py:69
  4241.8 84.7 %fusion.14 = (bf16[8192,2048]{1,0:T(8,128)(2,1)}, bf16[8192,2048]{1,0:T(8,128)(2,1)}) fusion(bf16[32,256,2048]{2,1,0:T(8,128)(2,1)} %param.10, f32[8192,2048]{1,0:T(8,128)} %all-reduce.12.cloned.1.call-done, f32[8192]{0:T(1024)S(1)} %broadcast_multiply_fusion, f32[2048]{0:T(1024)S(1)} %copy-done.16, f32[8192]{0:T(1024)S(1)} %bitcast.228, ...), kind=kLoop, calls=%fused_computation.21 | loop fusion | flops 184549376 | bytes 268509184 | tf_op jit(solution)/shard_map/convert_element_type | solution.py:87
  4326.5 338.1 %all-reduce.14.cloned.1.call-done = (f32[2048,1024]{1,0:T(8,128)}, f32[2048,512]{1,0:T(8,128)}, f32[2048,512]{1,0:T(8,128)}, f32[1024,2048]{1,0:T(8,128)}) async-done(((f32[2048,1024]{1,0:T(8,128)}, f32[2048,512]{1,0:T(8,128)}, f32[2048,512]{1,0:T(8,128)}, f32[1024,2048]{1,0:T(8,128)}), (f32[2048,1024]{1,0:T(8,128)}, f32[2048,512]{1,0:T(8,128)}, f32[2048,512]{1,0:T(8,128)}, ...) | async-done | bytes 25165840 | tf_op jit(solution)/shard_map/psum | solution.py:77
  (130 shorter events, 663.9 us)
Async XLA Ops:
  7.2 187.0 %copy-start = (bf16[2048,512]{1,0:T(8,128)(2,1)S(1)}, bf16[2048,512]{1,0:T(8,128)(2,1)}, u32[]{:S(2)}) copy-start(bf16[2048,512]{1,0:T(8,128)(2,1)} %param.17) | copy-start | bytes 6291460
  7.2 2778.5 %all-reduce.12.cloned.1.call-start = ((), (), s32[]{:S(2)}) async-start(), calls=%async_computation.1 | async-start | bytes 134217728 | tf_op jit(solution)/shard_map/psum | solution.py:81
  11.5 122.2 %copy-start.14 = (f32[2048]{0:T(1024)}, f32[2048]{0:T(1024)S(1)}, u32[]{:S(2)}) copy-start(f32[2048]{0:T(1024)S(1)} %convert_element_type.110) | copy-start | bytes 24580
  25.0 108.7 %copy-start.12 = (f32[4,2,8,128]{3,1,2,0:T(2,128)}, f32[4,2,8,128]{3,1,2,0:T(2,128)S(1)}, u32[]{:S(2)}) copy-start(f32[4,2,8,128]{3,1,2,0:T(2,128)S(1)} %copy.182) | copy-start | bytes 98308
  325.8 23.2 copy-start.18
  325.8 23.2 copy-start.24
  328.6 37.4 copy-start.6
  331.3 34.8 copy-start.22
  348.9 27.9 copy-start.10
  349.0 27.7 copy-start.8
  388.7 24.6 copy-start.2
  449.4 16.2 copy-start.3
  473.5 31.4 copy-start.19
  554.7 195.9 %copy-start.29 = (f32[32,4,2,256]{3,2,1,0:T(2,128)}, f32[32,4,2,256]{3,2,1,0:T(2,128)S(1)}, u32[]{:S(2)}) copy-start(f32[32,4,2,256]{3,2,1,0:T(2,128)S(1)} %get-tuple-element.37) | copy-start | bytes 786436
  853.7 26.5 copy-start.9
  853.7 26.5 copy-start.23
  880.1 21.1 copy-start.11
  976.0 46.3 copy-start.21
  1022.3 131.7 %copy-start.7 = (f32[32,256,8]{1,2,0:T(8,128)S(1)}, f32[32,256,8]{1,2,0:T(8,128)}, u32[]{:S(2)}) copy-start(f32[32,256,8]{1,2,0:T(8,128)} %copy-done.6) | copy-start | bytes 786436
  1329.8 2912.0 %all-reduce.10.cloned.1.call-start = ((), (), s32[]{:S(2)}) async-start(), calls=%async_computation | async-start | bytes 134217728 | tf_op jit(solution)/shard_map/psum | solution.py:69
  1435.3 3229.3 %all-reduce.14.cloned.1.call-start = ((), (), s32[]{:S(2)}) async-start(), calls=%async_computation.2 | async-start | bytes 50331648 | tf_op jit(solution)/shard_map/psum | solution.py:77
  1597.1 1188.6 %copy-start.13 = (f32[4,2,8,128]{3,1,2,0:T(2,128)S(1)}, f32[4,2,8,128]{3,1,2,0:T(2,128)}, u32[]{:S(2)}) copy-start(f32[4,2,8,128]{3,1,2,0:T(2,128)} %copy-done.12) | copy-start | bytes 98308
  1597.1 1188.6 %copy-start.16 = (f32[2048]{0:T(1024)S(1)}, f32[2048]{0:T(1024)}, u32[]{:S(2)}) copy-start(f32[2048]{0:T(1024)} %copy-done.14) | copy-start | bytes 24580
  4664.6 18.4 copy-start.1
  (12 other events, 82.2 us)
Sparse Core Ops, SparseCore 0:
  1330.0 1455.6 all-reduce.11
  2788.1 1453.6 all-reduce.9
  4245.2 419.3 all-reduce.13
where the time goes:
time: 4700 us; the launch traced here: 4690 us
  waiting for transfers between devices  2920 us (62%)
  matrix products  786 us (17%)
  other arithmetic  595 us (13%)
  local copies, waits for them, and re-layouts  343 us (7%)
    psum x1, waiting for transfers between devices, per_device(): lax.psum(jnp.dot(o_flat, w_o, preferred_element_type=jnp.float32), 'tp')  1420 us
    psum x1, waiting for transfers between devices, per_device(): d_normed = lax.psum(d_part, 'tp')  1160 us
    psum x1, waiting for transfers between devices, per_device(): lax.psum(jnp.einsum('td,ti->di', normed, dq_flat, preferred_element_type=...  338 us
    reduce_sum x2, other arithmetic, head_norm_rope(): scaled = t_hat * weight  150 us
    unnamed x77, local copies, waits for them, and re-layouts  142 us
    dot_general x1, matrix products, attention_pair(): jnp.einsum('bkgqs,bskd->bqkgd', d_score, k_rot, preferred_element_type=jn...  98.7 us
    dot_general x1, matrix products, attention_pair(): jnp.einsum('bkgqs,bqkgd->bskd', d_score, q_grp, preferred_element_type=jn...  97.2 us
  transfers between devices with their start and end apart: 3, of which 3 were waited for; matrix products, arithmetic and copies ran while one was open for 8% of the time, Pallas kernels for 0%

commit v1 on v0

v1 whole, which is shorter than its diff:
```python
import functools
import jax
import jax.numpy as jnp
from jax import lax
from jax.experimental import pallas as pl
from jax.experimental.pallas import tpu as pltpu
from jax.sharding import PartitionSpec as P


EPS = 1e-6
THETA = 1000000.0
F32 = jnp.float32
BF16 = jnp.bfloat16
HD = 128
NT = (((1,), (1,)), ((), ()))
TN = (((0,), (0,)), ((), ()))
NN = (((1,), (0,)), ((), ()))


def dot(a, b, dims=NN):
    return lax.dot_general(a, b, dims, preferred_element_type=F32)


def weave(*lists):
    order = []
    for n, pieces in enumerate(lists):
        total = sum(c for c, _ in pieces) or 1
        at = 0
        for k, (c, f) in enumerate(pieces):
            order.append(((at + c / 2) / total, n, k, f))
            at += c
    for _, _, _, f in sorted(order, key=lambda e: e[:3]):
        f()


CH = 32


def attn_kernel(own, seq, n_grp, sel_ref, *refs):
    if own:
        (x0_ref, xn_ref, dy_ref, cos_ref, sin_ref, gain_ref, qg_ref, kg_ref, wq_ref, wk_ref, wv_ref, wo_ref,
         n_out, o_out, dq_out, dk_out, dv_out, dgq_out, dgk_out) = refs[:19]
        refs = refs[19:]
    else:
        nin_ref, dy_ref, cos_ref, sin_ref, qg_ref, kg_ref, wq_ref, wk_ref, wv_ref, wo_ref, _, _, _, _, o_out, dq_out, dk_out, dv_out = refs[:18]
        refs = refs[18:]
        n_ref = nin_ref
    (wot_ref, qnew_ref, knew_ref, vnew_ref, raw_ref, inv_ref, rot_ref, do_ref, v_ref, s_ref, dp_ref, p_ref, ds_ref, dkf_ref, dqf_ref, st_ref,
     tab_ref, o_ref, dq_ref, dk_ref, dv_ref) = refs[:21]
    if own:
        n_ref, nn_ref, dgq_ref, dgk_ref = refs[21:]
    half = seq // 2
    scale = HD ** -0.5
    log2e = 1.4426950408889634
    step = pl.program_id(0)

    def norm_rows(src, dst):
        def piece(c):
            def run():
                xf = src[c:c + 32, :].astype(F32)
                inv = lax.rsqrt(jnp.mean(xf * xf, axis=-1, keepdims=True) + EPS)
                dst[c:c + 32, :] = (xf * inv * gain_ref[0:1, :]).astype(BF16)

            return (1.5, run)

        return [piece(c) for c in range(0, seq, 32)]

    def proj(g):
        def q():
            t = dot(n_ref[...], wq_ref[:, g * 2 * HD:(g + 1) * 2 * HD])
            for h in range(2):
                qnew_ref[g % 2, h] = t[:, h * HD:(h + 1) * HD].astype(BF16)

        def k():
            t = dot(n_ref[...], wk_ref[:, g * HD:(g + 2) * HD])
            for h in range(2):
                knew_ref[g + h] = t[:, h * HD:(h + 1) * HD].astype(BF16)

        def v():
            t = dot(n_ref[...], wv_ref[:, g * HD:(g + 2) * HD])
            for h in range(2):
                vnew_ref[g + h] = t[:, h * HD:(h + 1) * HD].astype(BF16)

        def do():
            t = dot(dy_ref[...], wot_ref[:, g * 2 * HD:(g + 1) * 2 * HD])
            for h in range(2):
                do_ref[g, h * half:(h + 1) * half, :] = t[:half, h * HD:(h + 1) * HD].astype(BF16)
                do_ref[g, seq + h * half:seq + (h + 1) * half, :] = t[half:, h * HD:(h + 1) * HD].astype(BF16)

        return [(1, q)] + ([(1, k), (1, v)] if g % 2 == 0 else []) + [(1, do)]

    def stacked(h, c):
        return (h * half + c) if c < half else (seq + h * half + c - half)

    def rope(g):
        cs, sn = (tab_ref.at[2], tab_ref.at[3]) if g == n_grp - 1 else (tab_ref.at[0], tab_ref.at[1])

        def size(h, c):
            def run():
                raw = knew_ref[g, c:c + CH, :] if h == 2 else qnew_ref[g % 2, h, c:c + CH, :]
                raw_ref[g, h, c:c + CH, :] = raw
                t = raw.astype(F32)
                inv_ref[g, h, c:c + CH, :] = jnp.broadcast_to(lax.rsqrt(jnp.mean(t * t, axis=-1, keepdims=True) + EPS), t.shape)

            return (0.4, run)

        def turn(h, c):
            def run():
                t = raw_ref[g, h, c:c + CH, :].astype(F32)
                w = (t * inv_ref[g, h, c:c + CH, :]) * (kg_ref if h == 2 else qg_ref)[0:1, :]
                o = 2 * seq + c if h == 2 else stacked(h, c)
                x = pltpu.roll(w, HD // 2, 1)
                co, si = cs[c:c + CH, :], sn[c:c + CH, :]
                rot_ref[g, o:o + CH, 0:HD] = (w * co + x * si).astype(BF16)
                rot_ref[g, o:o + CH, HD:] = (x * co - w * si).astype(BF16)
                if h == 2:
                    v_ref[g, c:c + CH, :] = vnew_ref[g, c:c + CH, :]

            return (0.6, run)

        return [f(h, c) for f in (size, turn) for h in (2, 0, 1) for c in range(0, seq, CH)]

    def scores(g):
        b = g % 2

        def s():
            s_ref[b, 0:seq, 0:half] = dot(rot_ref[g, 0:seq, 0:HD], rot_ref[g, 2 * seq:2 * seq + half, 0:HD], NT)
            s_ref[b, seq:, :] = dot(rot_ref[g, seq:2 * seq, 0:HD], rot_ref[g, 2 * seq:, 0:HD], NT)

        def dp():
            dp_ref[b, 0:seq, 0:half] = dot(do_ref[g, :seq, :], v_ref[g, :half, :], NT)
            dp_ref[b, seq:, :] = dot(do_ref[g, seq:, :], v_ref[g], NT)

        return [(1, s), (1, dp)]

    def soft(g):
        b = g % 2
        c2 = scale * log2e

        def part(blk, c):
            return slice(blk * seq + c, blk * seq + c + CH), half if blk == 0 else seq

        def masked(blk, c, s):
            row_id = lax.broadcasted_iota(jnp.int32, (CH, half), 0) + (c % half)
            keep = row_id >= lax.broadcasted_iota(jnp.int32, (CH, half), 1)
            if blk == 0:
                return jnp.where(keep, s, -jnp.inf)
            return jnp.concatenate([s[:, :half], jnp.where(keep, s[:, half:], -jnp.inf)], axis=1)

        def wide(ref, rows, width):
            t = ref[rows, :]
            return t if width == half else jnp.concatenate([t, t], axis=1)

        def top(blk, c):
            rows, width = part(blk, c)

            def run():
                m = jnp.max(masked(blk, c, s_ref[b, rows, 0:width]), axis=-1, keepdims=True)
                st_ref[0, rows, :] = jnp.broadcast_to(m * c2, (CH, HD))

            return (0.4 + 0.4 * blk, run)

        def power(blk, c):
            rows, width = part(blk, c)

            def run():
                e = jnp.exp2(masked(blk, c, s_ref[b, rows, 0:width] * c2) - wide(st_ref.at[0], rows, width))
                s_ref[b, rows, 0:width] = e
                st_ref[1, rows, :] = jnp.broadcast_to(1.0 / jnp.sum(e, axis=-1, keepdims=True), (CH, HD))

            return (0.8 + 0.8 * blk, run)

        def prob(blk, c):
            rows, width = part(blk, c)

            def run():
                pr = s_ref[b, rows, 0:width] * wide(st_ref.at[1], rows, width)
                s_ref[b, rows, 0:width] = pr
                p_ref[b, rows, 0:width] = pr.astype(BF16)
                st_ref[2, rows, :] = jnp.broadcast_to(jnp.sum(pr * dp_ref[b, rows, 0:width], axis=-1, keepdims=True), (CH, HD))

            return (0.8 + 0.8 * blk, run)

        def last(blk, c):
            rows, width = part(blk, c)

            def run():
                d = dp_ref[b, rows, 0:width] - wide(st_ref.at[2], rows, width)
                ds_ref[b, rows, 0:width] = (s_ref[b, rows, 0:width] * d * scale).astype(BF16)

            return (0.8 + 0.8 * blk, run)

        return [f(blk, c) for f in (top, power, prob, last) for blk in range(2) for c in range(0, seq, CH)]

    def grads(g):
        b = g % 2
        col, kcol = g * 2 * HD, g * HD

        def dq():
            dqf_ref[b, 0:seq, :] = dot(ds_ref[b, 0:seq, 0:half], rot_ref[g, 2 * seq:2 * seq + half, :])
            dqf_ref[b, seq:, :] = dot(ds_ref[b, seq:, :], rot_ref[g, 2 * seq:, :])

        def dk():
            tb = dot(ds_ref[b, seq:, :], rot_ref[g, seq:2 * seq, :], TN)
            ta = dot(ds_ref[b, 0:seq, 0:half], rot_ref[g, 0:seq, :], TN)
            dkf_ref[b, :half, :] = tb[:half] + ta
            dkf_ref[b, half:, :] = tb[half:]

        def o():
            ta = dot(p_ref[b, 0:seq, 0:half], v_ref[g, :half, :])
            tb = dot(p_ref[b, seq:, :], v_ref[g])
            for h in range(2):
                o_ref[0:half, col + h * HD:col + (h + 1) * HD] = ta[h * half:(h + 1) * half].astype(BF16)
                o_ref[half:seq, col + h * HD:col + (h + 1) * HD] = tb[h * half:(h + 1) * half].astype(BF16)

        def dv():
            tb = dot(p_ref[b, seq:, :], do_ref[g, seq:, :], TN)
            ta = dot(p_ref[b, 0:seq, 0:half], do_ref[g, :seq, :], TN)
            dv_ref[0:half, kcol:kcol + HD] = (tb[:half] + ta).astype(BF16)
            dv_ref[half:seq, kcol:kcol + HD] = tb[half:].astype(BF16)

        return [(1, dq), (1, dk), (1, o), (1, dv)]

    def back(g):
        b = g % 2

        def place(h, c):
            if h == 2:
                return dkf_ref, c, dk_ref, g * HD, kg_ref
            return dqf_ref, stacked(h, c), dq_ref, (2 * g + h) * HD, qg_ref

        def turn(h, c):
            src, o, _, _, g_ref = place(h, c)

            def run():
                d = src[b, o:o + CH, :].astype(BF16).astype(F32)
                that = raw_ref[g, h, c:c + CH, :].astype(F32) * inv_ref[g, h, c:c + CH, :]
                du = d[:, :HD] * tab_ref[2, c:c + CH, :] - d[:, HD:] * tab_ref[3, c:c + CH, :]
                src[b, o:o + CH, 0:HD] = du
                pr = du * that
                if own:
                    dg_ref = dgk_ref if h == 2 else dgq_ref
                    dg_ref[...] += jnp.sum(pr.reshape(CH // 8, 8, HD), axis=0)
                st_ref[3 + h, c:c + CH, :] = jnp.broadcast_to(jnp.mean(pr * g_ref[0:1, :], axis=-1, keepdims=True), (CH, HD))

            return (0.6, run)

        def out(h, c):
            src, o, out_ref, col, g_ref = place(h, c)

            def run():
                inv = inv_ref[g, h, c:c + CH, :]
                that = raw_ref[g, h, c:c + CH, :].astype(F32) * inv
                out_ref[c:c + CH, col:col + HD] = (inv * (src[b, o:o + CH, 0:HD] * g_ref[0:1, :] - that * st_ref[3 + h, c:c + CH, :])).astype(BF16)

            return (0.5, run)

        return [f(h, c) for f in (turn, out) for h in (0, 1, 2) for c in range(0, seq, CH)]

    @pl.when(step == 0)
    def _():
        for c in range(0, wo_ref.shape[0], 256):
            for d in range(0, wo_ref.shape[1], 256):
                wot_ref[d:d + 256, c:c + 256] = wo_ref[c:c + 256, d:d + 256].T
        if own:
            weave(norm_rows(x0_ref, n_ref))

    tab_ref[2:4] = tab_ref[0:2]
    tab_ref[0] = cos_ref[...]
    tab_ref[1] = sin_ref[...]
    if own:
        norms = norm_rows(xn_ref, nn_ref)
    for g in range(n_grp):
        vec = soft((g - 3) % n_grp)
        sc = scores((g - 2) % n_grp)
        vec = vec + rope((g - 1) % n_grp)
        if own:
            vec += norms[g * len(norms) // n_grp:(g + 1) * len(norms) // n_grp]
        vec += back(g)
        gr = grads(g)
        for _, f in gr[:2]:
            f()
        weave(vec, sc + gr[2:] + proj(g))

    for dst, src in ((o_out, o_ref), (dq_out, dq_ref), (dk_out, dk_ref), (dv_out, dv_ref)):
        dst[0] = src[...]
    if own:
        n_out[...] = n_ref[...]
        n_ref[...] = nn_ref[...]
        keep = step > 0
        for dst, acc in ((dgq_out, dgq_ref), (dgk_out, dgk_ref)):
            acc[...] = jnp.where(keep, acc[...], 0.0)
            dst[...] = acc[...]


def attn_call(own, sel, x, dy, cosd, sind, gain, qg, kg, wq, wk, wv, wo, prev=None, seq=256):
    T, D = x.shape
    nq, nk = wq.shape[1], wk.shape[1]
    n_grp = nk // HD
    rows = T // seq
    const = lambda *b: pl.BlockSpec(b, lambda i, s: (0,) * len(b), pipeline_mode=pl.Buffered(1))
    now = lambda c: pl.BlockSpec((seq, c), lambda i, s: (jnp.minimum(i, rows - 1), 0))
    nxt = lambda c: pl.BlockSpec((seq, c), lambda i, s: (jnp.minimum(i + 1, rows - 1), 0))
    out3 = lambda c: pl.BlockSpec((1, seq, c), lambda i, s: (s[0], jnp.maximum(i - 1, 0), 0))
    mid = [now(D), now(HD), now(HD)]
    tail = [const(1, HD), const(1, HD), const(D, nq), const(D, nk), const(D, nk), const(nq, D)]
    shapes = [jax.ShapeDtypeStruct((2, T, c), BF16) for c in (nq, nq, nk, nk)]
    specs = [out3(nq), out3(nq), out3(nk), out3(nk)]
    aliases = {}
    if own:
        in_specs = [const(seq, D), nxt(D)] + mid + [const(1, D)] + tail
        args = [x, x, dy, cosd, sind, gain, qg, kg, wq, wk, wv, wo]
        shapes = [jax.ShapeDtypeStruct((T, D), BF16)] + shapes + [jax.ShapeDtypeStruct((8, HD), F32)] * 2
        specs = [now(D)] + specs + [pl.BlockSpec((8, HD), lambda i, s: (0, 0))] * 2
    else:
        in_specs = [now(D)] + mid + tail + [pl.BlockSpec(memory_space=pl.ANY)] * 4
        args = [x, dy, cosd, sind, qg, kg, wq, wk, wv, wo]
        aliases = {1 + len(args) + i: i for i in range(4)}
        args += list(prev)
    flops = 2 * T * D * (nq + 2 * nk + nq) + 12 * T * nq * seq
    return pl.pallas_call(
        functools.partial(attn_kernel, own, seq, n_grp),
        grid_spec=pltpu.PrefetchScalarGridSpec(
            num_scalar_prefetch=1,
            grid=(rows + 1,),
            in_specs=in_specs,
            out_specs=specs,
            scratch_shapes=[
                pltpu.VMEM((D, nq), BF16),
                pltpu.VMEM((2, 2, seq, HD), BF16),
                pltpu.VMEM((n_grp, seq, HD), BF16),
                pltpu.VMEM((n_grp, seq, HD), BF16),
                pltpu.VMEM((n_grp, 3, seq, HD), BF16),
                pltpu.VMEM((n_grp, 3, seq, HD), F32),
                pltpu.VMEM((n_grp, 3 * seq, 2 * HD), BF16),
                pltpu.VMEM((n_grp, 2 * seq, HD), BF16),
                pltpu.VMEM((n_grp, seq, HD), BF16),
                pltpu.VMEM((2, 2 * seq, seq), F32),
                pltpu.VMEM((2, 2 * seq, seq), F32),
                pltpu.VMEM((2, 2 * seq, seq), BF16),
                pltpu.VMEM((2, 2 * seq, seq), BF16),
                pltpu.VMEM((2, seq, 2 * HD), F32),
                pltpu.VMEM((2, 2 * seq, 2 * HD), F32),
                pltpu.VMEM((6, 2 * seq, HD), F32),
                pltpu.VMEM((4, seq, HD), F32),
            ] + [pltpu.VMEM((seq, c), BF16) for c in (nq, nq, nk, nk)]
            + ([pltpu.VMEM((seq, D), BF16)] * 2 + [pltpu.VMEM((8, HD), F32)] * 2 if own else []),
        ),
        out_shape=shapes,
        input_output_aliases=aliases,
        compiler_params=pltpu.CompilerParams(dimension_semantics=("arbitrary",), vmem_limit_bytes=56 << 20),
        cost_estimate=pl.CostEstimate(flops=flops, bytes_accessed=T * D * 6 + T * (2 * nq + 2 * nk) * 2, transcendentals=T * nq * 2),
        name="attn_own" if own else "attn_other",
    )(sel, *args)


def unpack_kernel(f_ref, q_ref, k_ref, v_ref, o_ref):
    d = q_ref.shape[0]
    nq, nk = q_ref.shape[1], k_ref.shape[1]
    q_ref[...] = f_ref[0, 0:d, 0:nq].astype(BF16)
    k_ref[...] = f_ref[0, 0:d, nq:nq + nk].astype(BF16)
    v_ref[...] = f_ref[0, 0:d, nq + nk:].astype(BF16)
    o_ref[...] = f_ref[0, d:, :].astype(BF16)


def unpack_call(gathered, D, nq, nk):
    n, r, c = gathered.shape
    part = lambda a, b: pl.BlockSpec((a // n, b), lambda i: (i, 0))
    return pl.pallas_call(
        unpack_kernel,
        grid=(n,),
        in_specs=[pl.BlockSpec((1, r, c), lambda i: (i, 0, 0), pipeline_mode=pl.Buffered(1))],
        out_specs=[part(D, nq), part(D, nk), part(D, nk), part(nq, D)],
        out_shape=[jax.ShapeDtypeStruct(s, BF16) for s in ((D, nq), (D, nk), (D, nk), (nq, D))],
        compiler_params=pltpu.CompilerParams(dimension_semantics=("arbitrary",), vmem_limit_bytes=60 << 20),
        cost_estimate=pl.CostEstimate(flops=n * r * c, bytes_accessed=n * r * c * 6, transcendentals=0),
        name="unpack",
    )(gathered)


def dw_kernel(n_out, sel_ref, a_ref, *refs):
    a = a_ref[0] if len(a_ref.shape) == 3 else a_ref[...]
    for b_ref, out_ref in zip(refs[:n_out], refs[n_out:]):
        b = b_ref[0] if len(b_ref.shape) == 3 else b_ref[...]

        @pl.when(pl.program_id(0) == 0)
        def _():
            out_ref[...] = jnp.zeros_like(out_ref)

        out_ref[...] += dot(a, b, TN)


def dw_call(sel, a, bs, tile=1024):
    def spec(v):
        if v.ndim == 3:
            return pl.BlockSpec((1, tile, v.shape[2]), lambda i, s: (s[0], i, 0))
        return pl.BlockSpec((tile, v.shape[1]), lambda i, s: (i, 0))

    T, M = a.shape[-2:]
    width = sum(b.shape[-1] for b in bs)
    return pl.pallas_call(
        functools.partial(dw_kernel, len(bs)),
        grid_spec=pltpu.PrefetchScalarGridSpec(
            num_scalar_prefetch=1,
            grid=(T // tile,),
            in_specs=[spec(a)] + [spec(b) for b in bs],
            out_specs=[pl.BlockSpec((M, b.shape[-1]), lambda i, s: (0, 0)) for b in bs],
        ),
        out_shape=[jax.ShapeDtypeStruct((M, b.shape[-1]), F32) for b in bs],
        compiler_params=pltpu.CompilerParams(dimension_semantics=("arbitrary",), vmem_limit_bytes=56 << 20),
        cost_estimate=pl.CostEstimate(flops=2 * T * M * width, bytes_accessed=2 * T * (M + width) + 4 * M * width, transcendentals=0),
    )(sel, a, *bs)


def out_kernel(m, sel_ref, x_ref, dy_ref, o_ref, dq_ref, dk_ref, dv_ref, gain_ref, *refs):
    own, oth = refs[:4], refs[4:8]
    y_out, dx_out, dg_out, wq_ref, wk_ref, wv_ref, wo_ref, dn_ref, oc_ref, y_ref, dx_ref, st_ref, dg_ref, sem = refs[8:]
    D = x_ref.shape[1]
    step = pl.program_id(0)
    ME = sel_ref[0]

    @pl.when(step == 0)
    def _():
        copies = []
        for k, dst in enumerate((wq_ref, wk_ref, wv_ref, wo_ref)):
            copies.append(pltpu.make_async_copy(own[k], dst.at[ME], sem.at[k]))
            copies.append(pltpu.make_async_copy(oth[k], dst.at[1 - ME], sem.at[4 + k]))
        for c in copies:
            c.start()
        for c in copies:
            c.wait()
        dg_ref[...] = jnp.zeros_like(dg_ref)

    CR = 32
    NC = 256

    def stat(c):
        def run():
            xf = x_ref[c:c + CR, :].astype(F32)
            st_ref[0, c:c + CR, :] = jnp.broadcast_to(lax.rsqrt(jnp.mean(xf * xf, axis=-1, keepdims=True) + EPS), (CR, HD))
            st_ref[1, c:c + CR, :] = jnp.zeros((CR, HD), F32)

        return (1, run)

    def keep(c):
        def run():
            for s in range(2):
                oc_ref[s, c:c + CR, :] = o_ref[s, c:c + CR, :]

        return (0.5, run)

    def dn_dot(n):
        def run():
            cols = slice(n * NC, (n + 1) * NC)
            t = None
            for s in range(2):
                for a_ref, w_ref in ((dq_ref, wq_ref), (dk_ref, wk_ref), (dv_ref, wv_ref)):
                    u = dot(a_ref[s], w_ref[s, cols, :], NT)
                    t = u if t is None else t + u
            dn_ref[:, cols] = t

        return (1, run)

    def wide(v):
        return jnp.concatenate([v] * (NC // HD), axis=1)

    def first(n, c):
        def run():
            cols = slice(n * NC, (n + 1) * NC)
            w = dn_ref[c:c + CR, cols] * (x_ref[c:c + CR, cols].astype(F32) * wide(st_ref[0, c:c + CR, :]))
            dg_ref[:, cols] += jnp.sum(w.reshape(CR // 8, 8, NC), axis=0)
            w = w * gain_ref[0:1, cols]
            st_ref[1, c:c + CR, :] += w[:, :HD] + w[:, HD:]

        return (1, run)

    def mean(c):
        def run():
            st_ref[2, c:c + CR, :] = jnp.broadcast_to(jnp.sum(st_ref[1, c:c + CR, :], axis=-1, keepdims=True) * (1.0 / D), (CR, HD))

        return (0.2, run)

    def second(n, c):
        def run():
            cols = slice(n * NC, (n + 1) * NC)
            inv = wide(st_ref[0, c:c + CR, :])
            xh = x_ref[c:c + CR, cols].astype(F32) * inv
            e = dn_ref[c:c + CR, cols] * gain_ref[0:1, cols]
            dx_ref[c:c + CR, cols] = (dy_ref[c:c + CR, cols].astype(F32) + inv * (e - xh * wide(st_ref[2, c:c + CR, :]))).astype(BF16)

        return (1, run)

    def y_dot(n):
        def run():
            cols = slice(n * NC, (n + 1) * NC)
            t = dot(oc_ref[0], wo_ref[0, :, cols]) + dot(oc_ref[1], wo_ref[1, :, cols])
            y_ref[:, cols] = (x_ref[:, cols].astype(F32) + t).astype(BF16)

        return (1, run)

    nn = D // NC
    rows = range(0, m, CR)
    dn = [dn_dot(n) for n in range(nn)]
    for _, f in dn[:1]:
        f()
    head = [stat(c) for c in rows] + [keep(c) for c in rows]
    weave(head, [dn[1]])
    for n in range(2, nn):
        weave([first(n - 2, c) for c in rows], [dn[n]])
    yd = [y_dot(n) for n in range(nn)]
    weave([first(nn - 2, c) for c in rows], yd[:1])
    weave([first(nn - 1, c) for c in rows] + [mean(c) for c in rows], yd[1:2])
    weave([second(n, c) for n in range(nn) for c in rows], yd[2:])
    y_out[...] = y_ref[...]
    dx_out[...] = dx_ref[...]
    dg_out[...] = dg_ref[...]


def out_call(sel, x, dy, o, dq, dk, dv, gain, own, oth, m=256):
    T, D = x.shape
    nq, nk = dq.shape[2], dk.shape[2]
    row = pl.BlockSpec((m, D), lambda i, s: (i, 0))
    two = lambda c: pl.BlockSpec((2, m, c), lambda i, s: (0, i, 0))
    hbm = pl.BlockSpec(memory_space=pl.ANY)
    return pl.pallas_call(
        functools.partial(out_kernel, m),
        grid_spec=pltpu.PrefetchScalarGridSpec(
            num_scalar_prefetch=1,
            grid=(T // m,),
            in_specs=[row, row, two(nq), two(nq), two(nk), two(nk), pl.BlockSpec((1, D), lambda i, s: (0, 0), pipeline_mode=pl.Buffered(1))] + [hbm] * 8,
            out_specs=[row, row, pl.BlockSpec((8, D), lambda i, s: (0, 0))],
            scratch_shapes=[
                pltpu.VMEM((2, D, nq), BF16),
                pltpu.VMEM((2, D, nk), BF16),
                pltpu.VMEM((2, D, nk), BF16),
                pltpu.VMEM((2, nq, D), BF16),
                pltpu.VMEM((m, D), F32),
                pltpu.VMEM((2, m, nq), BF16),
                pltpu.VMEM((m, D), BF16),
                pltpu.VMEM((m, D), BF16),
                pltpu.VMEM((3, m, HD), F32),
                pltpu.VMEM((8, D), F32),
                pltpu.SemaphoreType.DMA((8,)),
            ],
        ),
        out_shape=[jax.ShapeDtypeStruct((T, D), BF16)] * 2 + [jax.ShapeDtypeStruct((8, D), F32)],
        compiler_params=pltpu.CompilerParams(dimension_semantics=("arbitrary",), vmem_limit_bytes=60 << 20),
        cost_estimate=pl.CostEstimate(flops=2 * T * D * 2 * (2 * nq + 2 * nk), bytes_accessed=T * D * 8 + T * (4 * nq + 4 * nk) * 2, transcendentals=T),
        name="out",
    )(sel, x, dy, o, dq, dk, dv, gain, *own, *oth)


def solution(mesh):
    tok_spec = P("dp", None, None)
    col_spec = P(None, "tp")
    row_spec = P("tp", None)
    n_dp = mesh.shape["dp"]

    def per_device(x_in, dy_in, positions, g_attn, q_gain, k_gain, w_q, w_k, w_v, w_o):
        n_batch, n_seq, D = x_in.shape
        T = n_batch * n_seq
        nq, nk = w_q.shape[1], w_k.shape[1]
        x, dy = x_in.reshape(T, D), dy_in.reshape(T, D)
        me = lax.axis_index("tp").astype(jnp.int32)
        own = me.reshape(1)
        other = 1 - own

        part = lax.axis_index("dp") % 2
        cut = lambda w: lax.dynamic_slice_in_dim(w, part * (w.shape[0] // 2), w.shape[0] // 2, 0)
        share = jnp.concatenate([jnp.concatenate([cut(w_q), cut(w_k), cut(w_v)], axis=1), cut(w_o)], axis=0).astype(F32)
        share = lax.ppermute(share, "tp", [(0, 1), (1, 0)])
        gathered = lax.all_gather(share, "dp", axis_index_groups=[[2 * i, 2 * i + 1] for i in range(n_dp // 2)])

        inv_freq = THETA ** (-jnp.arange(0, HD, 2, dtype=F32) / HD)
        angles = positions.reshape(T, 1).astype(F32) * inv_freq
        cos, sin = jnp.cos(angles), jnp.sin(angles)
        cosd, sind = jnp.concatenate([cos, cos], axis=1), jnp.concatenate([-sin, sin], axis=1)
        gain = g_attn.astype(F32).reshape(1, D)
        qg, kg = q_gain.astype(F32).reshape(1, HD), k_gain.astype(F32).reshape(1, HD)

        n, o, dq, dk, dv, dgq, dgk = attn_call(True, own, x, dy, cosd, sind, gain, qg, kg, w_q, w_k, w_v, w_o, seq=n_seq)
        (dw_o,) = dw_call(own, o, [dy])
        (dw_q,) = dw_call(own, n, [dq])
        dw_k, dw_v = dw_call(own, n, [dk, dv])
        dw_o, dw_q, dw_k, dw_v = lax.psum((dw_o, dw_q, dw_k, dw_v), "dp")
        q_sum, k_sum = lax.psum((jnp.sum(dgq, axis=0), jnp.sum(dgk, axis=0)), ("tp", "dp"))

        theirs = unpack_call(gathered, D, nq, nk)
        o, dq, dk, dv = attn_call(False, other, n, dy, cosd, sind, gain, qg, kg, *theirs, prev=(o, dq, dk, dv), seq=n_seq)
        y, dx, dg = out_call(own, x, dy, o, dq, dk, dv, gain, (w_q, w_k, w_v, w_o), theirs)
        g_sum = lax.psum(jnp.sum(dg, axis=0), "dp")
        return y.reshape(x_in.shape), dx.reshape(x_in.shape), dw_q, dw_k, dw_v, dw_o, q_sum, k_sum, g_sum

    return jax.shard_map(per_device, mesh=mesh, in_specs=(tok_spec, tok_spec, P("dp", None), P(), P(), P(), col_spec, col_spec, col_spec, row_spec), out_specs=(tok_spec, tok_spec, col_spec, col_spec, col_spec, row_spec, P(), P(), P()), check_vma=False)
```

time: 4700 us -> 1250 us (0.27)
  waiting for transfers between devices: 2920 us -> 270 us
  Pallas kernels: 0 us -> 835 us
  matrix products: 786 us -> 0 us
  other arithmetic: 595 us -> 59 us
  local copies, waits for them, and re-layouts: 343 us -> 24.9 us
    psum x3 -> x1, waiting for transfers between devices: 2920 us -> 0.01 us  [per_device(): dw_o, dw_q, dw_k, dw_v = lax.psum((dw_o, dw_q, dw_k, dw_v), 'dp')]
    pallas_call x0 -> x7, Pallas kernels: none -> 835 us  [the longest x2 425 us: attn_call(): pl.pallas_call(functools.partial(attn_kernel, own, seq, n_grp), grid_spec...]
    dot_general x17 -> x0, matrix products: 737 us -> none  [the longest x1 98.7 us: attention_pair(): jnp.einsum('bkgqs,bskd->bqkgd', d_score, k_rot, preferred_element_type=jn...]
    ppermute x0 -> x1, waiting for transfers between devices: none -> 270 us  [per_device(): share = lax.ppermute(share, 'tp', [(0, 1), (1, 0)])]
    reduce_sum x6 -> x3, other arithmetic: 225 us -> 0.89 us  [the longest x1 0.86 us: per_device(): g_sum = lax.psum(jnp.sum(dg, axis=0), 'dp')]
    convert_element_type x9 -> x1, other arithmetic: 195 us -> 25.4 us  [per_device(): jnp.concatenate([jnp.concatenate([cut(w_q), cut(w_k), cut(w_v)], axis=1),...]
    unnamed x77 -> x31, local copies, waits for them, and re-layouts: 142 us -> 22.6 us
    another operation x4 -> x0, local copies, waits for them, and re-layouts: 92 us -> none  [the longest x2 67.9 us: attention_pair(): do_grp = d_out.reshape(n_batch, n_seq, n_kv, group_size, head_dim)]
  transfers between devices with their start and end apart: 3 -> 3, of which waited for: 3 -> 1; matrix products, arithmetic and copies ran while one was open for 8% -> 3% of each run, Pallas kernels for 0% -> 67%
where the time goes in v1:
time: 1250 us; the launch traced here: 1240 us
  Pallas kernels  835 us (67%)
  waiting for transfers between devices  270 us (22%)
  other arithmetic  59 us (5%)
  blocking collectives  32.2 us (3%)
  local copies, waits for them, and re-layouts  24.9 us (2%)
  between operations  16.1 us (1%)
    pallas_call x2, Pallas kernels, attn_call(): pl.pallas_call(functools.partial(attn_kernel, own, seq, n_grp), grid_spec...  425 us
    ppermute x1, waiting for transfers between devices, per_device(): share = lax.ppermute(share, 'tp', [(0, 1), (1, 0)])  270 us
    pallas_call x1, Pallas kernels, out_call(): pl.pallas_call(functools.partial(out_kernel, m), grid_spec=pltpu.Prefetch...  249 us
    pallas_call x3, Pallas kernels, dw_call(): pl.pallas_call(functools.partial(dw_kernel, len(bs)), grid_spec=pltpu.Pre...  145 us
    convert_element_type x1, other arithmetic, per_device(): jnp.concatenate([jnp.concatenate([cut(w_q), cut(w_k), cut(w_v)], axis=1),...  25.4 us
  transfers between devices with their start and end apart: 3, of which 1 were waited for; matrix products, arithmetic and copies ran while one was open for 3% of the time, Pallas kernels for 67%

profile of v1, /device:TPU:0, one launch (start us, length us, event | category | flops | bytes accessed | tf_op | source)
XLA Modules:
  0.0 1240.6 jit_solution(16266250734444286388)
XLA Ops:
  8.1 2.0 constant_dynamic-slice_fusion
  10.1 0.8 copy-done.2
  12.4 25.4 %maximum_convert_fusion = f32[1536,2048]{1,0:T(8,128)} fusion(bf16[512,2048]{1,0:T(8,128)(2,1)S(1)} %constant_dynamic-slice_fusion, bf16[1024,512]{1,0:T(8,128)(2,1)S(1)} %get-tuple-element.62, bf16[1024,512]{1,0:T(8,128)(2,1)S(1)} %get-tuple-element.63, bf16[1024,1024]{1,0:T(8,128)(2,1)S(1)} %constant_dynamic-slice_fusion.3), kind=kLoop, calls=%fused_computation | loop fusion | flops 25165824 | bytes 18874368 | tf_op jit(solution)/shard_map/convert_element_type | solution.py:570
  37.8 3.3 collective-permute-start
  41.8 270.0 %collective-permute-done = f32[1536,2048]{1,0:T(8,128)} collective-permute-done((f32[1536,2048]{1,0:T(8,128)}, f32[1536,2048]{1,0:T(8,128)}, u32[]{:S(2)}, u32[]{:S(2)}) %collective-permute-start) | collective-permute-done | bytes 12582944 | tf_op jit(solution)/shard_map/ppermute | solution.py:571
  313.0 18.1 %fusion = (f32[8192,64]{1,0:T(8,128)S(1)}, f32[8192,64]{1,0:T(8,128)}, f32[8192,64]{1,0:T(8,128)}) fusion(f32[64]{0:T(128)S(1)} %multiply_power_fusion, f32[8192]{0:T(1024)S(1)} %bitcast.19), kind=kLoop, calls=%fused_computation.5 | loop fusion | flops 1048576 | bytes 6324480 | tf_op jit(solution)/shard_map/neg | solution.py:577
  331.0 13.5 %pad_maximum_fusion = (f32[8192,128]{1,0:T(8,128)}, f32[8192,128]{1,0:T(8,128)}) fusion(f32[8192,64]{1,0:T(8,128)} %get-tuple-element.57, f32[8192,64]{1,0:T(8,128)} %get-tuple-element.56, f32[8192,64]{1,0:T(8,128)S(1)} %get-tuple-element.55), kind=kLoop, calls=%fused_computation.3 | loop fusion | flops 2097152 | bytes 14680064 | tf_op jit(solution)/shard_map/concatenate | solution.py:577
  344.5 218.5 %attn_own.1 = (bf16[8192,2048]{1,0:T(8,128)(2,1)}, bf16[2,8192,1024]{2,1,0:T(8,128)(2,1)}, bf16[2,8192,1024]{2,1,0:T(8,128)(2,1)}, bf16[2,8192,512]{2,1,0:T(8,12...) custom-call(s32[1]{0:T(128)} %bitcast.sel_ref, bf16[8192,2048]{1,0:T(8,128)(2,1)} %bitcast.22, ...), custom_call_target="tpu_custom_call" | custom-call | flops 128849018880 | bytes 150994944 | tf_op jit(solution)/shard_map/attn_own/pallas_call | solution.py:321
  563.0 46.5 %shard_map.171 = f32[1024,2048]{1,0:T(8,128)} custom-call(s32[1]{0:T(128)} %bitcast.sel_ref, bf16[2,8192,1024]{2,1,0:T(8,128)(2,1)} %get-tuple-element.34.refs_10_.a_ref, bf16[8192,2048]{1,0:T(8,128)(2,1)} %bitcast.26), custom_call_target="tpu_custom_call" | custom-call | flops 34359738368 | bytes 58720256 | tf_op jit(solution)/shard_map/pallas_call | solution.py:401
  609.6 49.3 %shard_map.169 = f32[2048,1024]{1,0:T(8,128)} custom-call(s32[1]{0:T(128)} %bitcast.sel_ref, bf16[8192,2048]{1,0:T(8,128)(2,1)} %get-tuple-element.29.refs_0_.a_ref, bf16[2,8192,1024]{2,1,0:T(8,128)(2,1)} %get-tuple-element.35.refs_11_.refs_0_), custom_call_target="tpu_custom_call" | custom-call | flops 34359738368 | bytes 58720256 | tf_op jit(solution)/shard_map/pallas_call | solution.py:401
  658.9 49.0 %shard_map.170 = (f32[2048,512]{1,0:T(8,128)}, f32[2048,512]{1,0:T(8,128)}) custom-call(s32[1]{0:T(128)} %bitcast.sel_ref, bf16[8192,2048]{1,0:T(8,128)(2,1)} %get-tuple-element.29.refs_0_.a_ref, bf16[2,8192,512]{2,1,0:T(8,128)(2,1)} %get-tuple-element.36.refs_12_.refs_0_, bf16[2,8192,512]{2,1,0:T(8,128)(2,1)} %get-tuple-element.37.refs_13_.refs_1_), custom_call_target="tpu_custom_call" | custom-call | flops 34359738368 | bytes 58720256 | tf_op jit(solution)/shard_map/pallas_call | solution.py:401
  707.9 0.7 copy-done.8
  708.6 24.7 %all-reduce = (f32[128]{0:T(128)}, f32[128]{0:T(128)}) all-reduce(f32[128]{0:T(128)S(1)} %reduce_sum.27, f32[128]{0:T(128)S(1)} %reduce_sum.28), channel_id=1, replica_groups=mesh['tp'=2,'dp'=4] {'tp','dp'}, use_global_device_ids=true, to_apply=%region_5.6 | all-reduce | flops 256 | bytes 2048 | tf_op jit(solution)/shard_map/psum | solution.py:586
  733.4 15.5 %unpack.1 = (bf16[2048,1024]{1,0:T(8,128)(2,1)}, bf16[2048,512]{1,0:T(8,128)(2,1)}, bf16[2048,512]{1,0:T(8,128)(2,1)}, bf16[1024,2048]{1,0:T(8,128)(2,1)}) custom-call(f32[2,1536,2048]{2,1,0:T(8,128)} %bitcast.16), custom_call_target="tpu_custom_call" | custom-call | flops 6291456 | bytes 37748736 | tf_op jit(solution)/shard_map/unpack/pallas_call | solution.py:369
  748.8 206.9 %attn_other.1 = (bf16[2,8192,1024]{2,1,0:T(8,128)(2,1)}, bf16[2,8192,1024]{2,1,0:T(8,128)(2,1)}, bf16[2,8192,512]{2,1,0:T(8,128)(2,1)}, bf16[2,8192,512]{2,1,0:T(8,128)(2,1)}) custom-call(s32[1]{0:T(128)S(6)} %sub.3.sel_ref, ...), custom_call_target="tpu_custom_call", output_to_operand_aliasing={{0}: (11, {}), {1}: (12, {}), {2}: (13, {}), {3}: (14, {})} | custom-call | flops 128849018880 | bytes 150994944 | tf_op jit(solution)/shard_map/attn_other/pallas_call | solution.py:321
  955.7 248.9 %out.1 = (bf16[8192,2048]{1,0:T(8,128)(2,1)}, bf16[8192,2048]{1,0:T(8,128)(2,1)}, f32[8,2048]{1,0:T(8,128)}) custom-call(s32[1]{0:T(128)} %bitcast.sel_ref, bf16[8192,2048]{1,0:T(8,128)(2,1)} %bitcast.24, bf16[8192,2048]{1,0:T(8,128)(2,1)} %bitcast.28, bf16[2,8192,1024]{2,1,0:T(8,128)(2,1)} %get-tuple-element.38.o_ref, ...), custom_call_target="tpu_custom_call" | custom-call | flops 206158430208 | bytes 234881024 | tf_op jit(solution)/shard_map/out/pallas_call | solution.py:525
  1204.6 0.9 reduce_sum.29
  1205.4 7.4 psum.55
  1212.9 8.6 copy.32
  1221.5 2.1 copy.33
  1223.6 1.6 copy-done
  1225.2 2.1 copy.34
  1227.3 2.1 slice-done.1
  1229.4 3.4 copy.35
  (38 shorter events, 3.4 us)
Async XLA Ops:
  8.0 725.4 %all-gather.3.cloned.1.call-start = ((), (), s32[]{:S(2)}) async-start(), calls=%async_computation | async-start | bytes 37748736 | tf_op jit(solution)/shard_map/all_gather | solution.py:572
  8.1 2.8 copy-start.2
  8.1 3.5 copy-start.3
  8.1 4.1 copy-start.4
  12.3 28.8 %copy-start.6 = (bf16[2048]{0:T(1024)(128)(2,1)S(1)}, bf16[2048]{0:T(1024)(128)(2,1)}, u32[]{:S(2)}) copy-start(bf16[2048]{0:T(1024)(128)(2,1)} %param.13) | copy-start | bytes 12292
  12.3 29.4 %copy-start.5 = (s32[32,256]{1,0:T(8,128)S(1)}, s32[32,256]{1,0:T(8,128)}, u32[]{:S(2)}) copy-start(s32[32,256]{1,0:T(8,128)} %param.12) | copy-start | bytes 98308
  37.8 274.0 %collective-permute-start = (f32[1536,2048]{1,0:T(8,128)}, f32[1536,2048]{1,0:T(8,128)}, u32[]{:S(2)}, u32[]{:S(2)}) collective-permute-start(f32[1536,2048]{1,0:T(8,128)} %maximum_convert_fusion), channel_id=1, source_target_pairs={{0,4},{4,0},{1,5},{5,1},{2,6},{6,2},{3,7},{7,3}} | collective-permute-start | bytes 37748744 | tf_op jit(solution)/shard_map/ppermute | solution.py:571
  311.8 0.7 copy-start.9
  311.8 0.7 copy-start.10
  311.8 901.1 %all-reduce.4.cloned.1.call-start = ((), (), s32[]{:S(2)}) async-start(), calls=%async_computation.1 | async-start | bytes 50331648 | tf_op jit(solution)/shard_map/psum | solution.py:585
  707.9 0.7 copy-start.8
  707.9 0.7 copy-start.7
  1212.9 8.6 copy-start.1
  1221.5 3.7 copy-start
  1221.5 5.8 slice-start
  1225.2 4.2 slice-start.1
Sparse Core Ops, SparseCore 0:
  311.9 38.7 all-gather.2
Sparse Core Ops, SparseCore 1:
  708.0 419.6 all-reduce.3

commit v2 on v1

--- a/solution.py
+++ b/solution.py
@@ -550,6 +550,70 @@
     )(sel, x, dy, o, dq, dk, dv, gain, *own, *oth)
 
 
+def pack_kernel(sel_ref, q_ref, k_ref, v_ref, o_ref, out_ref):
+    d, nq, nk = q_ref.shape[0], q_ref.shape[1], k_ref.shape[1]
+    out_ref[0, 0:d, 0:nq] = q_ref[...].astype(F32)
+    out_ref[0, 0:d, nq:nq + nk] = k_ref[...].astype(F32)
+    out_ref[0, 0:d, nq + nk:] = v_ref[...].astype(F32)
+    out_ref[0, d:, :] = o_ref[...].astype(F32)
+
+
+def pack_call(part, w_q, w_k, w_v, w_o, parts=2, cuts=4):
+    D, nq = w_q.shape
+    spec = lambda w: pl.BlockSpec((w.shape[0] // (parts * cuts), w.shape[1]), lambda i, s: (s[0] * cuts + i, 0))
+    r = (D + nq) // (parts * cuts)
+    return pl.pallas_call(
+        pack_kernel,
+        grid_spec=pltpu.PrefetchScalarGridSpec(
+            num_scalar_prefetch=1,
+            grid=(cuts,),
+            in_specs=[spec(w) for w in (w_q, w_k, w_v, w_o)],
+            out_specs=pl.BlockSpec((1, r, D), lambda i, s: (i, 0, 0)),
+        ),
+        out_shape=jax.ShapeDtypeStruct((cuts, r, D), F32),
+        compiler_params=pltpu.CompilerParams(dimension_semantics=("arbitrary",), vmem_limit_bytes=60 << 20),
+        cost_estimate=pl.CostEstimate(flops=cuts * r * D, bytes_accessed=cuts * r * D * 6, transcendentals=0),
+        name="pack",
+    )(part, w_q, w_k, w_v, w_o)
+
+
+def table_kernel(pos_ref, freq_ref, cos_ref, sin_ref):
+    n, seq = pos_ref.shape
+    lane = lax.broadcasted_iota(jnp.int32, (HD, HD), 1)
+    for r in range(n):
+        for h in range(seq // HD):
+            p = pos_ref[r:r + 1, h * HD:(h + 1) * HD].astype(F32)
+            a = jnp.broadcast_to(p, (HD, HD)).T * freq_ref[0:1, :]
+            k = jnp.round(a * 0.6366197723675814)
+            x = ((a - k * 1.5703125) - k * 4.837512969970703125e-4) - k * 7.549789948768648e-8
+            z = x * x
+            s = ((-1.9515295891e-4 * z + 8.3321608736e-3) * z - 1.6666654611e-1) * z * x + x
+            c = ((2.443315711809948e-5 * z - 1.388731625493765e-3) * z + 4.166664568298827e-2) * z * z - 0.5 * z + 1.0
+            q = k.astype(jnp.int32)
+            odd = (q & 1) == 1
+            co, si = jnp.where(odd, s, c), jnp.where(odd, c, s)
+            rows = slice((r * (seq // HD) + h) * HD, (r * (seq // HD) + h + 1) * HD)
+            cos_ref[rows, :] = jnp.where(((q + 1) & 2) == 0, co, -co)
+            sin_ref[rows, :] = jnp.where(((q & 2) == 0) == (lane >= HD // 2), si, -si)
+
+
+def table_call(positions, rows=8):
+    n, seq = positions.shape
+    freq = THETA ** (-jnp.arange(0, HD, 2, dtype=F32) / HD)
+    freq = jnp.concatenate([freq, freq]).reshape(1, HD)
+    out = pl.BlockSpec((rows * seq, HD), lambda i: (i, 0))
+    return pl.pallas_call(
+        table_kernel,
+        grid=(n // rows,),
+        in_specs=[pl.BlockSpec((rows, seq), lambda i: (i, 0)), pl.BlockSpec((1, HD), lambda i: (0, 0))],
+        out_specs=[out, out],
+        out_shape=[jax.ShapeDtypeStruct((n * seq, HD), F32)] * 2,
+        compiler_params=pltpu.CompilerParams(dimension_semantics=("arbitrary",), vmem_limit_bytes=60 << 20),
+        cost_estimate=pl.CostEstimate(flops=n * seq * HD * 30, bytes_accessed=n * seq * HD * 8, transcendentals=0),
+        name="table",
+    )(positions, freq)
+
+
 def solution(mesh):
     tok_spec = P("dp", None, None)
     col_spec = P(None, "tp")
@@ -565,16 +629,13 @@
         own = me.reshape(1)
         other = 1 - own
 
-        part = lax.axis_index("dp") % 2
-        cut = lambda w: lax.dynamic_slice_in_dim(w, part * (w.shape[0] // 2), w.shape[0] // 2, 0)
-        share = jnp.concatenate([jnp.concatenate([cut(w_q), cut(w_k), cut(w_v)], axis=1), cut(w_o)], axis=0).astype(F32)
+        part = (lax.axis_index("dp") % 2).astype(jnp.int32).reshape(1)
+        share = pack_call(part, w_q, w_k, w_v, w_o)
         share = lax.ppermute(share, "tp", [(0, 1), (1, 0)])
         gathered = lax.all_gather(share, "dp", axis_index_groups=[[2 * i, 2 * i + 1] for i in range(n_dp // 2)])
-
-        inv_freq = THETA ** (-jnp.arange(0, HD, 2, dtype=F32) / HD)
-        angles = positions.reshape(T, 1).astype(F32) * inv_freq
-        cos, sin = jnp.cos(angles), jnp.sin(angles)
-        cosd, sind = jnp.concatenate([cos, cos], axis=1), jnp.concatenate([-sin, sin], axis=1)
+        gathered = gathered.reshape(-1, *gathered.shape[2:])
+
+        cosd, sind = table_call(positions)
         gain = g_attn.astype(F32).reshape(1, D)
         qg, kg = q_gain.astype(F32).reshape(1, HD), k_gain.astype(F32).reshape(1, HD)
 
@@ -583,12 +644,13 @@
         (dw_q,) = dw_call(own, n, [dq])
         dw_k, dw_v = dw_call(own, n, [dk, dv])
         dw_o, dw_q, dw_k, dw_v = lax.psum((dw_o, dw_q, dw_k, dw_v), "dp")
-        q_sum, k_sum = lax.psum((jnp.sum(dgq, axis=0), jnp.sum(dgk, axis=0)), ("tp", "dp"))
 
         theirs = unpack_call(gathered, D, nq, nk)
         o, dq, dk, dv = attn_call(False, other, n, dy, cosd, sind, gain, qg, kg, *theirs, prev=(o, dq, dk, dv), seq=n_seq)
         y, dx, dg = out_call(own, x, dy, o, dq, dk, dv, gain, (w_q, w_k, w_v, w_o), theirs)
-        g_sum = lax.psum(jnp.sum(dg, axis=0), "dp")
+        small = jnp.sum(jnp.concatenate([0.5 * dg, dgq, dgk], axis=1), axis=0)
+        small = lax.psum(small, ("tp", "dp"))
+        g_sum, q_sum, k_sum = small[:D], small[D:D + HD], small[D + HD:]
         return y.reshape(x_in.shape), dx.reshape(x_in.shape), dw_q, dw_k, dw_v, dw_o, q_sum, k_sum, g_sum
 
     return jax.shard_map(per_device, mesh=mesh, in_specs=(tok_spec, tok_spec, P("dp", None), P(), P(), P(), col_spec, col_spec, col_spec, row_spec), out_specs=(tok_spec, tok_spec, col_spec, col_spec, col_spec, row_spec, P(), P(), P()), check_vma=False)

time: 1250 us -> 1210 us (0.968)
  other arithmetic: 59 us -> 2.6 us
  Pallas kernels: 835 us -> 862 us
    convert_element_type x1 -> x0, other arithmetic: 25.4 us -> none  [per_device(): jnp.concatenate([jnp.concatenate([cut(w_q), cut(w_k), cut(w_v)], axis=1),...]
    neg x1 -> x0, other arithmetic: 18.1 us -> none  [per_device(): -sin]
    pallas_call x0 -> x2, Pallas kernels: none -> 16 us  [the longest x1 8.21 us: table_call(): pl.pallas_call(table_kernel, grid=(n // rows,), in_specs=[pl.BlockSpec((r...]
    concatenate x1 -> x0, other arithmetic: 13.5 us -> none  [per_device(): jnp.concatenate([cos, cos], axis=1)]
    psum x2 -> x1, blocking collectives: 32.2 us -> 23.2 us  [per_device(): small = lax.psum(small, ('tp', 'dp'))]
  transfers between devices with their start and end apart: 3 -> 3, of which waited for: 1 -> 1; matrix products, arithmetic and copies ran while one was open for 3% -> 0% of each run, Pallas kernels for 67% -> 71%
where the time goes in v2:
time: 1210 us; the launch traced here: 1200 us
  Pallas kernels  862 us (71%)
  waiting for transfers between devices  271 us (22%)
  blocking collectives  23.2 us (2%)
  local copies, waits for them, and re-layouts  21 us (2%)
  between operations  15.8 us (1%)
    pallas_call x2, Pallas kernels, attn_call(): pl.pallas_call(functools.partial(attn_kernel, own, seq, n_grp), grid_spec...  430 us
    ppermute x1, waiting for transfers between devices, per_device(): share = lax.ppermute(share, 'tp', [(0, 1), (1, 0)])  271 us
    pallas_call x1, Pallas kernels, out_call(): pl.pallas_call(functools.partial(out_kernel, m), grid_spec=pltpu.Prefetch...  249 us
    pallas_call x3, Pallas kernels, dw_call(): pl.pallas_call(functools.partial(dw_kernel, len(bs)), grid_spec=pltpu.Pre...  145 us
  transfers between devices with their start and end apart: 3, of which 1 were waited for; matrix products, arithmetic and copies ran while one was open for 0% of the time, Pallas kernels for 71%

profile of v2, /device:TPU:0, one launch (start us, length us, event | category | flops | bytes accessed | tf_op | source)
XLA Modules:
  0.0 1199.1 jit_solution(7162683413682900075)
XLA Ops:
  8.1 7.8 pack.1
  15.8 3.4 collective-permute-start
  19.2 270.7 %collective-permute-done = f32[4,384,2048]{2,1,0:T(8,128)} collective-permute-done((f32[4,384,2048]{2,1,0:T(8,128)}, f32[4,384,2048]{2,1,0:T(8,128)}, u32[]{:S(2)}, u32[]{:S(2)}) %collective-permute-start) | collective-permute-done | bytes 12582944 | tf_op jit(solution)/shard_map/ppermute | solution.py:634
  289.9 0.6 reshape.71
  290.5 0.6 maximum_bitcast_fusion.freq_ref
  291.1 8.2 table.1
  299.4 0.5 bitcast_convert_fusion
  299.9 223.1 %attn_own.1 = (bf16[8192,2048]{1,0:T(8,128)(2,1)}, bf16[2,8192,1024]{2,1,0:T(8,128)(2,1)}, bf16[2,8192,1024]{2,1,0:T(8,128)(2,1)}, bf16[2,8192,512]{2,1,0:T(8,12...) custom-call(s32[1]{0:T(128)} %bitcast.sel_ref, bf16[8192,2048]{1,0:T(8,128)(2,1)} %bitcast.19, ...), custom_call_target="tpu_custom_call" | custom-call | flops 128849018880 | bytes 150994944 | tf_op jit(solution)/shard_map/attn_own/pallas_call | solution.py:321
  523.0 46.7 %shard_map.171 = f32[1024,2048]{1,0:T(8,128)} custom-call(s32[1]{0:T(128)} %bitcast.sel_ref, bf16[2,8192,1024]{2,1,0:T(8,128)(2,1)} %get-tuple-element.38.refs_10_.a_ref, bf16[8192,2048]{1,0:T(8,128)(2,1)} %bitcast.23), custom_call_target="tpu_custom_call" | custom-call | flops 34359738368 | bytes 58720256 | tf_op jit(solution)/shard_map/pallas_call | solution.py:401
  569.7 49.3 %shard_map.169 = f32[2048,1024]{1,0:T(8,128)} custom-call(s32[1]{0:T(128)} %bitcast.sel_ref, bf16[8192,2048]{1,0:T(8,128)(2,1)} %get-tuple-element.33.refs_0_.a_ref, bf16[2,8192,1024]{2,1,0:T(8,128)(2,1)} %get-tuple-element.39.refs_11_.refs_0_), custom_call_target="tpu_custom_call" | custom-call | flops 34359738368 | bytes 58720256 | tf_op jit(solution)/shard_map/pallas_call | solution.py:401
  618.9 49.5 %shard_map.170 = (f32[2048,512]{1,0:T(8,128)}, f32[2048,512]{1,0:T(8,128)}) custom-call(s32[1]{0:T(128)} %bitcast.sel_ref, bf16[8192,2048]{1,0:T(8,128)(2,1)} %get-tuple-element.33.refs_0_.a_ref, bf16[2,8192,512]{2,1,0:T(8,128)(2,1)} %get-tuple-element.40.refs_12_.refs_0_, bf16[2,8192,512]{2,1,0:T(8,128)(2,1)} %get-tuple-element.41.refs_13_.refs_1_), custom_call_target="tpu_custom_call" | custom-call | flops 34359738368 | bytes 58720256 | tf_op jit(solution)/shard_map/pallas_call | solution.py:401
  668.5 21.8 %unpack.1 = (bf16[2048,1024]{1,0:T(8,128)(2,1)}, bf16[2048,512]{1,0:T(8,128)(2,1)}, bf16[2048,512]{1,0:T(8,128)(2,1)}, bf16[1024,2048]{1,0:T(8,128)(2,1)}) custom-call(f32[8,384,2048]{2,1,0:T(8,128)} %all-gather.3.cloned.1.call-done.f_ref), custom_call_target="tpu_custom_call" | custom-call | flops 6291456 | bytes 37748736 | tf_op jit(solution)/shard_map/unpack/pallas_call | solution.py:369
  690.4 207.3 %attn_other.1 = (bf16[2,8192,1024]{2,1,0:T(8,128)(2,1)}, bf16[2,8192,1024]{2,1,0:T(8,128)(2,1)}, bf16[2,8192,512]{2,1,0:T(8,128)(2,1)}, bf16[2,8192,512]{2,1,0:T(8,128)(2,1)}) custom-call(s32[1]{0:T(128)S(6)} %sub.3.sel_ref, ...), custom_call_target="tpu_custom_call", output_to_operand_aliasing={{0}: (11, {}), {1}: (12, {}), {2}: (13, {}), {3}: (14, {})} | custom-call | flops 128849018880 | bytes 150994944 | tf_op jit(solution)/shard_map/attn_other/pallas_call | solution.py:321
  897.7 248.6 %out.1 = (bf16[8192,2048]{1,0:T(8,128)(2,1)}, bf16[8192,2048]{1,0:T(8,128)(2,1)}, f32[8,2048]{1,0:T(8,128)}) custom-call(s32[1]{0:T(128)} %bitcast.sel_ref, bf16[8192,2048]{1,0:T(8,128)(2,1)} %bitcast.21, bf16[8192,2048]{1,0:T(8,128)(2,1)} %bitcast.25, bf16[2,8192,1024]{2,1,0:T(8,128)(2,1)} %get-tuple-element.42.o_ref, ...), custom_call_target="tpu_custom_call" | custom-call | flops 206158430208 | bytes 234881024 | tf_op jit(solution)/shard_map/out/pallas_call | solution.py:525
  1146.3 0.8 broadcast_multiply_fusion
  1147.2 23.2 %psum.39 = f32[2304]{0:T(1024)S(1)} all-reduce(f32[2304]{0:T(1024)S(1)} %maximum_reduce_fusion), channel_id=1, replica_groups=mesh['tp'=2,'dp'=4] {'tp','dp'}, use_global_device_ids=true, to_apply=%region_5.6 | all-reduce | flops 2304 | bytes 18432 | tf_op jit(solution)/shard_map/psum | solution.py:652
  1170.4 0.6 slice.14
  1171.0 0.5 fusion
  1171.5 8.6 copy.31
  1180.1 2.1 copy.32
  1182.2 1.6 copy-done
  1183.8 2.1 copy.33
  1185.9 2.1 slice-done.1
  1188.0 3.4 copy.34
  (25 shorter events, 0.2 us)
Async XLA Ops:
  8.0 660.5 %all-gather.3.cloned.1.call-start = ((), (), s32[]{:S(2)}) async-start(), calls=%async_computation | async-start | bytes 37748736 | tf_op jit(solution)/shard_map/all_gather | solution.py:635
  15.8 274.1 %copy-start.2 = (bf16[2048]{0:T(1024)(128)(2,1)S(1)}, bf16[2048]{0:T(1024)(128)(2,1)}, u32[]{:S(2)}) copy-start(bf16[2048]{0:T(1024)(128)(2,1)} %param.13) | copy-start | bytes 12292
  15.8 283.5 %copy-start.5 = (bf16[128]{0:T(256)(128)(2,1)S(1)}, bf16[128]{0:T(256)(128)(2,1)}, u32[]{:S(2)}) copy-start(bf16[128]{0:T(256)(128)(2,1)} %param.15) | copy-start | bytes 772
  15.8 283.5 %copy-start.6 = (bf16[128]{0:T(256)(128)(2,1)S(1)}, bf16[128]{0:T(256)(128)(2,1)}, u32[]{:S(2)}) copy-start(bf16[128]{0:T(256)(128)(2,1)} %param.14) | copy-start | bytes 772
  15.8 274.0 %collective-permute-start = (f32[4,384,2048]{2,1,0:T(8,128)}, f32[4,384,2048]{2,1,0:T(8,128)}, u32[]{:S(2)}, u32[]{:S(2)}) collective-permute-start(f32[4,384,2048]{2,1,0:T(8,128)} %pack.1), channel_id=1, source_target_pairs={{0,4},{4,0},{1,5},{5,1},{2,6},{6,2},{3,7},{7,3}} | collective-permute-start | bytes 37748744 | tf_op jit(solution)/shard_map/ppermute | solution.py:634
  289.9 881.6 %all-reduce.3.cloned.1.call-start = ((), (), s32[]{:S(2)}) async-start(), calls=%async_computation.1 | async-start | bytes 50331648 | tf_op jit(solution)/shard_map/psum | solution.py:646
  897.7 249.5 %copy-start.3 = (f32[8,128]{1,0:T(8,128)S(1)}, f32[8,128]{1,0:T(8,128)}, u32[]{:S(2)}) copy-start(f32[8,128]{1,0:T(8,128)} %get-tuple-element.51) | copy-start | bytes 12292
  897.7 249.5 %copy-start.4 = (f32[8,128]{1,0:T(8,128)S(1)}, f32[8,128]{1,0:T(8,128)}, u32[]{:S(2)}) copy-start(f32[8,128]{1,0:T(8,128)} %get-tuple-element.52) | copy-start | bytes 12292
  1171.5 8.6 copy-start.1
  1180.1 3.7 copy-start
  1180.1 5.8 slice-start
  1183.8 4.2 slice-start.1
Sparse Core Ops, SparseCore 0:
  290.0 38.7 all-gather.2
Sparse Core Ops, SparseCore 1:
  668.6 418.3 all-reduce.2

commit v3 on v1

--- a/solution.py
+++ b/solution.py
@@ -1,4 +1,5 @@
 import functools
+from types import SimpleNamespace
 import jax
 import jax.numpy as jnp
 from jax import lax
@@ -369,7 +370,7 @@
     return pl.pallas_call(
         unpack_kernel,
         grid=(n,),
-        in_specs=[pl.BlockSpec((1, r, c), lambda i: (i, 0, 0), pipeline_mode=pl.Buffered(1))],
+        in_specs=[pl.BlockSpec((1, r, c), lambda i: (i, 0, 0))],
         out_specs=[part(D, nq), part(D, nk), part(D, nk), part(nq, D)],
         out_shape=[jax.ShapeDtypeStruct(s, BF16) for s in ((D, nq), (D, nk), (D, nk), (nq, D))],
         compiler_params=pltpu.CompilerParams(dimension_semantics=("arbitrary",), vmem_limit_bytes=60 << 20),
@@ -412,142 +413,491 @@
     )(sel, a, *bs)
 
 
-def out_kernel(m, sel_ref, x_ref, dy_ref, o_ref, dq_ref, dk_ref, dv_ref, gain_ref, *refs):
-    own, oth = refs[:4], refs[4:8]
-    y_out, dx_out, dg_out, wq_ref, wk_ref, wv_ref, wo_ref, dn_ref, oc_ref, y_ref, dx_ref, st_ref, dg_ref, sem = refs[8:]
-    D = x_ref.shape[1]
+def pack_kernel(sel_ref, q_ref, k_ref, v_ref, o_ref, out_ref):
+    d, nq, nk = q_ref.shape[0], q_ref.shape[1], k_ref.shape[1]
+    out_ref[0, 0:d, 0:nq] = q_ref[...].astype(F32)
+    out_ref[0, 0:d, nq:nq + nk] = k_ref[...].astype(F32)
+    out_ref[0, 0:d, nq + nk:] = v_ref[...].astype(F32)
+    out_ref[0, d:, :] = o_ref[...].astype(F32)
+
+
+def pack_call(part, w_q, w_k, w_v, w_o, parts=2, cuts=4):
+    D, nq = w_q.shape
+    spec = lambda w: pl.BlockSpec((w.shape[0] // (parts * cuts), w.shape[1]), lambda i, s: (s[0] * cuts + i, 0))
+    r = (D + nq) // (parts * cuts)
+    return pl.pallas_call(
+        pack_kernel,
+        grid_spec=pltpu.PrefetchScalarGridSpec(
+            num_scalar_prefetch=1,
+            grid=(cuts,),
+            in_specs=[spec(w) for w in (w_q, w_k, w_v, w_o)],
+            out_specs=pl.BlockSpec((1, r, D), lambda i, s: (i, 0, 0)),
+        ),
+        out_shape=jax.ShapeDtypeStruct((cuts, r, D), F32),
+        compiler_params=pltpu.CompilerParams(dimension_semantics=("arbitrary",), vmem_limit_bytes=60 << 20),
+        cost_estimate=pl.CostEstimate(flops=cuts * r * D, bytes_accessed=cuts * r * D * 6, transcendentals=0),
+        name="pack",
+    )(part, w_q, w_k, w_v, w_o)
+
+
+def table_kernel(pos_ref, freq_ref, cos_ref, sin_ref):
+    n, seq = pos_ref.shape
+    lane = lax.broadcasted_iota(jnp.int32, (HD, HD), 1)
+    for r in range(n):
+        for h in range(seq // HD):
+            p = pos_ref[r:r + 1, h * HD:(h + 1) * HD].astype(F32)
+            a = jnp.broadcast_to(p, (HD, HD)).T * freq_ref[0:1, :]
+            k = jnp.round(a * 0.6366197723675814)
+            x = ((a - k * 1.5703125) - k * 4.837512969970703125e-4) - k * 7.549789948768648e-8
+            z = x * x
+            s = ((-1.9515295891e-4 * z + 8.3321608736e-3) * z - 1.6666654611e-1) * z * x + x
+            c = ((2.443315711809948e-5 * z - 1.388731625493765e-3) * z + 4.166664568298827e-2) * z * z - 0.5 * z + 1.0
+            q = k.astype(jnp.int32)
+            odd = (q & 1) == 1
+            co, si = jnp.where(odd, s, c), jnp.where(odd, c, s)
+            rows = slice((r * (seq // HD) + h) * HD, (r * (seq // HD) + h + 1) * HD)
+            cos_ref[rows, :] = jnp.where(((q + 1) & 2) == 0, co, -co)
+            sin_ref[rows, :] = jnp.where(((q & 2) == 0) == (lane >= HD // 2), si, -si)
+
+
+def table_call(positions, rows=8):
+    n, seq = positions.shape
+    freq = THETA ** (-jnp.arange(0, HD, 2, dtype=F32) / HD)
+    freq = jnp.concatenate([freq, freq]).reshape(1, HD)
+    out = pl.BlockSpec((rows * seq, HD), lambda i: (i, 0))
+    return pl.pallas_call(
+        table_kernel,
+        grid=(n // rows,),
+        in_specs=[pl.BlockSpec((rows, seq), lambda i: (i, 0)), pl.BlockSpec((1, HD), lambda i: (0, 0))],
+        out_specs=[out, out],
+        out_shape=[jax.ShapeDtypeStruct((n * seq, HD), F32)] * 2,
+        compiler_params=pltpu.CompilerParams(dimension_semantics=("arbitrary",), vmem_limit_bytes=60 << 20),
+        cost_estimate=pl.CostEstimate(flops=n * seq * HD * 30, bytes_accessed=n * seq * HD * 8, transcendentals=0),
+        name="table",
+    )(positions, freq)
+
+
+def attn_stages(seq, n_grp, r):
+    half = seq // 2
+    scale = HD ** -0.5
+    log2e = 1.4426950408889634
+
+    def norm_rows(src, dst):
+        def piece(c):
+            def run():
+                xf = src[c:c + 32, :].astype(F32)
+                inv = lax.rsqrt(jnp.mean(xf * xf, axis=-1, keepdims=True) + EPS)
+                dst[c:c + 32, :] = (xf * inv * r.gain[0:1, :]).astype(BF16)
+
+            return (1.5, run)
+
+        return [piece(c) for c in range(0, seq, 32)]
+
+    def proj(g):
+        def q():
+            t = dot(r.n[...], r.wq(slice(g * 2 * HD, (g + 1) * 2 * HD)))
+            for h in range(2):
+                r.qnew[g % 2, h] = t[:, h * HD:(h + 1) * HD].astype(BF16)
+
+        def k():
+            t = dot(r.n[...], r.wk(slice(g * HD, (g + 2) * HD)))
+            for h in range(2):
+                r.knew[g + h] = t[:, h * HD:(h + 1) * HD].astype(BF16)
+
+        def v():
+            t = dot(r.n[...], r.wv(slice(g * HD, (g + 2) * HD)))
+            for h in range(2):
+                r.vnew[g + h] = t[:, h * HD:(h + 1) * HD].astype(BF16)
+
+        def do():
+            t = r.do_dot(slice(g * 2 * HD, (g + 1) * 2 * HD))
+            for h in range(2):
+                r.do[g, h * half:(h + 1) * half, :] = t[:half, h * HD:(h + 1) * HD].astype(BF16)
+                r.do[g, seq + h * half:seq + (h + 1) * half, :] = t[half:, h * HD:(h + 1) * HD].astype(BF16)
+
+        return [(1, q)] + ([(1, k), (1, v)] if g % 2 == 0 else []) + [(1, do)]
+
+    def stacked(h, c):
+        return (h * half + c) if c < half else (seq + h * half + c - half)
+
+    def rope(g):
+        cs, sn = (r.tab.at[2], r.tab.at[3]) if g == n_grp - 1 else (r.tab.at[0], r.tab.at[1])
+
+        def size(h, c):
+            def run():
+                raw = r.knew[g, c:c + CH, :] if h == 2 else r.qnew[g % 2, h, c:c + CH, :]
+                r.raw[g, h, c:c + CH, :] = raw
+                t = raw.astype(F32)
+                r.inv[g, h, c:c + CH, :] = jnp.broadcast_to(lax.rsqrt(jnp.mean(t * t, axis=-1, keepdims=True) + EPS), t.shape)
+
+            return (0.4, run)
+
+        def turn(h, c):
+            def run():
+                t = r.raw[g, h, c:c + CH, :].astype(F32)
+                w = (t * r.inv[g, h, c:c + CH, :]) * (r.kg if h == 2 else r.qg)[0:1, :]
+                o = 2 * seq + c if h == 2 else stacked(h, c)
+                x = pltpu.roll(w, HD // 2, 1)
+                co, si = cs[c:c + CH, :], sn[c:c + CH, :]
+                r.rot[g, o:o + CH, 0:HD] = (w * co + x * si).astype(BF16)
+                r.rot[g, o:o + CH, HD:] = (x * co - w * si).astype(BF16)
+                if h == 2:
+                    r.v[g, c:c + CH, :] = r.vnew[g, c:c + CH, :]
+
+            return (0.6, run)
+
+        return [f(h, c) for f in (size, turn) for h in (2, 0, 1) for c in range(0, seq, CH)]
+
+    def scores(g):
+        b = g % 2
+
+        def s():
+            r.s[b, 0:seq, 0:half] = dot(r.rot[g, 0:seq, 0:HD], r.rot[g, 2 * seq:2 * seq + half, 0:HD], NT)
+            r.s[b, seq:, :] = dot(r.rot[g, seq:2 * seq, 0:HD], r.rot[g, 2 * seq:, 0:HD], NT)
+
+        def dp():
+            r.dp[b, 0:seq, 0:half] = dot(r.do[g, :seq, :], r.v[g, :half, :], NT)
+            r.dp[b, seq:, :] = dot(r.do[g, seq:, :], r.v[g], NT)
+
+        return [(1, s), (1, dp)]
+
+    def soft(g):
+        b = g % 2
+        c2 = scale * log2e
+
+        def part(blk, c):
+            return slice(blk * seq + c, blk * seq + c + CH), half if blk == 0 else seq
+
+        def masked(blk, c, s):
+            row_id = lax.broadcasted_iota(jnp.int32, (CH, half), 0) + (c % half)
+            keep = row_id >= lax.broadcasted_iota(jnp.int32, (CH, half), 1)
+            if blk == 0:
+                return jnp.where(keep, s, -jnp.inf)
+            return jnp.concatenate([s[:, :half], jnp.where(keep, s[:, half:], -jnp.inf)], axis=1)
+
+        def wide(ref, rows, width):
+            t = ref[rows, :]
+            return t if width == half else jnp.concatenate([t, t], axis=1)
+
+        def top(blk, c):
+            rows, width = part(blk, c)
+
+            def run():
+                m = jnp.max(masked(blk, c, r.s[b, rows, 0:width]), axis=-1, keepdims=True)
+                r.st[0, rows, :] = jnp.broadcast_to(m * c2, (CH, HD))
+
+            return (0.4 + 0.4 * blk, run)
+
+        def power(blk, c):
+            rows, width = part(blk, c)
+
+            def run():
+                e = jnp.exp2(masked(blk, c, r.s[b, rows, 0:width] * c2) - wide(r.st.at[0], rows, width))
+                r.s[b, rows, 0:width] = e
+                r.st[1, rows, :] = jnp.broadcast_to(1.0 / jnp.sum(e, axis=-1, keepdims=True), (CH, HD))
+
+            return (0.8 + 0.8 * blk, run)
+
+        def prob(blk, c):
+            rows, width = part(blk, c)
+
+            def run():
+                pr = r.s[b, rows, 0:width] * wide(r.st.at[1], rows, width)
+                r.s[b, rows, 0:width] = pr
+                r.p[b, rows, 0:width] = pr.astype(BF16)
+                r.st[2, rows, :] = jnp.broadcast_to(jnp.sum(pr * r.dp[b, rows, 0:width], axis=-1, keepdims=True), (CH, HD))
+
+            return (0.8 + 0.8 * blk, run)
+
+        def last(blk, c):
+            rows, width = part(blk, c)
+
+            def run():
+                d = r.dp[b, rows, 0:width] - wide(r.st.at[2], rows, width)
+                r.ds[b, rows, 0:width] = (r.s[b, rows, 0:width] * d * scale).astype(BF16)
+
+            return (0.8 + 0.8 * blk, run)
+
+        return [f(blk, c) for f in (top, power, prob, last) for blk in range(2) for c in range(0, seq, CH)]
+
+    def grads(g):
+        b = g % 2
+        col, kcol = g * 2 * HD, g * HD
+
+        def dq():
+            r.dqf[b, 0:seq, :] = dot(r.ds[b, 0:seq, 0:half], r.rot[g, 2 * seq:2 * seq + half, :])
+            r.dqf[b, seq:, :] = dot(r.ds[b, seq:, :], r.rot[g, 2 * seq:, :])
+
+        def dk():
+            tb = dot(r.ds[b, seq:, :], r.rot[g, seq:2 * seq, :], TN)
+            ta = dot(r.ds[b, 0:seq, 0:half], r.rot[g, 0:seq, :], TN)
+            r.dkf[b, :half, :] = tb[:half] + ta
+            r.dkf[b, half:, :] = tb[half:]
+
+        def o():
+            ta = dot(r.p[b, 0:seq, 0:half], r.v[g, :half, :])
+            tb = dot(r.p[b, seq:, :], r.v[g])
+            for h in range(2):
+                r.o[0:half, col + h * HD:col + (h + 1) * HD] = ta[h * half:(h + 1) * half].astype(BF16)
+                r.o[half:seq, col + h * HD:col + (h + 1) * HD] = tb[h * half:(h + 1) * half].astype(BF16)
+
+        def dv():
+            tb = dot(r.p[b, seq:, :], r.do[g, seq:, :], TN)
+            ta = dot(r.p[b, 0:seq, 0:half], r.do[g, :seq, :], TN)
+            r.dv[0:half, kcol:kcol + HD] = (tb[:half] + ta).astype(BF16)
+            r.dv[half:seq, kcol:kcol + HD] = tb[half:].astype(BF16)
+
+        return [(1, dq), (1, dk), (1, o), (1, dv)]
+
+    def back(g):
+        b = g % 2
+
+        def place(h, c):
+            if h == 2:
+                return r.dkf, c, r.dk, g * HD, r.kg
+            return r.dqf, stacked(h, c), r.dq, (2 * g + h) * HD, r.qg
+
+        def turn(h, c):
+            src, o, _, _, g_ref = place(h, c)
+
+            def run():
+                d = src[b, o:o + CH, :].astype(BF16).astype(F32)
+                that = r.raw[g, h, c:c + CH, :].astype(F32) * r.inv[g, h, c:c + CH, :]
+                du = d[:, :HD] * r.tab[2, c:c + CH, :] - d[:, HD:] * r.tab[3, c:c + CH, :]
+                src[b, o:o + CH, 0:HD] = du
+                pr = du * that
+                dg_ref = r.dgk if h == 2 else r.dgq
+                dg_ref[...] += jnp.sum(pr.reshape(CH // 8, 8, HD), axis=0)
+                r.sb[h, c:c + CH, :] = jnp.broadcast_to(jnp.mean(pr * g_ref[0:1, :], axis=-1, keepdims=True), (CH, HD))
+
+            return (0.6, run)
+
+        def out(h, c):
+            src, o, out_ref, col, g_ref = place(h, c)
+
+            def run():
+                inv = r.inv[g, h, c:c + CH, :]
+                that = r.raw[g, h, c:c + CH, :].astype(F32) * inv
+                out_ref[c:c + CH, col:col + HD] = (inv * (src[b, o:o + CH, 0:HD] * g_ref[0:1, :] - that * r.sb[h, c:c + CH, :])).astype(BF16)
+
+            return (0.5, run)
+
+        return [f(h, c) for f in (turn, out) for h in (0, 1, 2) for c in range(0, seq, CH)]
+
+    return SimpleNamespace(norm=norm_rows, proj=proj, rope=rope, scores=scores, soft=soft, grads=grads, back=back)
+
+
+def attn_tick(st, g, n_grp, extra=()):
+    vec = st.soft((g - 3) % n_grp) + st.rope((g - 1) % n_grp)
+    more = [e for e in extra]
+    if more:
+        vec = vec + more[0]
+    vec = vec + st.back(g)
+    gr = st.grads(g)
+    for _, f in gr[:2]:
+        f()
+    weave(vec, st.scores((g - 2) % n_grp) + gr[2:] + st.proj(g), *more[1:])
+
+
+def attn_scratch(seq, n_grp, nq, nk):
+    return dict(
+        qnew=pltpu.VMEM((2, 2, seq, HD), BF16),
+        knew=pltpu.VMEM((n_grp, seq, HD), BF16),
+        vnew=pltpu.VMEM((n_grp, seq, HD), BF16),
+        raw=pltpu.VMEM((n_grp, 3, seq, HD), BF16),
+        inv=pltpu.VMEM((n_grp, 3, seq, HD), F32),
+        rot=pltpu.VMEM((n_grp, 3 * seq, 2 * HD), BF16),
+        do=pltpu.VMEM((n_grp, 2 * seq, HD), BF16),
+        v=pltpu.VMEM((n_grp, seq, HD), BF16),
+        s=pltpu.VMEM((2, 2 * seq, seq), F32),
+        dp=pltpu.VMEM((2, 2 * seq, seq), F32),
+        p=pltpu.VMEM((2, 2 * seq, seq), BF16),
+        ds=pltpu.VMEM((2, 2 * seq, seq), BF16),
+        dkf=pltpu.VMEM((2, seq, 2 * HD), F32),
+        dqf=pltpu.VMEM((2, 2 * seq, 2 * HD), F32),
+        st=pltpu.VMEM((3, 2 * seq, HD), F32),
+        sb=pltpu.VMEM((3, seq, HD), F32),
+        tab=pltpu.VMEM((4, seq, HD), F32),
+        o=pltpu.VMEM((seq, nq), BF16),
+        dq=pltpu.VMEM((seq, nq), BF16),
+        dk=pltpu.VMEM((seq, nk), BF16),
+        dv=pltpu.VMEM((seq, nk), BF16),
+    )
+
+
+def tail_kernel(seq, n_grp, rows, keys, sel_ref, n_in, dy_in, cos_in, sin_in, x_in, dyx_in, gain_ref, qg_ref, kg_ref, *refs):
+    own_w, oth_w, own_a = refs[:4], refs[4:8], refs[8:12]
+    y_out, dx_out, dg_out, dgq_out, dgk_out = refs[12:17]
+    r = SimpleNamespace(n=n_in, dy=dy_in, qg=qg_ref, kg=kg_ref, gain=gain_ref, **dict(zip(keys, refs[17:])))
     step = pl.program_id(0)
-    ME = sel_ref[0]
+    me = sel_ref[0]
+    oth = 1 - me
+    D = x_in.shape[1]
+    r.wq = lambda c: r.wq_all[oth, :, c]
+    r.wk = lambda c: r.wk_all[oth, :, c]
+    r.wv = lambda c: r.wv_all[oth, :, c]
+    r.do_dot = lambda c: dot(dy_in[...], r.wo_all[oth, c, :], NT)
+    st = attn_stages(seq, n_grp, r)
+
+    def fetch(row):
+        return [pltpu.make_async_copy(src.at[me, pl.ds(row * seq, seq), :], dst, r.sem.at[8 + k])
+                for k, (src, dst) in enumerate(zip(own_a, (r.o_own, r.dq_own, r.dk_own, r.dv_own)))]
 
     @pl.when(step == 0)
     def _():
         copies = []
-        for k, dst in enumerate((wq_ref, wk_ref, wv_ref, wo_ref)):
-            copies.append(pltpu.make_async_copy(own[k], dst.at[ME], sem.at[k]))
-            copies.append(pltpu.make_async_copy(oth[k], dst.at[1 - ME], sem.at[4 + k]))
+        for k, dst in enumerate((r.wq_all, r.wk_all, r.wv_all, r.wo_all)):
+            copies.append(pltpu.make_async_copy(oth_w[k], dst.at[oth], r.sem.at[4 + k]))
+            copies.append(pltpu.make_async_copy(own_w[k], dst.at[me], r.sem.at[k]))
         for c in copies:
             c.start()
         for c in copies:
             c.wait()
-        dg_ref[...] = jnp.zeros_like(dg_ref)
-
-    CR = 32
-    NC = 256
+        for c in fetch(0):
+            c.start()
+        r.dg[...] = jnp.zeros_like(r.dg)
+
+    CR, NC = 32, 256
+    nn = D // NC
+    lines = range(0, seq, CR)
+
+    def wide(v):
+        return jnp.concatenate([v] * (NC // HD), axis=1)
 
     def stat(c):
         def run():
-            xf = x_ref[c:c + CR, :].astype(F32)
-            st_ref[0, c:c + CR, :] = jnp.broadcast_to(lax.rsqrt(jnp.mean(xf * xf, axis=-1, keepdims=True) + EPS), (CR, HD))
-            st_ref[1, c:c + CR, :] = jnp.zeros((CR, HD), F32)
+            xf = x_in[c:c + CR, :].astype(F32)
+            r.xs[0, c:c + CR, :] = jnp.broadcast_to(lax.rsqrt(jnp.mean(xf * xf, axis=-1, keepdims=True) + EPS), (CR, HD))
+            r.xs[1, c:c + CR, :] = jnp.zeros((CR, HD), F32)
 
         return (1, run)
-
-    def keep(c):
-        def run():
-            for s in range(2):
-                oc_ref[s, c:c + CR, :] = o_ref[s, c:c + CR, :]
-
-        return (0.5, run)
 
     def dn_dot(n):
         def run():
             cols = slice(n * NC, (n + 1) * NC)
             t = None
             for s in range(2):
-                for a_ref, w_ref in ((dq_ref, wq_ref), (dk_ref, wk_ref), (dv_ref, wv_ref)):
+                for a_ref, w_ref in ((r.dqc, r.wq_all), (r.dkc, r.wk_all), (r.dvc, r.wv_all)):
                     u = dot(a_ref[s], w_ref[s, cols, :], NT)
                     t = u if t is None else t + u
-            dn_ref[:, cols] = t
-
-        return (1, run)
-
-    def wide(v):
-        return jnp.concatenate([v] * (NC // HD), axis=1)
+            r.dn[:, cols] = t
+
+        return (2, run)
 
     def first(n, c):
         def run():
             cols = slice(n * NC, (n + 1) * NC)
-            w = dn_ref[c:c + CR, cols] * (x_ref[c:c + CR, cols].astype(F32) * wide(st_ref[0, c:c + CR, :]))
-            dg_ref[:, cols] += jnp.sum(w.reshape(CR // 8, 8, NC), axis=0)
+            w = r.dn[c:c + CR, cols] * (x_in[c:c + CR, cols].astype(F32) * wide(r.xs[0, c:c + CR, :]))
+            r.dg[:, cols] += jnp.sum(w.reshape(CR // 8, 8, NC), axis=0)
             w = w * gain_ref[0:1, cols]
-            st_ref[1, c:c + CR, :] += w[:, :HD] + w[:, HD:]
+            r.xs[1, c:c + CR, :] += w[:, :HD] + w[:, HD:]
 
         return (1, run)
 
     def mean(c):
         def run():
-            st_ref[2, c:c + CR, :] = jnp.broadcast_to(jnp.sum(st_ref[1, c:c + CR, :], axis=-1, keepdims=True) * (1.0 / D), (CR, HD))
+            r.xs[2, c:c + CR, :] = jnp.broadcast_to(jnp.sum(r.xs[1, c:c + CR, :], axis=-1, keepdims=True) * (1.0 / D), (CR, HD))
 
         return (0.2, run)
 
     def second(n, c):
         def run():
             cols = slice(n * NC, (n + 1) * NC)
-            inv = wide(st_ref[0, c:c + CR, :])
-            xh = x_ref[c:c + CR, cols].astype(F32) * inv
-            e = dn_ref[c:c + CR, cols] * gain_ref[0:1, cols]
-            dx_ref[c:c + CR, cols] = (dy_ref[c:c + CR, cols].astype(F32) + inv * (e - xh * wide(st_ref[2, c:c + CR, :]))).astype(BF16)
-
-        return (1, run)
+            inv = wide(r.xs[0, c:c + CR, :])
+            xh = x_in[c:c + CR, cols].astype(F32) * inv
+            e = r.dn[c:c + CR, cols] * gain_ref[0:1, cols]
+            dx_out[c:c + CR, cols] = (dyx_in[c:c + CR, cols].astype(F32) + inv * (e - xh * wide(r.xs[2, c:c + CR, :]))).astype(BF16)
+
+        return (1.2, run)
 
     def y_dot(n):
         def run():
             cols = slice(n * NC, (n + 1) * NC)
-            t = dot(oc_ref[0], wo_ref[0, :, cols]) + dot(oc_ref[1], wo_ref[1, :, cols])
-            y_ref[:, cols] = (x_ref[:, cols].astype(F32) + t).astype(BF16)
+            t = dot(r.oc[0], r.wo_all[0, :, cols]) + dot(r.oc[1], r.wo_all[1, :, cols])
+            y_out[:, cols] = (x_in[:, cols].astype(F32) + t).astype(BF16)
 
         return (1, run)
 
-    nn = D // NC
-    rows = range(0, m, CR)
     dn = [dn_dot(n) for n in range(nn)]
-    for _, f in dn[:1]:
-        f()
-    head = [stat(c) for c in rows] + [keep(c) for c in rows]
-    weave(head, [dn[1]])
-    for n in range(2, nn):
-        weave([first(n - 2, c) for c in rows], [dn[n]])
     yd = [y_dot(n) for n in range(nn)]
-    weave([first(nn - 2, c) for c in rows], yd[:1])
-    weave([first(nn - 1, c) for c in rows] + [mean(c) for c in rows], yd[1:2])
-    weave([second(n, c) for n in range(nn) for c in rows], yd[2:])
-    y_out[...] = y_ref[...]
-    dx_out[...] = dx_ref[...]
-    dg_out[...] = dg_ref[...]
-
-
-def out_call(sel, x, dy, o, dq, dk, dv, gain, own, oth, m=256):
+    f = [[first(n, c) for c in lines] for n in range(nn)]
+    sec = [second(n, c) for n in range(nn) for c in lines]
+    out_mat = [dn[:3], dn[3:6], dn[6:], []]
+    out_vec = [[stat(c) for c in lines], f[0] + f[1] + f[2], f[3] + f[4] + f[5], f[6] + f[7] + [mean(c) for c in lines]]
+
+    def body(attn, out):
+        if attn:
+            r.tab[2:4] = r.tab[0:2]
+            r.tab[0] = cos_in[...]
+            r.tab[1] = sin_in[...]
+        for g in range(n_grp):
+            if attn:
+                attn_tick(st, g, n_grp, ([], out_mat[g], out_vec[g]) if out else ())
+            else:
+                weave(out_mat[g], out_vec[g])
+        if out:
+            weave(yd, sec)
+        if attn:
+            row = jnp.clip(step - 1, 0, rows - 1)
+            for c in fetch(row):
+                c.wait()
+            for dst, theirs, mine in ((r.oc, r.o, r.o_own), (r.dqc, r.dq, r.dq_own), (r.dkc, r.dk, r.dk_own), (r.dvc, r.dv, r.dv_own)):
+                dst[oth] = theirs[...]
+                dst[me] = mine[...]
+
+            for acc in (r.dgq, r.dgk):
+                acc[...] = jnp.where(step > 0, acc[...], 0.0)
+
+            @pl.when(step < rows)
+            def _():
+                for c in fetch(step):
+                    c.start()
+
+    @pl.when(step < 2)
+    def _():
+        body(True, False)
+
+    @pl.when((step >= 2) & (step <= rows))
+    def _():
+        body(True, True)
+
+    @pl.when(step > rows)
+    def _():
+        body(False, True)
+        dg_out[...] = r.dg[...]
+        dgq_out[...] = r.dgq[...]
+        dgk_out[...] = r.dgk[...]
+
+
+def tail_call(sel, n, x, dy, cosd, sind, o, dq, dk, dv, gain, qg, kg, own, oth, seq=256):
     T, D = x.shape
     nq, nk = dq.shape[2], dk.shape[2]
-    row = pl.BlockSpec((m, D), lambda i, s: (i, 0))
-    two = lambda c: pl.BlockSpec((2, m, c), lambda i, s: (0, i, 0))
+    n_grp = nk // HD
+    rows = T // seq
+    lag = lambda k, c: pl.BlockSpec((seq, c), lambda i, s: (jnp.clip(i - k, 0, rows - 1), 0))
+    const = lambda *b: pl.BlockSpec(b, lambda i, s: (0,) * len(b), pipeline_mode=pl.Buffered(1))
     hbm = pl.BlockSpec(memory_space=pl.ANY)
+    scratch = attn_scratch(seq, n_grp, nq, nk)
+    scratch.update(
+        wq_all=pltpu.VMEM((2, D, nq), BF16), wk_all=pltpu.VMEM((2, D, nk), BF16), wv_all=pltpu.VMEM((2, D, nk), BF16), wo_all=pltpu.VMEM((2, nq, D), BF16),
+        dn=pltpu.VMEM((seq, D), F32), oc=pltpu.VMEM((2, seq, nq), BF16), dqc=pltpu.VMEM((2, seq, nq), BF16), dkc=pltpu.VMEM((2, seq, nk), BF16), dvc=pltpu.VMEM((2, seq, nk), BF16),
+        o_own=pltpu.VMEM((seq, nq), BF16), dq_own=pltpu.VMEM((seq, nq), BF16), dk_own=pltpu.VMEM((seq, nk), BF16), dv_own=pltpu.VMEM((seq, nk), BF16),
+        xs=pltpu.VMEM((3, seq, HD), F32), dg=pltpu.VMEM((8, D), F32), dgq=pltpu.VMEM((8, HD), F32), dgk=pltpu.VMEM((8, HD), F32), sem=pltpu.SemaphoreType.DMA((12,)))
+    flops = 2 * T * D * (nq + 2 * nk + nq) * 3 + 12 * T * nq * seq
     return pl.pallas_call(
-        functools.partial(out_kernel, m),
+        functools.partial(tail_kernel, seq, n_grp, rows, tuple(scratch)),
         grid_spec=pltpu.PrefetchScalarGridSpec(
             num_scalar_prefetch=1,
-            grid=(T // m,),
-            in_specs=[row, row, two(nq), two(nq), two(nk), two(nk), pl.BlockSpec((1, D), lambda i, s: (0, 0), pipeline_mode=pl.Buffered(1))] + [hbm] * 8,
-            out_specs=[row, row, pl.BlockSpec((8, D), lambda i, s: (0, 0))],
-            scratch_shapes=[
-                pltpu.VMEM((2, D, nq), BF16),
-                pltpu.VMEM((2, D, nk), BF16),
-                pltpu.VMEM((2, D, nk), BF16),
-                pltpu.VMEM((2, nq, D), BF16),
-                pltpu.VMEM((m, D), F32),
-                pltpu.VMEM((2, m, nq), BF16),
-                pltpu.VMEM((m, D), BF16),
-                pltpu.VMEM((m, D), BF16),
-                pltpu.VMEM((3, m, HD), F32),
-                pltpu.VMEM((8, D), F32),
-                pltpu.SemaphoreType.DMA((8,)),
-            ],
+            grid=(rows + 2,),
+            in_specs=[lag(0, D), lag(0, D), lag(0, HD), lag(0, HD), lag(2, D), lag(2, D), const(1, D), const(1, HD), const(1, HD)] + [hbm] * 12,
+            out_specs=[lag(2, D), lag(2, D), pl.BlockSpec((8, D), lambda i, s: (0, 0))] + [pl.BlockSpec((8, HD), lambda i, s: (0, 0))] * 2,
+            scratch_shapes=list(scratch.values()),
         ),
-        out_shape=[jax.ShapeDtypeStruct((T, D), BF16)] * 2 + [jax.ShapeDtypeStruct((8, D), F32)],
-        compiler_params=pltpu.CompilerParams(dimension_semantics=("arbitrary",), vmem_limit_bytes=60 << 20),
-        cost_estimate=pl.CostEstimate(flops=2 * T * D * 2 * (2 * nq + 2 * nk), bytes_accessed=T * D * 8 + T * (4 * nq + 4 * nk) * 2, transcendentals=T),
-        name="out",
-    )(sel, x, dy, o, dq, dk, dv, gain, *own, *oth)
+        out_shape=[jax.ShapeDtypeStruct((T, D), BF16)] * 2 + [jax.ShapeDtypeStruct((8, c), F32) for c in (D, HD, HD)],
+        compiler_params=pltpu.CompilerParams(dimension_semantics=("arbitrary",), vmem_limit_bytes=67043328),
+        cost_estimate=pl.CostEstimate(flops=flops, bytes_accessed=T * D * 14, transcendentals=T * nq * 2),
+        name="tail",
+    )(sel, n, dy, cosd, sind, x, dy, gain, qg, kg, *own, *oth, o, dq, dk, dv)
 
 
 def solution(mesh):
@@ -563,18 +913,14 @@
         x, dy = x_in.reshape(T, D), dy_in.reshape(T, D)
         me = lax.axis_index("tp").astype(jnp.int32)
         own = me.reshape(1)
-        other = 1 - own
-
-        part = lax.axis_index("dp") % 2
-        cut = lambda w: lax.dynamic_slice_in_dim(w, part * (w.shape[0] // 2), w.shape[0] // 2, 0)
-        share = jnp.concatenate([jnp.concatenate([cut(w_q), cut(w_k), cut(w_v)], axis=1), cut(w_o)], axis=0).astype(F32)
+
+        part = (lax.axis_index("dp") % 2).astype(jnp.int32).reshape(1)
+        share = pack_call(part, w_q, w_k, w_v, w_o)
         share = lax.ppermute(share, "tp", [(0, 1), (1, 0)])
         gathered = lax.all_gather(share, "dp", axis_index_groups=[[2 * i, 2 * i + 1] for i in range(n_dp // 2)])
-
-        inv_freq = THETA ** (-jnp.arange(0, HD, 2, dtype=F32) / HD)
-        angles = positions.reshape(T, 1).astype(F32) * inv_freq
-        cos, sin = jnp.cos(angles), jnp.sin(angles)
-        cosd, sind = jnp.concatenate([cos, cos], axis=1), jnp.concatenate([-sin, sin], axis=1)
+        gathered = gathered.reshape(-1, *gathered.shape[2:])
+
+        cosd, sind = table_call(positions)
         gain = g_attn.astype(F32).reshape(1, D)
         qg, kg = q_gain.astype(F32).reshape(1, HD), k_gain.astype(F32).reshape(1, HD)
 
@@ -583,12 +929,11 @@
         (dw_q,) = dw_call(own, n, [dq])
         dw_k, dw_v = dw_call(own, n, [dk, dv])
         dw_o, dw_q, dw_k, dw_v = lax.psum((dw_o, dw_q, dw_k, dw_v), "dp")
-        q_sum, k_sum = lax.psum((jnp.sum(dgq, axis=0), jnp.sum(dgk, axis=0)), ("tp", "dp"))
 
         theirs = unpack_call(gathered, D, nq, nk)
-        o, dq, dk, dv = attn_call(False, other, n, dy, cosd, sind, gain, qg, kg, *theirs, prev=(o, dq, dk, dv), seq=n_seq)
-        y, dx, dg = out_call(own, x, dy, o, dq, dk, dv, gain, (w_q, w_k, w_v, w_o), theirs)
-        g_sum = lax.psum(jnp.sum(dg, axis=0), "dp")
+        y, dx, dg, dgq2, dgk2 = tail_call(own, n, x, dy, cosd, sind, o, dq, dk, dv, gain, qg, kg, (w_q, w_k, w_v, w_o), theirs, seq=n_seq)
+        small = lax.psum(jnp.sum(jnp.concatenate([dg, dgq + dgq2, dgk + dgk2], axis=1), axis=0), "dp")
+        g_sum, q_sum, k_sum = small[:D], small[D:D + HD], small[D + HD:]
         return y.reshape(x_in.shape), dx.reshape(x_in.shape), dw_q, dw_k, dw_v, dw_o, q_sum, k_sum, g_sum
 
     return jax.shard_map(per_device, mesh=mesh, in_specs=(tok_spec, tok_spec, P("dp", None), P(), P(), P(), col_spec, col_spec, col_spec, row_spec), out_specs=(tok_spec, tok_spec, col_spec, col_spec, col_spec, row_spec, P(), P(), P()), check_vma=False)

time: 1250 us -> 1180 us (0.944)
  other arithmetic: 59 us -> 3.99 us
  blocking collectives: 32.2 us -> 11.3 us
    pallas_call x1 -> x3, Pallas kernels: 249 us -> 459 us  [the longest x1 443 us: tail_call(): pl.pallas_call(functools.partial(tail_kernel, seq, n_grp, rows, tuple(scr...]
    pallas_call x2 -> x1, Pallas kernels: 425 us -> 223 us  [attn_call(): pl.pallas_call(functools.partial(attn_kernel, own, seq, n_grp), grid_spec...]
    convert_element_type x1 -> x0, other arithmetic: 25.4 us -> none  [per_device(): jnp.concatenate([jnp.concatenate([cut(w_q), cut(w_k), cut(w_v)], axis=1),...]
    psum x2 -> x1, blocking collectives: 32.2 us -> 11.3 us  [per_device(): lax.psum(jnp.sum(jnp.concatenate([dg, dgq + dgq2, dgk + dgk2], axis=1), a...]
    neg x1 -> x0, other arithmetic: 18.1 us -> none  [per_device(): -sin]
    concatenate x1 -> x0, other arithmetic: 13.5 us -> none  [per_device(): jnp.concatenate([cos, cos], axis=1)]
  transfers between devices with their start and end apart: 3 -> 3, of which waited for: 1 -> 1; matrix products, arithmetic and copies ran while one was open for 3% -> 0% of each run, Pallas kernels for 67% -> 71%
where the time goes in v3:
time: 1180 us; the launch traced here: 1170 us
  Pallas kernels  842 us (71%)
  waiting for transfers between devices  271 us (23%)
  local copies, waits for them, and re-layouts  21 us (2%)
  between operations  15.9 us (1%)
    pallas_call x1, Pallas kernels, tail_call(): pl.pallas_call(functools.partial(tail_kernel, seq, n_grp, rows, tuple(scr...  443 us
    ppermute x1, waiting for transfers between devices, per_device(): share = lax.ppermute(share, 'tp', [(0, 1), (1, 0)])  271 us
    pallas_call x1, Pallas kernels, attn_call(): pl.pallas_call(functools.partial(attn_kernel, own, seq, n_grp), grid_spec...  223 us
    pallas_call x3, Pallas kernels, dw_call(): pl.pallas_call(functools.partial(dw_kernel, len(bs)), grid_spec=pltpu.Pre...  145 us
  transfers between devices with their start and end apart: 3, of which 1 were waited for; matrix products, arithmetic and copies ran while one was open for 0% of the time, Pallas kernels for 71%

profile of v3, /device:TPU:0, one launch (start us, length us, event | category | flops | bytes accessed | tf_op | source)
XLA Modules:
  0.0 1168.3 jit_solution(2239977008216988509)
XLA Ops:
  8.1 7.8 pack.1
  15.8 3.4 collective-permute-start
  19.2 270.7 %collective-permute-done = f32[4,384,2048]{2,1,0:T(8,128)} collective-permute-done((f32[4,384,2048]{2,1,0:T(8,128)}, f32[4,384,2048]{2,1,0:T(8,128)}, u32[]{:S(2)}, u32[]{:S(2)}) %collective-permute-start) | collective-permute-done | bytes 12582944 | tf_op jit(solution)/shard_map/ppermute | solution.py:919
  289.9 0.6 reshape.71
  290.5 0.6 maximum_bitcast_fusion.freq_ref
  291.1 8.2 table.1
  299.4 0.5 bitcast_convert_fusion
  299.9 223.1 %attn_own.1 = (bf16[8192,2048]{1,0:T(8,128)(2,1)}, bf16[2,8192,1024]{2,1,0:T(8,128)(2,1)}, bf16[2,8192,1024]{2,1,0:T(8,128)(2,1)}, bf16[2,8192,512]{2,1,0:T(8,12...) custom-call(s32[1]{0:T(128)} %bitcast.sel_ref, bf16[8192,2048]{1,0:T(8,128)(2,1)} %bitcast.19, ...), custom_call_target="tpu_custom_call" | custom-call | flops 128849018880 | bytes 150994944 | tf_op jit(solution)/shard_map/attn_own/pallas_call | solution.py:322
  523.0 46.6 %shard_map.171 = f32[1024,2048]{1,0:T(8,128)} custom-call(s32[1]{0:T(128)} %bitcast.sel_ref, bf16[2,8192,1024]{2,1,0:T(8,128)(2,1)} %get-tuple-element.36.refs_8_.a_ref, bf16[8192,2048]{1,0:T(8,128)(2,1)} %bitcast.23), custom_call_target="tpu_custom_call" | custom-call | flops 34359738368 | bytes 58720256 | tf_op jit(solution)/shard_map/pallas_call | solution.py:402
  569.6 49.3 %shard_map.169 = f32[2048,1024]{1,0:T(8,128)} custom-call(s32[1]{0:T(128)} %bitcast.sel_ref, bf16[8192,2048]{1,0:T(8,128)(2,1)} %get-tuple-element.31.n_in.a_ref, bf16[2,8192,1024]{2,1,0:T(8,128)(2,1)} %get-tuple-element.37.refs_9_.refs_0_), custom_call_target="tpu_custom_call" | custom-call | flops 34359738368 | bytes 58720256 | tf_op jit(solution)/shard_map/pallas_call | solution.py:402
  618.9 49.4 %shard_map.170 = (f32[2048,512]{1,0:T(8,128)}, f32[2048,512]{1,0:T(8,128)}) custom-call(s32[1]{0:T(128)} %bitcast.sel_ref, bf16[8192,2048]{1,0:T(8,128)(2,1)} %get-tuple-element.31.n_in.a_ref, bf16[2,8192,512]{2,1,0:T(8,128)(2,1)} %get-tuple-element.38.refs_10_.refs_0_, bf16[2,8192,512]{2,1,0:T(8,128)(2,1)} %get-tuple-element.39.refs_11_.refs_1_), custom_call_target="tpu_custom_call" | custom-call | flops 34359738368 | bytes 58720256 | tf_op jit(solution)/shard_map/pallas_call | solution.py:402
  668.4 14.7 %unpack.1 = (bf16[2048,1024]{1,0:T(8,128)(2,1)}, bf16[2048,512]{1,0:T(8,128)(2,1)}, bf16[2048,512]{1,0:T(8,128)(2,1)}, bf16[1024,2048]{1,0:T(8,128)(2,1)}) custom-call(f32[8,384,2048]{2,1,0:T(8,128)} %all-gather.3.cloned.1.call-done.f_ref), custom_call_target="tpu_custom_call" | custom-call | flops 6291456 | bytes 37748736 | tf_op jit(solution)/shard_map/unpack/pallas_call | solution.py:370
  683.1 442.8 %tail.1 = (bf16[8192,2048]{1,0:T(8,128)(2,1)}, bf16[8192,2048]{1,0:T(8,128)(2,1)}, f32[8,2048]{1,0:T(8,128)}, f32[8,128]{1,0:T(8,128)}, f32[8,128]{1,0:T(8,128)}) custom-call(s32[1]{0:T(128)} %bitcast.sel_ref, bf16[8192,2048]{1,0:T(8,128)(2,1)} %get-tuple-element.31.n_in.a_ref, bf16[8192,2048]{1,0:T(8,128)(2,1)} %bitcast.24, ...), custom_call_target="tpu_custom_call" | custom-call | flops 335007449088 | bytes 234881024 | tf_op jit(solution)/shard_map/tail/pallas_call | solution.py:887
  1125.9 0.7 add.21
  1126.6 0.7 add.22
  1127.3 0.9 maximum_reduce_fusion
  1128.2 11.3 psum.39
  1139.4 0.6 slice.14
  1140.6 8.6 copy.23
  1149.2 2.1 copy.24
  1151.3 1.6 copy-done
  1152.9 2.1 copy.25
  1155.0 2.1 slice-done.1
  1157.1 3.4 copy.26
  (21 shorter events, 0.7 us)
Async XLA Ops:
  8.0 660.4 %all-gather.3.cloned.1.call-start = ((), (), s32[]{:S(2)}) async-start(), calls=%async_computation | async-start | bytes 37748736 | tf_op jit(solution)/shard_map/all_gather | solution.py:920
  15.8 274.1 %copy-start.2 = (bf16[2048]{0:T(1024)(128)(2,1)S(1)}, bf16[2048]{0:T(1024)(128)(2,1)}, u32[]{:S(2)}) copy-start(bf16[2048]{0:T(1024)(128)(2,1)} %param.13) | copy-start | bytes 12292
  15.8 283.5 %copy-start.3 = (bf16[128]{0:T(256)(128)(2,1)S(1)}, bf16[128]{0:T(256)(128)(2,1)}, u32[]{:S(2)}) copy-start(bf16[128]{0:T(256)(128)(2,1)} %param.15) | copy-start | bytes 772
  15.8 283.5 %copy-start.4 = (bf16[128]{0:T(256)(128)(2,1)S(1)}, bf16[128]{0:T(256)(128)(2,1)}, u32[]{:S(2)}) copy-start(bf16[128]{0:T(256)(128)(2,1)} %param.14) | copy-start | bytes 772
  15.8 274.0 %collective-permute-start = (f32[4,384,2048]{2,1,0:T(8,128)}, f32[4,384,2048]{2,1,0:T(8,128)}, u32[]{:S(2)}, u32[]{:S(2)}) collective-permute-start(f32[4,384,2048]{2,1,0:T(8,128)} %pack.1), channel_id=1, source_target_pairs={{0,4},{4,0},{1,5},{5,1},{2,6},{6,2},{3,7},{7,3}} | collective-permute-start | bytes 37748744 | tf_op jit(solution)/shard_map/ppermute | solution.py:919
  289.9 850.7 %all-reduce.3.cloned.1.call-start = ((), (), s32[]{:S(2)}) async-start(), calls=%async_computation.1 | async-start | bytes 50331648 | tf_op jit(solution)/shard_map/psum | solution.py:931
  1140.6 8.6 copy-start.1
  1149.2 3.7 copy-start
  1149.2 5.8 slice-start
  1152.9 4.2 slice-start.1
Sparse Core Ops, SparseCore 0:
  290.0 38.7 all-gather.2
Sparse Core Ops, SparseCore 1:
  668.5 418.4 all-reduce.2

commit v4 on v3

--- a/solution.py
+++ b/solution.py
@@ -379,68 +379,12 @@
     )(gathered)
 
 
-def dw_kernel(n_out, sel_ref, a_ref, *refs):
-    a = a_ref[0] if len(a_ref.shape) == 3 else a_ref[...]
-    for b_ref, out_ref in zip(refs[:n_out], refs[n_out:]):
-        b = b_ref[0] if len(b_ref.shape) == 3 else b_ref[...]
-
-        @pl.when(pl.program_id(0) == 0)
-        def _():
-            out_ref[...] = jnp.zeros_like(out_ref)
-
-        out_ref[...] += dot(a, b, TN)
-
-
-def dw_call(sel, a, bs, tile=1024):
-    def spec(v):
-        if v.ndim == 3:
-            return pl.BlockSpec((1, tile, v.shape[2]), lambda i, s: (s[0], i, 0))
-        return pl.BlockSpec((tile, v.shape[1]), lambda i, s: (i, 0))
-
-    T, M = a.shape[-2:]
-    width = sum(b.shape[-1] for b in bs)
-    return pl.pallas_call(
-        functools.partial(dw_kernel, len(bs)),
-        grid_spec=pltpu.PrefetchScalarGridSpec(
-            num_scalar_prefetch=1,
-            grid=(T // tile,),
-            in_specs=[spec(a)] + [spec(b) for b in bs],
-            out_specs=[pl.BlockSpec((M, b.shape[-1]), lambda i, s: (0, 0)) for b in bs],
-        ),
-        out_shape=[jax.ShapeDtypeStruct((M, b.shape[-1]), F32) for b in bs],
-        compiler_params=pltpu.CompilerParams(dimension_semantics=("arbitrary",), vmem_limit_bytes=56 << 20),
-        cost_estimate=pl.CostEstimate(flops=2 * T * M * width, bytes_accessed=2 * T * (M + width) + 4 * M * width, transcendentals=0),
-    )(sel, a, *bs)
-
-
-def pack_kernel(sel_ref, q_ref, k_ref, v_ref, o_ref, out_ref):
+def pre_kernel(sel_ref, q_ref, k_ref, v_ref, o_ref, pos_ref, freq_ref, out_ref, cos_ref, sin_ref):
     d, nq, nk = q_ref.shape[0], q_ref.shape[1], k_ref.shape[1]
     out_ref[0, 0:d, 0:nq] = q_ref[...].astype(F32)
     out_ref[0, 0:d, nq:nq + nk] = k_ref[...].astype(F32)
     out_ref[0, 0:d, nq + nk:] = v_ref[...].astype(F32)
     out_ref[0, d:, :] = o_ref[...].astype(F32)
-
-
-def pack_call(part, w_q, w_k, w_v, w_o, parts=2, cuts=4):
-    D, nq = w_q.shape
-    spec = lambda w: pl.BlockSpec((w.shape[0] // (parts * cuts), w.shape[1]), lambda i, s: (s[0] * cuts + i, 0))
-    r = (D + nq) // (parts * cuts)
-    return pl.pallas_call(
-        pack_kernel,
-        grid_spec=pltpu.PrefetchScalarGridSpec(
-            num_scalar_prefetch=1,
-            grid=(cuts,),
-            in_specs=[spec(w) for w in (w_q, w_k, w_v, w_o)],
-            out_specs=pl.BlockSpec((1, r, D), lambda i, s: (i, 0, 0)),
-        ),
-        out_shape=jax.ShapeDtypeStruct((cuts, r, D), F32),
-        compiler_params=pltpu.CompilerParams(dimension_semantics=("arbitrary",), vmem_limit_bytes=60 << 20),
-        cost_estimate=pl.CostEstimate(flops=cuts * r * D, bytes_accessed=cuts * r * D * 6, transcendentals=0),
-        name="pack",
-    )(part, w_q, w_k, w_v, w_o)
-
-
-def table_kernel(pos_ref, freq_ref, cos_ref, sin_ref):
     n, seq = pos_ref.shape
     lane = lax.broadcasted_iota(jnp.int32, (HD, HD), 1)
     for r in range(n):
@@ -460,21 +404,84 @@
             sin_ref[rows, :] = jnp.where(((q & 2) == 0) == (lane >= HD // 2), si, -si)
 
 
-def table_call(positions, rows=8):
+def pre_call(part, w_q, w_k, w_v, w_o, positions, parts=2, cuts=4):
+    D, nq = w_q.shape
     n, seq = positions.shape
+    rows = n // cuts
     freq = THETA ** (-jnp.arange(0, HD, 2, dtype=F32) / HD)
     freq = jnp.concatenate([freq, freq]).reshape(1, HD)
-    out = pl.BlockSpec((rows * seq, HD), lambda i: (i, 0))
+    spec = lambda w: pl.BlockSpec((w.shape[0] // (parts * cuts), w.shape[1]), lambda i, s: (s[0] * cuts + i, 0))
+    r = (D + nq) // (parts * cuts)
+    table = pl.BlockSpec((rows * seq, HD), lambda i, s: (i, 0))
     return pl.pallas_call(
-        table_kernel,
-        grid=(n // rows,),
-        in_specs=[pl.BlockSpec((rows, seq), lambda i: (i, 0)), pl.BlockSpec((1, HD), lambda i: (0, 0))],
-        out_specs=[out, out],
-        out_shape=[jax.ShapeDtypeStruct((n * seq, HD), F32)] * 2,
+        pre_kernel,
+        grid_spec=pltpu.PrefetchScalarGridSpec(
+            num_scalar_prefetch=1,
+            grid=(cuts,),
+            in_specs=[spec(w) for w in (w_q, w_k, w_v, w_o)] + [pl.BlockSpec((rows, seq), lambda i, s: (i, 0)), pl.BlockSpec((1, HD), lambda i, s: (0, 0))],
+            out_specs=[pl.BlockSpec((1, r, D), lambda i, s: (i, 0, 0)), table, table],
+        ),
+        out_shape=[jax.ShapeDtypeStruct((cuts, r, D), F32)] + [jax.ShapeDtypeStruct((n * seq, HD), F32)] * 2,
         compiler_params=pltpu.CompilerParams(dimension_semantics=("arbitrary",), vmem_limit_bytes=60 << 20),
-        cost_estimate=pl.CostEstimate(flops=n * seq * HD * 30, bytes_accessed=n * seq * HD * 8, transcendentals=0),
-        name="table",
-    )(positions, freq)
+        cost_estimate=pl.CostEstimate(flops=n * seq * HD * 30, bytes_accessed=cuts * r * D * 6 + n * seq * HD * 8, transcendentals=0),
+        name="pre",
+    )(part, w_q, w_k, w_v, w_o, positions, freq)
+
+
+def dw_kernel(n_b, sel_ref, a_ref, *refs):
+    bs, outs, accs, (at_ref, sem) = refs[:n_b], refs[n_b:2 * n_b], refs[2 * n_b:3 * n_b], refs[3 * n_b:]
+    flat = lambda ref: ref.at[0] if len(ref.shape) == 3 else ref
+    a, bs = flat(a_ref), [flat(b) for b in bs]
+    M, tile = at_ref.shape
+    step = pl.program_id(0)
+
+    @pl.when(step == 0)
+    def _():
+        for acc in accs:
+            acc[...] = jnp.zeros_like(acc)
+
+    def part(acc, b, c):
+        def run():
+            acc[:, c:c + 256] += dot(at_ref[...], b[:, c:c + 256])
+
+        return (1, run)
+
+    for c in range(0, M, 256):
+        for k in range(0, tile, 256):
+            at_ref[c:c + 256, k:k + 256] = a[k:k + 256, c:c + 256].T
+    weave([part(acc, b, c) for acc, b in zip(accs, bs) for c in range(0, b.shape[1], 256)])
+
+    @pl.when(step == pl.num_programs(0) - 1)
+    def _():
+        copies = [pltpu.make_async_copy(acc, out, sem.at[k]) for k, (acc, out) in enumerate(zip(accs, outs))]
+        for c in copies:
+            c.start()
+        for c in copies:
+            c.wait()
+
+
+def dw_call(sel, a, bs, tile):
+    def spec(v):
+        if v.ndim == 3:
+            return pl.BlockSpec((1, tile, v.shape[2]), lambda i, s: (s[0], i, 0))
+        return pl.BlockSpec((tile, v.shape[1]), lambda i, s: (i, 0))
+
+    T, M = a.shape[-2:]
+    shapes = [(M, b.shape[-1]) for b in bs]
+    width = sum(s[1] for s in shapes)
+    return pl.pallas_call(
+        functools.partial(dw_kernel, len(bs)),
+        grid_spec=pltpu.PrefetchScalarGridSpec(
+            num_scalar_prefetch=1,
+            grid=(T // tile,),
+            in_specs=[spec(a)] + [spec(b) for b in bs],
+            out_specs=[pl.BlockSpec(memory_space=pl.ANY)] * len(bs),
+            scratch_shapes=[pltpu.VMEM(s, F32) for s in shapes] + [pltpu.VMEM((M, tile), BF16), pltpu.SemaphoreType.DMA((len(bs),))],
+        ),
+        out_shape=[jax.ShapeDtypeStruct(s, F32) for s in shapes],
+        compiler_params=pltpu.CompilerParams(dimension_semantics=("arbitrary",), vmem_limit_bytes=60 << 20),
+        cost_estimate=pl.CostEstimate(flops=2 * T * M * width, bytes_accessed=2 * T * (M + width) + 4 * M * width, transcendentals=0),
+    )(sel, a, *bs)
 
 
 def attn_stages(seq, n_grp, r):
@@ -815,6 +822,7 @@
             cols = slice(n * NC, (n + 1) * NC)
             t = dot(r.oc[0], r.wo_all[0, :, cols]) + dot(r.oc[1], r.wo_all[1, :, cols])
             y_out[:, cols] = (x_in[:, cols].astype(F32) + t).astype(BF16)
+            r.xs[3 + me, 0:8, :] = t[0:8, :HD]
 
         return (1, run)
 
@@ -822,8 +830,9 @@
     yd = [y_dot(n) for n in range(nn)]
     f = [[first(n, c) for c in lines] for n in range(nn)]
     sec = [second(n, c) for n in range(nn) for c in lines]
-    out_mat = [dn[:3], dn[3:6], dn[6:], []]
-    out_vec = [[stat(c) for c in lines], f[0] + f[1] + f[2], f[3] + f[4] + f[5], f[6] + f[7] + [mean(c) for c in lines]]
+    k = nn // 2
+    out_mat = [dn[:k], dn[k:], yd[:3], yd[3:]]
+    out_vec = [[stat(c) for c in lines], sum(f[:k], []), sum(f[k:], []) + [mean(c) for c in lines], sec]
 
     def body(attn, out):
         if attn:
@@ -835,8 +844,6 @@
                 attn_tick(st, g, n_grp, ([], out_mat[g], out_vec[g]) if out else ())
             else:
                 weave(out_mat[g], out_vec[g])
-        if out:
-            weave(yd, sec)
         if attn:
             row = jnp.clip(step - 1, 0, rows - 1)
             for c in fetch(row):
@@ -882,7 +889,7 @@
         wq_all=pltpu.VMEM((2, D, nq), BF16), wk_all=pltpu.VMEM((2, D, nk), BF16), wv_all=pltpu.VMEM((2, D, nk), BF16), wo_all=pltpu.VMEM((2, nq, D), BF16),
         dn=pltpu.VMEM((seq, D), F32), oc=pltpu.VMEM((2, seq, nq), BF16), dqc=pltpu.VMEM((2, seq, nq), BF16), dkc=pltpu.VMEM((2, seq, nk), BF16), dvc=pltpu.VMEM((2, seq, nk), BF16),
         o_own=pltpu.VMEM((seq, nq), BF16), dq_own=pltpu.VMEM((seq, nq), BF16), dk_own=pltpu.VMEM((seq, nk), BF16), dv_own=pltpu.VMEM((seq, nk), BF16),
-        xs=pltpu.VMEM((3, seq, HD), F32), dg=pltpu.VMEM((8, D), F32), dgq=pltpu.VMEM((8, HD), F32), dgk=pltpu.VMEM((8, HD), F32), sem=pltpu.SemaphoreType.DMA((12,)))
+        xs=pltpu.VMEM((5, seq, HD), F32), dg=pltpu.VMEM((8, D), F32), dgq=pltpu.VMEM((8, HD), F32), dgk=pltpu.VMEM((8, HD), F32), sem=pltpu.SemaphoreType.DMA((12,)))
     flops = 2 * T * D * (nq + 2 * nk + nq) * 3 + 12 * T * nq * seq
     return pl.pallas_call(
         functools.partial(tail_kernel, seq, n_grp, rows, tuple(scratch)),
@@ -915,19 +922,17 @@
         own = me.reshape(1)
 
         part = (lax.axis_index("dp") % 2).astype(jnp.int32).reshape(1)
-        share = pack_call(part, w_q, w_k, w_v, w_o)
+        share, cosd, sind = pre_call(part, w_q, w_k, w_v, w_o, positions)
         share = lax.ppermute(share, "tp", [(0, 1), (1, 0)])
         gathered = lax.all_gather(share, "dp", axis_index_groups=[[2 * i, 2 * i + 1] for i in range(n_dp // 2)])
         gathered = gathered.reshape(-1, *gathered.shape[2:])
 
-        cosd, sind = table_call(positions)
         gain = g_attn.astype(F32).reshape(1, D)
         qg, kg = q_gain.astype(F32).reshape(1, HD), k_gain.astype(F32).reshape(1, HD)
 
         n, o, dq, dk, dv, dgq, dgk = attn_call(True, own, x, dy, cosd, sind, gain, qg, kg, w_q, w_k, w_v, w_o, seq=n_seq)
-        (dw_o,) = dw_call(own, o, [dy])
-        (dw_q,) = dw_call(own, n, [dq])
-        dw_k, dw_v = dw_call(own, n, [dk, dv])
+        dw_q, dw_k, dw_v = dw_call(own, n, [dq, dk, dv], 512)
+        (dw_o,) = dw_call(own, o, [dy], 1024)
         dw_o, dw_q, dw_k, dw_v = lax.psum((dw_o, dw_q, dw_k, dw_v), "dp")
 
         theirs = unpack_call(gathered, D, nq, nk)

time: 1180 us -> 1170 us (level)
    pallas_call x3 -> x2, Pallas kernels: 145 us -> 124 us  [dw_call(): pl.pallas_call(functools.partial(dw_kernel, len(bs)), grid_spec=pltpu.Pre...]
    pallas_call x1, Pallas kernels: 443 us -> 462 us  [tail_call(): pl.pallas_call(functools.partial(tail_kernel, seq, n_grp, rows, tuple(scr...]
where the time goes in v4:
time: 1170 us; the launch traced here: 1160 us
  Pallas kernels  834 us (71%)
  waiting for transfers between devices  271 us (23%)
  local copies, waits for them, and re-layouts  21 us (2%)
  between operations  16 us (1%)
    pallas_call x1, Pallas kernels, tail_call(): pl.pallas_call(functools.partial(tail_kernel, seq, n_grp, rows, tuple(scr...  462 us
    ppermute x1, waiting for transfers between devices, per_device(): share = lax.ppermute(share, 'tp', [(0, 1), (1, 0)])  271 us
    pallas_call x1, Pallas kernels, attn_call(): pl.pallas_call(functools.partial(attn_kernel, own, seq, n_grp), grid_spec...  221 us
    pallas_call x2, Pallas kernels, dw_call(): pl.pallas_call(functools.partial(dw_kernel, len(bs)), grid_spec=pltpu.Pre...  124 us
  transfers between devices with their start and end apart: 3, of which 1 were waited for; matrix products, arithmetic and copies ran while one was open for 0% of the time, Pallas kernels for 71%

profile of v4, /device:TPU:0, one launch (start us, length us, event | category | flops | bytes accessed | tf_op | source)
XLA Modules:
  0.0 1158.8 jit_solution(8114645419323769439)
XLA Ops:
  8.1 0.6 maximum_bitcast_fusion.freq_ref
  8.7 11.4 pre.1
  20.1 3.4 collective-permute-start
  23.4 270.7 %collective-permute-done = f32[4,384,2048]{2,1,0:T(8,128)} collective-permute-done((f32[4,384,2048]{2,1,0:T(8,128)}, f32[4,384,2048]{2,1,0:T(8,128)}, u32[]{:S(2)}, u32[]{:S(2)}) %collective-permute-start) | collective-permute-done | bytes 12582944 | tf_op jit(solution)/shard_map/ppermute | solution.py:926
  294.1 0.0 all-reduce.3.cloned.1.call-start
  294.2 0.6 reshape.71
  294.8 0.5 bitcast_convert_fusion
  295.3 221.4 %attn_own.1 = (bf16[8192,2048]{1,0:T(8,128)(2,1)}, bf16[2,8192,1024]{2,1,0:T(8,128)(2,1)}, bf16[2,8192,1024]{2,1,0:T(8,128)(2,1)}, bf16[2,8192,512]{2,1,0:T(8,12...) custom-call(s32[1]{0:T(128)} %bitcast.sel_ref, bf16[8192,2048]{1,0:T(8,128)(2,1)} %bitcast.19, ...), custom_call_target="tpu_custom_call" | custom-call | flops 128849018880 | bytes 150994944 | tf_op jit(solution)/shard_map/attn_own/pallas_call | solution.py:322
  516.7 43.2 %shard_map.170 = f32[1024,2048]{1,0:T(8,128)} custom-call(s32[1]{0:T(128)} %bitcast.sel_ref, bf16[2,8192,1024]{2,1,0:T(8,128)(2,1)} %get-tuple-element.39.refs_8_.a_ref, bf16[8192,2048]{1,0:T(8,128)(2,1)} %bitcast.23), custom_call_target="tpu_custom_call" | custom-call | flops 34359738368 | bytes 58720256 | tf_op jit(solution)/shard_map/pallas_call | solution.py:472
  560.0 81.2 %shard_map.169 = (f32[2048,1024]{1,0:T(8,128)}, f32[2048,512]{1,0:T(8,128)}, f32[2048,512]{1,0:T(8,128)}) custom-call(s32[1]{0:T(128)} %bitcast.sel_ref, bf16[8192,2048]{1,0:T(8,128)(2,1)} %get-tuple-element.33.n_in.a_ref, bf16[2,8192,1024]{2,1,0:T(8,128)(2,1)} %get-tuple-element.40.refs_9_.refs_0_, ...), custom_call_target="tpu_custom_call" | custom-call | flops 68719476736 | bytes 83886080 | tf_op jit(solution)/shard_map/pallas_call | solution.py:472
  641.2 14.7 %unpack.1 = (bf16[2048,1024]{1,0:T(8,128)(2,1)}, bf16[2048,512]{1,0:T(8,128)(2,1)}, bf16[2048,512]{1,0:T(8,128)(2,1)}, bf16[1024,2048]{1,0:T(8,128)(2,1)}) custom-call(f32[8,384,2048]{2,1,0:T(8,128)} %all-gather.3.cloned.1.call-done.f_ref), custom_call_target="tpu_custom_call" | custom-call | flops 6291456 | bytes 37748736 | tf_op jit(solution)/shard_map/unpack/pallas_call | solution.py:370
  655.9 461.6 %tail.1 = (bf16[8192,2048]{1,0:T(8,128)(2,1)}, bf16[8192,2048]{1,0:T(8,128)(2,1)}, f32[8,2048]{1,0:T(8,128)}, f32[8,128]{1,0:T(8,128)}, f32[8,128]{1,0:T(8,128)}) custom-call(s32[1]{0:T(128)} %bitcast.sel_ref, bf16[8192,2048]{1,0:T(8,128)(2,1)} %get-tuple-element.33.n_in.a_ref, bf16[8192,2048]{1,0:T(8,128)(2,1)} %bitcast.24, ...), custom_call_target="tpu_custom_call" | custom-call | flops 335007449088 | bytes 234881024 | tf_op jit(solution)/shard_map/tail/pallas_call | solution.py:894
  1117.5 0.7 add.21
  1118.2 0.7 add.22
  1118.9 0.9 maximum_reduce_fusion
  1119.8 10.1 psum.39
  1129.9 0.6 slice.14
  1130.5 0.5 fusion
  1131.0 8.6 copy.23
  1139.6 2.1 copy.24
  1141.8 1.6 copy-done
  1143.3 2.1 copy.25
  1145.5 2.1 slice-done.1
  1147.5 3.4 copy.26
  (19 shorter events, 0.1 us)
Async XLA Ops:
  8.0 633.2 %all-gather.3.cloned.1.call-start = ((), (), s32[]{:S(2)}) async-start(), calls=%async_computation | async-start | bytes 37748736 | tf_op jit(solution)/shard_map/all_gather | solution.py:927
  20.1 274.1 %copy-start.2 = (bf16[2048]{0:T(1024)(128)(2,1)S(1)}, bf16[2048]{0:T(1024)(128)(2,1)}, u32[]{:S(2)}) copy-start(bf16[2048]{0:T(1024)(128)(2,1)} %param.13) | copy-start | bytes 12292
  20.1 274.7 %copy-start.3 = (bf16[128]{0:T(256)(128)(2,1)S(1)}, bf16[128]{0:T(256)(128)(2,1)}, u32[]{:S(2)}) copy-start(bf16[128]{0:T(256)(128)(2,1)} %param.15) | copy-start | bytes 772
  20.1 274.7 %copy-start.4 = (bf16[128]{0:T(256)(128)(2,1)S(1)}, bf16[128]{0:T(256)(128)(2,1)}, u32[]{:S(2)}) copy-start(bf16[128]{0:T(256)(128)(2,1)} %param.14) | copy-start | bytes 772
  20.1 274.0 %collective-permute-start = (f32[4,384,2048]{2,1,0:T(8,128)}, f32[4,384,2048]{2,1,0:T(8,128)}, u32[]{:S(2)}, u32[]{:S(2)}) collective-permute-start(f32[4,384,2048]{2,1,0:T(8,128)} %get-tuple-element.34), channel_id=1, source_target_pairs={{0,4},{4,0},{1,5},{5,1},{2,6},{6,2},{3,7},{7,3}} | collective-permute-start | bytes 37748744 | tf_op jit(solution)/shard_map/ppermute | solution.py:926
  294.1 836.9 %all-reduce.3.cloned.1.call-start = ((), (), s32[]{:S(2)}) async-start(), calls=%async_computation.1 | async-start | bytes 50331648 | tf_op jit(solution)/shard_map/psum | solution.py:936
  1131.0 8.6 copy-start.1
  1139.6 3.7 copy-start
  1139.6 5.8 slice-start
  1143.3 4.2 slice-start.1
Sparse Core Ops, SparseCore 0:
  294.2 38.7 all-gather.2
Sparse Core Ops, SparseCore 1:
  641.2 418.3 all-reduce.2

commit v5 on v4

--- a/solution.py
+++ b/solution.py
@@ -355,30 +355,6 @@
     )(sel, *args)
 
 
-def unpack_kernel(f_ref, q_ref, k_ref, v_ref, o_ref):
-    d = q_ref.shape[0]
-    nq, nk = q_ref.shape[1], k_ref.shape[1]
-    q_ref[...] = f_ref[0, 0:d, 0:nq].astype(BF16)
-    k_ref[...] = f_ref[0, 0:d, nq:nq + nk].astype(BF16)
-    v_ref[...] = f_ref[0, 0:d, nq + nk:].astype(BF16)
-    o_ref[...] = f_ref[0, d:, :].astype(BF16)
-
-
-def unpack_call(gathered, D, nq, nk):
-    n, r, c = gathered.shape
-    part = lambda a, b: pl.BlockSpec((a // n, b), lambda i: (i, 0))
-    return pl.pallas_call(
-        unpack_kernel,
-        grid=(n,),
-        in_specs=[pl.BlockSpec((1, r, c), lambda i: (i, 0, 0))],
-        out_specs=[part(D, nq), part(D, nk), part(D, nk), part(nq, D)],
-        out_shape=[jax.ShapeDtypeStruct(s, BF16) for s in ((D, nq), (D, nk), (D, nk), (nq, D))],
-        compiler_params=pltpu.CompilerParams(dimension_semantics=("arbitrary",), vmem_limit_bytes=60 << 20),
-        cost_estimate=pl.CostEstimate(flops=n * r * c, bytes_accessed=n * r * c * 6, transcendentals=0),
-        name="unpack",
-    )(gathered)
-
-
 def pre_kernel(sel_ref, q_ref, k_ref, v_ref, o_ref, pos_ref, freq_ref, out_ref, cos_ref, sin_ref):
     d, nq, nk = q_ref.shape[0], q_ref.shape[1], k_ref.shape[1]
     out_ref[0, 0:d, 0:nq] = q_ref[...].astype(F32)
@@ -428,7 +404,18 @@
     )(part, w_q, w_k, w_v, w_o, positions, freq)
 
 
-def dw_kernel(n_b, sel_ref, a_ref, *refs):
+def dw_kernel(n_b, unpack, sel_ref, a_ref, *refs):
+    if unpack:
+        f_ref, parts = refs[n_b], refs[2 * n_b + 1:2 * n_b + 5]
+        refs = refs[:n_b] + refs[n_b + 1:2 * n_b + 1] + refs[2 * n_b + 5:]
+        q_ref, k_ref, v_ref, o_ref = parts
+        per, nq, nk = f_ref.shape[0], q_ref.shape[1], k_ref.shape[1]
+        d, e = q_ref.shape[0] // per, o_ref.shape[0] // per
+        for j in range(per):
+            q_ref[j * d:(j + 1) * d, :] = f_ref[j, 0:d, 0:nq].astype(BF16)
+            k_ref[j * d:(j + 1) * d, :] = f_ref[j, 0:d, nq:nq + nk].astype(BF16)
+            v_ref[j * d:(j + 1) * d, :] = f_ref[j, 0:d, nq + nk:].astype(BF16)
+            o_ref[j * e:(j + 1) * e, :] = f_ref[j, d:, :].astype(BF16)
     bs, outs, accs, (at_ref, sem) = refs[:n_b], refs[n_b:2 * n_b], refs[2 * n_b:3 * n_b], refs[3 * n_b:]
     flat = lambda ref: ref.at[0] if len(ref.shape) == 3 else ref
     a, bs = flat(a_ref), [flat(b) for b in bs]
@@ -460,7 +447,7 @@
             c.wait()
 
 
-def dw_call(sel, a, bs, tile):
+def dw_call(sel, a, bs, tile, gathered=None, nk=0):
     def spec(v):
         if v.ndim == 3:
             return pl.BlockSpec((1, tile, v.shape[2]), lambda i, s: (s[0], i, 0))
@@ -469,19 +456,29 @@
     T, M = a.shape[-2:]
     shapes = [(M, b.shape[-1]) for b in bs]
     width = sum(s[1] for s in shapes)
+    steps = T // tile
+    more_in, more_out, more_shapes, more = [], [], [], []
+    if gathered is not None:
+        n, r, D = gathered.shape
+        per = n // 2 // steps
+        more = [gathered]
+        more_in = [pl.BlockSpec((per, r, D), lambda i, s: ((1 - s[0]) * steps + i, 0, 0))]
+        nq = D - 2 * nk
+        more_shapes = [jax.ShapeDtypeStruct(s, BF16) for s in ((D, nq), (D, nk), (D, nk), (nq, D))]
+        more_out = [pl.BlockSpec((s.shape[0] // steps, s.shape[1]), lambda i, s: (i, 0)) for s in more_shapes]
     return pl.pallas_call(
-        functools.partial(dw_kernel, len(bs)),
+        functools.partial(dw_kernel, len(bs), gathered is not None),
         grid_spec=pltpu.PrefetchScalarGridSpec(
             num_scalar_prefetch=1,
-            grid=(T // tile,),
-            in_specs=[spec(a)] + [spec(b) for b in bs],
-            out_specs=[pl.BlockSpec(memory_space=pl.ANY)] * len(bs),
+            grid=(steps,),
+            in_specs=[spec(a)] + [spec(b) for b in bs] + more_in,
+            out_specs=[pl.BlockSpec(memory_space=pl.ANY)] * len(bs) + more_out,
             scratch_shapes=[pltpu.VMEM(s, F32) for s in shapes] + [pltpu.VMEM((M, tile), BF16), pltpu.SemaphoreType.DMA((len(bs),))],
         ),
-        out_shape=[jax.ShapeDtypeStruct(s, F32) for s in shapes],
+        out_shape=[jax.ShapeDtypeStruct(s, F32) for s in shapes] + more_shapes,
         compiler_params=pltpu.CompilerParams(dimension_semantics=("arbitrary",), vmem_limit_bytes=60 << 20),
         cost_estimate=pl.CostEstimate(flops=2 * T * M * width, bytes_accessed=2 * T * (M + width) + 4 * M * width, transcendentals=0),
-    )(sel, a, *bs)
+    )(sel, a, *bs, *more)
 
 
 def attn_stages(seq, n_grp, r):
@@ -822,7 +819,6 @@
             cols = slice(n * NC, (n + 1) * NC)
             t = dot(r.oc[0], r.wo_all[0, :, cols]) + dot(r.oc[1], r.wo_all[1, :, cols])
             y_out[:, cols] = (x_in[:, cols].astype(F32) + t).astype(BF16)
-            r.xs[3 + me, 0:8, :] = t[0:8, :HD]
 
         return (1, run)
 
@@ -830,9 +826,8 @@
     yd = [y_dot(n) for n in range(nn)]
     f = [[first(n, c) for c in lines] for n in range(nn)]
     sec = [second(n, c) for n in range(nn) for c in lines]
-    k = nn // 2
-    out_mat = [dn[:k], dn[k:], yd[:3], yd[3:]]
-    out_vec = [[stat(c) for c in lines], sum(f[:k], []), sum(f[k:], []) + [mean(c) for c in lines], sec]
+    out_mat = [dn[:3], dn[3:6], dn[6:], []]
+    out_vec = [[stat(c) for c in lines], f[0] + f[1] + f[2], f[3] + f[4] + f[5], f[6] + f[7] + [mean(c) for c in lines]]
 
     def body(attn, out):
         if attn:
@@ -844,6 +839,8 @@
                 attn_tick(st, g, n_grp, ([], out_mat[g], out_vec[g]) if out else ())
             else:
                 weave(out_mat[g], out_vec[g])
+        if out:
+            weave(yd, sec)
         if attn:
             row = jnp.clip(step - 1, 0, rows - 1)
             for c in fetch(row):
@@ -889,7 +886,7 @@
         wq_all=pltpu.VMEM((2, D, nq), BF16), wk_all=pltpu.VMEM((2, D, nk), BF16), wv_all=pltpu.VMEM((2, D, nk), BF16), wo_all=pltpu.VMEM((2, nq, D), BF16),
         dn=pltpu.VMEM((seq, D), F32), oc=pltpu.VMEM((2, seq, nq), BF16), dqc=pltpu.VMEM((2, seq, nq), BF16), dkc=pltpu.VMEM((2, seq, nk), BF16), dvc=pltpu.VMEM((2, seq, nk), BF16),
         o_own=pltpu.VMEM((seq, nq), BF16), dq_own=pltpu.VMEM((seq, nq), BF16), dk_own=pltpu.VMEM((seq, nk), BF16), dv_own=pltpu.VMEM((seq, nk), BF16),
-        xs=pltpu.VMEM((5, seq, HD), F32), dg=pltpu.VMEM((8, D), F32), dgq=pltpu.VMEM((8, HD), F32), dgk=pltpu.VMEM((8, HD), F32), sem=pltpu.SemaphoreType.DMA((12,)))
+        xs=pltpu.VMEM((3, seq, HD), F32), dg=pltpu.VMEM((8, D), F32), dgq=pltpu.VMEM((8, HD), F32), dgk=pltpu.VMEM((8, HD), F32), sem=pltpu.SemaphoreType.DMA((12,)))
     flops = 2 * T * D * (nq + 2 * nk + nq) * 3 + 12 * T * nq * seq
     return pl.pallas_call(
         functools.partial(tail_kernel, seq, n_grp, rows, tuple(scratch)),
@@ -916,26 +913,23 @@
     def per_device(x_in, dy_in, positions, g_attn, q_gain, k_gain, w_q, w_k, w_v, w_o):
         n_batch, n_seq, D = x_in.shape
         T = n_batch * n_seq
-        nq, nk = w_q.shape[1], w_k.shape[1]
+        nk = w_k.shape[1]
         x, dy = x_in.reshape(T, D), dy_in.reshape(T, D)
         me = lax.axis_index("tp").astype(jnp.int32)
         own = me.reshape(1)
 
-        part = (lax.axis_index("dp") % 2).astype(jnp.int32).reshape(1)
-        share, cosd, sind = pre_call(part, w_q, w_k, w_v, w_o, positions)
-        share = lax.ppermute(share, "tp", [(0, 1), (1, 0)])
-        gathered = lax.all_gather(share, "dp", axis_index_groups=[[2 * i, 2 * i + 1] for i in range(n_dp // 2)])
-        gathered = gathered.reshape(-1, *gathered.shape[2:])
+        part = lax.axis_index("dp").astype(jnp.int32).reshape(1)
+        share, cosd, sind = pre_call(part, w_q, w_k, w_v, w_o, positions, parts=n_dp)
+        gathered = lax.all_gather(share, ("tp", "dp"), tiled=True)
 
         gain = g_attn.astype(F32).reshape(1, D)
         qg, kg = q_gain.astype(F32).reshape(1, HD), k_gain.astype(F32).reshape(1, HD)
 
         n, o, dq, dk, dv, dgq, dgk = attn_call(True, own, x, dy, cosd, sind, gain, qg, kg, w_q, w_k, w_v, w_o, seq=n_seq)
         dw_q, dw_k, dw_v = dw_call(own, n, [dq, dk, dv], 512)
-        (dw_o,) = dw_call(own, o, [dy], 1024)
+        dw_o, *theirs = dw_call(own, o, [dy], 1024, gathered=gathered, nk=nk)
         dw_o, dw_q, dw_k, dw_v = lax.psum((dw_o, dw_q, dw_k, dw_v), "dp")
 
-        theirs = unpack_call(gathered, D, nq, nk)
         y, dx, dg, dgq2, dgk2 = tail_call(own, n, x, dy, cosd, sind, o, dq, dk, dv, gain, qg, kg, (w_q, w_k, w_v, w_o), theirs, seq=n_seq)
         small = lax.psum(jnp.sum(jnp.concatenate([dg, dgq + dgq2, dgk + dgk2], axis=1), axis=0), "dp")
         g_sum, q_sum, k_sum = small[:D], small[D:D + HD], small[D + HD:]

time: 1170 us -> 863 us (0.74)
  waiting for transfers between devices: 271 us -> 0.06 us
  Pallas kernels: 834 us -> 801 us
    ppermute x1 -> x0, waiting for transfers between devices: 271 us -> none  [per_device(): share = lax.ppermute(share, 'tp', [(0, 1), (1, 0)])]
    pallas_call x1, Pallas kernels: 462 us -> 444 us  [tail_call(): pl.pallas_call(functools.partial(tail_kernel, seq, n_grp, rows, tuple(scr...]
    pallas_call x3 -> x2, Pallas kernels: 139 us -> 128 us  [dw_call(): pl.pallas_call(functools.partial(dw_kernel, len(bs), gathered is not None...]
  transfers between devices with their start and end apart: 3 -> 2, of which waited for: 1 -> 0; matrix products, arithmetic and copies ran while one was open for 0% -> 1% of each run, Pallas kernels for 71% -> 87%
where the time goes in v5:
time: 863 us; the launch traced here: 856 us
  Pallas kernels  801 us (93%)
  local copies, waits for them, and re-layouts  21.6 us (3%)
  blocking collectives  14.9 us (2%)
  between operations  14.5 us (2%)
    pallas_call x1, Pallas kernels, tail_call(): pl.pallas_call(functools.partial(tail_kernel, seq, n_grp, rows, tuple(scr...  444 us
    pallas_call x1, Pallas kernels, attn_call(): pl.pallas_call(functools.partial(attn_kernel, own, seq, n_grp), grid_spec...  220 us
    pallas_call x2, Pallas kernels, dw_call(): pl.pallas_call(functools.partial(dw_kernel, len(bs), gathered is not None...  128 us
    unnamed x18, local copies, waits for them, and re-layouts  20.5 us
  transfers between devices with their start and end apart: 2, of which 0 were waited for; matrix products, arithmetic and copies ran while one was open for 1% of the time, Pallas kernels for 87%

profile of v5, /device:TPU:0, one launch (start us, length us, event | category | flops | bytes accessed | tf_op | source)
XLA Modules:
  0.0 855.8 jit_solution(5363067559053468371)
XLA Ops:
  7.2 0.0 all-gather.2.cloned.1.call-start
  7.2 0.6 maximum_bitcast_fusion.freq_ref
  7.8 9.4 %pre.1 = (f32[4,192,2048]{2,1,0:T(8,128)}, f32[8192,128]{1,0:T(8,128)}, f32[8192,128]{1,0:T(8,128)}) custom-call(s32[1]{0:T(128)} %bitcast.3.sel_ref, bf16[2048,1024]{1,0:T(8,128)(2,1)} %refs_0_.1, bf16[2048,512]{1,0:T(8,128)(2,1)} %refs_1_.1, bf16[2048,512]{1,0:T(8,128)(2,1)} %refs_2_.1, bf16[1024,2048]{1,0:T(8,128)(2,1)} %refs_3_.1, s32[32,256]{1,0:T(8,128)} %pos_ref.1, ...), custom_call_target="tpu_custom_call" | custom-call | flops 31457280 | bytes 17825792 | tf_op jit(solution)/shard_map/pre/pallas_call | solution.py:392
  17.3 0.0 all-reduce.3.cloned.1.call-start
  17.3 0.6 copy-done.2
  17.9 0.6 reshape.67
  18.5 0.5 bitcast_convert_fusion
  19.0 219.7 %attn_own.1 = (bf16[8192,2048]{1,0:T(8,128)(2,1)}, bf16[2,8192,1024]{2,1,0:T(8,128)(2,1)}, bf16[2,8192,1024]{2,1,0:T(8,128)(2,1)}, bf16[2,8192,512]{2,1,0:T(8,12...) custom-call(s32[1]{0:T(128)} %bitcast.sel_ref, bf16[8192,2048]{1,0:T(8,128)(2,1)} %bitcast.19, ...), custom_call_target="tpu_custom_call" | custom-call | flops 128849018880 | bytes 150994944 | tf_op jit(solution)/shard_map/attn_own/pallas_call | solution.py:322
  238.8 81.0 %shard_map.170 = (f32[2048,1024]{1,0:T(8,128)}, f32[2048,512]{1,0:T(8,128)}, f32[2048,512]{1,0:T(8,128)}) custom-call(s32[1]{0:T(128)} %bitcast.sel_ref, bf16[8192,2048]{1,0:T(8,128)(2,1)} %get-tuple-element.34.n_in.a_ref, bf16[2,8192,1024]{2,1,0:T(8,128)(2,1)} %get-tuple-element.41.refs_9_.refs_0_, ...), custom_call_target="tpu_custom_call" | custom-call | flops 68719476736 | bytes 83886080 | tf_op jit(solution)/shard_map/pallas_call | solution.py:469
  319.8 0.0 all-gather.2.cloned.1.call-done.refs_1_
  319.8 46.7 %shard_map.169 = (f32[1024,2048]{1,0:T(8,128)}, bf16[2048,1024]{1,0:T(8,128)(2,1)}, bf16[2048,512]{1,0:T(8,128)(2,1)}, bf16[2048,512]{1,0:T(8,128)(2,1)}, bf16[1024,2048]{1,0:T(8,128)(2,1)}) custom-call(s32[1]{0:T(128)} %bitcast.sel_ref, bf16[2,8192,1024]{2,1,0:T(8,128)(2,1)} %get-tuple-element.35.a_ref.refs_8_, bf16[8192,2048]{1,0:T(8,128)(2,1)} %bitcast.23, ...), custom_call_target="tpu_custom_call" | custom-call | flops 34359738368 | bytes 58720256 | tf_op jit(solution)/shard_map/pallas_call | solution.py:469
  366.6 443.8 %tail.1 = (bf16[8192,2048]{1,0:T(8,128)(2,1)}, bf16[8192,2048]{1,0:T(8,128)(2,1)}, f32[8,2048]{1,0:T(8,128)}, f32[8,128]{1,0:T(8,128)}, f32[8,128]{1,0:T(8,128)}) custom-call(s32[1]{0:T(128)} %bitcast.sel_ref, bf16[8192,2048]{1,0:T(8,128)(2,1)} %get-tuple-element.34.n_in.a_ref, bf16[8192,2048]{1,0:T(8,128)(2,1)} %bitcast.24, ...), custom_call_target="tpu_custom_call" | custom-call | flops 335007449088 | bytes 234881024 | tf_op jit(solution)/shard_map/tail/pallas_call | solution.py:891
  810.4 0.7 add.16
  811.1 0.7 add.17
  811.8 0.9 maximum_reduce_fusion
  812.7 14.9 %psum.39 = f32[2304]{0:T(1024)S(1)} all-reduce(f32[2304]{0:T(1024)S(1)} %maximum_reduce_fusion), channel_id=1, replica_groups=mesh['tp'=2,'dp'=4] {'dp'}, use_global_device_ids=true, to_apply=%region_5.0 | all-reduce | flops 2304 | bytes 18432 | tf_op jit(solution)/shard_map/psum | solution.py:934
  827.6 0.6 slice.14
  828.2 0.5 fusion
  828.7 8.6 %copy.23 = f32[2048,1024]{1,0:T(8,128)} copy(f32[2048,1024]{1,0:T(8,128)} %get-tuple-element.65) | data formatting | bytes 16777216
  837.3 2.1 copy.24
  839.4 1.6 copy-done
  841.0 2.1 copy.25
  843.1 2.1 slice-done.1
  845.2 3.4 copy.26
  (16 shorter events, 0.1 us)
Async XLA Ops:
  7.2 312.7 %all-gather.2.cloned.1.call-start = ((), (), s32[]{:S(2)}) async-start(), calls=%async_computation | async-start | bytes 56623104 | tf_op jit(solution)/shard_map/all_gather | solution.py:923
  17.2 0.7 copy-start.2
  17.2 1.3 copy-start.3
  17.2 1.3 copy-start.4
  17.3 811.4 %all-reduce.3.cloned.1.call-start = ((), (), s32[]{:S(2)}) async-start(), calls=%async_computation.1 | async-start | bytes 50331648 | tf_op jit(solution)/shard_map/psum | solution.py:931
  828.7 8.6 %copy-start.1 = (f32[2048,512]{1,0:T(8,128)S(1)}, f32[2048,512]{1,0:T(8,128)}, u32[]{:S(2)}) copy-start(f32[2048,512]{1,0:T(8,128)} %get-tuple-element.66) | copy-start | bytes 12582916
  837.3 3.7 copy-start
  837.3 5.8 slice-start
  841.0 4.2 slice-start.1
Sparse Core Ops, SparseCore 0:
  17.4 229.2 all-gather.1
  366.7 421.8 all-reduce.2

commit v6 on v5

--- a/solution.py
+++ b/solution.py
@@ -260,9 +260,12 @@
 
     @pl.when(step == 0)
     def _():
-        for c in range(0, wo_ref.shape[0], 256):
+        @pl.loop(0, wo_ref.shape[0] // 256)
+        def _(j):
+            c = pl.ds(pl.multiple_of(j * 256, 256), 256)
             for d in range(0, wo_ref.shape[1], 256):
-                wot_ref[d:d + 256, c:c + 256] = wo_ref[c:c + 256, d:d + 256].T
+                wot_ref[d:d + 256, c] = wo_ref[c, d:d + 256].T
+
         if own:
             weave(norm_rows(x0_ref, n_ref))
 
@@ -425,7 +428,9 @@
     @pl.when(step == 0)
     def _():
         for acc in accs:
-            acc[...] = jnp.zeros_like(acc)
+            @pl.loop(0, M // 64)
+            def _(j):
+                acc[pl.ds(pl.multiple_of(j * 64, 64), 64), :] = jnp.zeros((64, acc.shape[1]), F32)
 
     def part(acc, b, c):
         def run():
@@ -691,19 +696,15 @@
     return SimpleNamespace(norm=norm_rows, proj=proj, rope=rope, scores=scores, soft=soft, grads=grads, back=back)
 
 
-def attn_tick(st, g, n_grp, extra=()):
-    vec = st.soft((g - 3) % n_grp) + st.rope((g - 1) % n_grp)
-    more = [e for e in extra]
-    if more:
-        vec = vec + more[0]
-    vec = vec + st.back(g)
+def attn_tick(st, g, n_grp):
+    vec = st.soft((g - 3) % n_grp) + st.rope((g - 1) % n_grp) + st.back(g)
     gr = st.grads(g)
     for _, f in gr[:2]:
         f()
-    weave(vec, st.scores((g - 2) % n_grp) + gr[2:] + st.proj(g), *more[1:])
-
-
-def attn_scratch(seq, n_grp, nq, nk):
+    weave(vec, st.scores((g - 2) % n_grp) + gr[2:] + st.proj(g))
+
+
+def attn_scratch(seq, n_grp):
     return dict(
         qnew=pltpu.VMEM((2, 2, seq, HD), BF16),
         knew=pltpu.VMEM((n_grp, seq, HD), BF16),
@@ -722,10 +723,6 @@
         st=pltpu.VMEM((3, 2 * seq, HD), F32),
         sb=pltpu.VMEM((3, seq, HD), F32),
         tab=pltpu.VMEM((4, seq, HD), F32),
-        o=pltpu.VMEM((seq, nq), BF16),
-        dq=pltpu.VMEM((seq, nq), BF16),
-        dk=pltpu.VMEM((seq, nk), BF16),
-        dv=pltpu.VMEM((seq, nk), BF16),
     )
 
 
@@ -741,25 +738,29 @@
     r.wk = lambda c: r.wk_all[oth, :, c]
     r.wv = lambda c: r.wv_all[oth, :, c]
     r.do_dot = lambda c: dot(dy_in[...], r.wo_all[oth, c, :], NT)
+    r.o, r.dq, r.dk, r.dv = r.oc.at[oth], r.dqc.at[oth], r.dkc.at[oth], r.dvc.at[oth]
     st = attn_stages(seq, n_grp, r)
 
     def fetch(row):
-        return [pltpu.make_async_copy(src.at[me, pl.ds(row * seq, seq), :], dst, r.sem.at[8 + k])
-                for k, (src, dst) in enumerate(zip(own_a, (r.o_own, r.dq_own, r.dk_own, r.dv_own)))]
+        return [pltpu.make_async_copy(src.at[me, pl.ds(row * seq, seq), :], dst.at[me], r.sem.at[8 + k])
+                for k, (src, dst) in enumerate(zip(own_a, (r.oc, r.dqc, r.dkc, r.dvc)))]
+
+    weights = (r.wq_all, r.wk_all, r.wv_all, r.wo_all)
+    theirs = [pltpu.make_async_copy(oth_w[k], dst.at[oth], r.sem.at[4 + k]) for k, dst in enumerate(weights)]
+    mine = [pltpu.make_async_copy(own_w[k], dst.at[me], r.sem.at[k]) for k, dst in enumerate(weights)]
 
     @pl.when(step == 0)
     def _():
-        copies = []
-        for k, dst in enumerate((r.wq_all, r.wk_all, r.wv_all, r.wo_all)):
-            copies.append(pltpu.make_async_copy(oth_w[k], dst.at[oth], r.sem.at[4 + k]))
-            copies.append(pltpu.make_async_copy(own_w[k], dst.at[me], r.sem.at[k]))
-        for c in copies:
-            c.start()
-        for c in copies:
-            c.wait()
-        for c in fetch(0):
+        for c in theirs + mine:
             c.start()
         r.dg[...] = jnp.zeros_like(r.dg)
+        for c in theirs:
+            c.wait()
+
+    @pl.when(step > 0)
+    def _():
+        for c in fetch(step - 1):
+            c.start()
 
     CR, NC = 32, 256
     nn = D // NC
@@ -822,52 +823,36 @@
 
         return (1, run)
 
-    dn = [dn_dot(n) for n in range(nn)]
-    yd = [y_dot(n) for n in range(nn)]
-    f = [[first(n, c) for c in lines] for n in range(nn)]
-    sec = [second(n, c) for n in range(nn) for c in lines]
-    out_mat = [dn[:3], dn[3:6], dn[6:], []]
-    out_vec = [[stat(c) for c in lines], f[0] + f[1] + f[2], f[3] + f[4] + f[5], f[6] + f[7] + [mean(c) for c in lines]]
-
-    def body(attn, out):
-        if attn:
-            r.tab[2:4] = r.tab[0:2]
-            r.tab[0] = cos_in[...]
-            r.tab[1] = sin_in[...]
-        for g in range(n_grp):
-            if attn:
-                attn_tick(st, g, n_grp, ([], out_mat[g], out_vec[g]) if out else ())
-            else:
-                weave(out_mat[g], out_vec[g])
-        if out:
-            weave(yd, sec)
-        if attn:
-            row = jnp.clip(step - 1, 0, rows - 1)
-            for c in fetch(row):
-                c.wait()
-            for dst, theirs, mine in ((r.oc, r.o, r.o_own), (r.dqc, r.dq, r.dq_own), (r.dkc, r.dk, r.dk_own), (r.dvc, r.dv, r.dv_own)):
-                dst[oth] = theirs[...]
-                dst[me] = mine[...]
-
-            for acc in (r.dgq, r.dgk):
-                acc[...] = jnp.where(step > 0, acc[...], 0.0)
-
-            @pl.when(step < rows)
-            def _():
-                for c in fetch(step):
-                    c.start()
-
-    @pl.when(step < 2)
+    r.tab[2:4] = r.tab[0:2]
+    r.tab[0] = cos_in[...]
+    r.tab[1] = sin_in[...]
+    for g in range(n_grp):
+        attn_tick(st, g, n_grp)
+    for acc in (r.dgq, r.dgk):
+        acc[...] = jnp.where(step > 0, acc[...], 0.0)
+
+    @pl.when(step == 0)
     def _():
-        body(True, False)
-
-    @pl.when((step >= 2) & (step <= rows))
+        for c in mine:
+            c.wait()
+
+    @pl.when(step > 0)
     def _():
-        body(True, True)
-
-    @pl.when(step > rows)
+        for c in fetch(step - 1):
+            c.wait()
+        dn = [dn_dot(n) for n in range(nn)]
+        yd = [y_dot(n) for n in range(nn)]
+        for _, f in dn[:1]:
+            f()
+        weave([stat(c) for c in lines], dn[1:2])
+        for n in range(2, nn):
+            weave([first(n - 2, c) for c in lines], dn[n:n + 1])
+        weave([first(nn - 2, c) for c in lines], yd[:1])
+        weave([first(nn - 1, c) for c in lines] + [mean(c) for c in lines], yd[1:2])
+        weave([second(n, c) for n in range(nn) for c in lines], yd[2:])
+
+    @pl.when(step == rows)
     def _():
-        body(False, True)
         dg_out[...] = r.dg[...]
         dgq_out[...] = r.dgq[...]
         dgk_out[...] = r.dgk[...]
@@ -881,20 +866,19 @@
     lag = lambda k, c: pl.BlockSpec((seq, c), lambda i, s: (jnp.clip(i - k, 0, rows - 1), 0))
     const = lambda *b: pl.BlockSpec(b, lambda i, s: (0,) * len(b), pipeline_mode=pl.Buffered(1))
     hbm = pl.BlockSpec(memory_space=pl.ANY)
-    scratch = attn_scratch(seq, n_grp, nq, nk)
+    scratch = attn_scratch(seq, n_grp)
     scratch.update(
         wq_all=pltpu.VMEM((2, D, nq), BF16), wk_all=pltpu.VMEM((2, D, nk), BF16), wv_all=pltpu.VMEM((2, D, nk), BF16), wo_all=pltpu.VMEM((2, nq, D), BF16),
         dn=pltpu.VMEM((seq, D), F32), oc=pltpu.VMEM((2, seq, nq), BF16), dqc=pltpu.VMEM((2, seq, nq), BF16), dkc=pltpu.VMEM((2, seq, nk), BF16), dvc=pltpu.VMEM((2, seq, nk), BF16),
-        o_own=pltpu.VMEM((seq, nq), BF16), dq_own=pltpu.VMEM((seq, nq), BF16), dk_own=pltpu.VMEM((seq, nk), BF16), dv_own=pltpu.VMEM((seq, nk), BF16),
         xs=pltpu.VMEM((3, seq, HD), F32), dg=pltpu.VMEM((8, D), F32), dgq=pltpu.VMEM((8, HD), F32), dgk=pltpu.VMEM((8, HD), F32), sem=pltpu.SemaphoreType.DMA((12,)))
     flops = 2 * T * D * (nq + 2 * nk + nq) * 3 + 12 * T * nq * seq
     return pl.pallas_call(
         functools.partial(tail_kernel, seq, n_grp, rows, tuple(scratch)),
         grid_spec=pltpu.PrefetchScalarGridSpec(
             num_scalar_prefetch=1,
-            grid=(rows + 2,),
-            in_specs=[lag(0, D), lag(0, D), lag(0, HD), lag(0, HD), lag(2, D), lag(2, D), const(1, D), const(1, HD), const(1, HD)] + [hbm] * 12,
-            out_specs=[lag(2, D), lag(2, D), pl.BlockSpec((8, D), lambda i, s: (0, 0))] + [pl.BlockSpec((8, HD), lambda i, s: (0, 0))] * 2,
+            grid=(rows + 1,),
+            in_specs=[lag(0, D), lag(0, D), lag(0, HD), lag(0, HD), lag(1, D), lag(1, D), const(1, D), const(1, HD), const(1, HD)] + [hbm] * 12,
+            out_specs=[lag(1, D), lag(1, D), pl.BlockSpec((8, D), lambda i, s: (0, 0))] + [pl.BlockSpec((8, HD), lambda i, s: (0, 0))] * 2,
             scratch_shapes=list(scratch.values()),
         ),
         out_shape=[jax.ShapeDtypeStruct((T, D), BF16)] * 2 + [jax.ShapeDtypeStruct((8, c), F32) for c in (D, HD, HD)],

time: 863 us -> 861 us (level)
  no operation moved by 1% of the time
where the time goes in v6:
time: 861 us; the launch traced here: 860 us
  Pallas kernels  804 us (93%)
  local copies, waits for them, and re-layouts  21.6 us (3%)
  blocking collectives  15.9 us (2%)
  between operations  14.1 us (2%)
    pallas_call x1, Pallas kernels, tail_call(): pl.pallas_call(functools.partial(tail_kernel, seq, n_grp, rows, tuple(scr...  446 us
    pallas_call x1, Pallas kernels, attn_call(): pl.pallas_call(functools.partial(attn_kernel, own, seq, n_grp), grid_spec...  220 us
    pallas_call x2, Pallas kernels, dw_call(): pl.pallas_call(functools.partial(dw_kernel, len(bs), gathered is not None...  130 us
    unnamed x18, local copies, waits for them, and re-layouts  20.5 us
  transfers between devices with their start and end apart: 2, of which 0 were waited for; matrix products, arithmetic and copies ran while one was open for 1% of the time, Pallas kernels for 87%

profile of v6, /device:TPU:0, one launch (start us, length us, event | category | flops | bytes accessed | tf_op | source)
XLA Modules:
  0.0 860.2 jit_solution(3593919173184125336)
XLA Ops:
  7.2 0.0 all-gather.2.cloned.1.call-start
  7.2 0.6 maximum_bitcast_fusion.freq_ref
  7.8 9.4 %pre.1 = (f32[4,192,2048]{2,1,0:T(8,128)}, f32[8192,128]{1,0:T(8,128)}, f32[8192,128]{1,0:T(8,128)}) custom-call(s32[1]{0:T(128)} %bitcast.3.sel_ref, bf16[2048,1024]{1,0:T(8,128)(2,1)} %refs_0_.1, bf16[2048,512]{1,0:T(8,128)(2,1)} %refs_1_.1, bf16[2048,512]{1,0:T(8,128)(2,1)} %refs_2_.1, bf16[1024,2048]{1,0:T(8,128)(2,1)} %refs_3_.1, s32[32,256]{1,0:T(8,128)} %pos_ref.1, ...), custom_call_target="tpu_custom_call" | custom-call | flops 31457280 | bytes 17825792 | tf_op jit(solution)/shard_map/pre/pallas_call | solution.py:395
  17.3 0.0 all-reduce.3.cloned.1.call-start
  17.3 0.6 copy-done.2
  17.9 0.6 reshape.67
  18.5 0.5 bitcast_convert_fusion
  19.0 220.1 %attn_own.1 = (bf16[8192,2048]{1,0:T(8,128)(2,1)}, bf16[2,8192,1024]{2,1,0:T(8,128)(2,1)}, bf16[2,8192,1024]{2,1,0:T(8,128)(2,1)}, bf16[2,8192,512]{2,1,0:T(8,12...) custom-call(s32[1]{0:T(128)} %bitcast.sel_ref, bf16[8192,2048]{1,0:T(8,128)(2,1)} %bitcast.19, ...), custom_call_target="tpu_custom_call" | custom-call | flops 128849018880 | bytes 150994944 | tf_op jit(solution)/shard_map/attn_own/pallas_call | solution.py:325
  239.1 82.5 %shard_map.170 = (f32[2048,1024]{1,0:T(8,128)}, f32[2048,512]{1,0:T(8,128)}, f32[2048,512]{1,0:T(8,128)}) custom-call(s32[1]{0:T(128)} %bitcast.sel_ref, bf16[8192,2048]{1,0:T(8,128)(2,1)} %get-tuple-element.34.n_in.a_ref, bf16[2,8192,1024]{2,1,0:T(8,128)(2,1)} %get-tuple-element.41.refs_9_.refs_0_, ...), custom_call_target="tpu_custom_call" | custom-call | flops 68719476736 | bytes 83886080 | tf_op jit(solution)/shard_map/pallas_call | solution.py:474
  321.7 0.0 all-gather.2.cloned.1.call-done.refs_1_
  321.7 47.0 %shard_map.169 = (f32[1024,2048]{1,0:T(8,128)}, bf16[2048,1024]{1,0:T(8,128)(2,1)}, bf16[2048,512]{1,0:T(8,128)(2,1)}, bf16[2048,512]{1,0:T(8,128)(2,1)}, bf16[1024,2048]{1,0:T(8,128)(2,1)}) custom-call(s32[1]{0:T(128)} %bitcast.sel_ref, bf16[2,8192,1024]{2,1,0:T(8,128)(2,1)} %get-tuple-element.35.a_ref.refs_8_, bf16[8192,2048]{1,0:T(8,128)(2,1)} %bitcast.23, ...), custom_call_target="tpu_custom_call" | custom-call | flops 34359738368 | bytes 58720256 | tf_op jit(solution)/shard_map/pallas_call | solution.py:474
  368.7 445.5 %tail.1 = (bf16[8192,2048]{1,0:T(8,128)(2,1)}, bf16[8192,2048]{1,0:T(8,128)(2,1)}, f32[8,2048]{1,0:T(8,128)}, f32[8,128]{1,0:T(8,128)}, f32[8,128]{1,0:T(8,128)}) custom-call(s32[1]{0:T(128)} %bitcast.sel_ref, bf16[8192,2048]{1,0:T(8,128)(2,1)} %get-tuple-element.34.n_in.a_ref, bf16[8192,2048]{1,0:T(8,128)(2,1)} %bitcast.24, ...), custom_call_target="tpu_custom_call" | custom-call | flops 335007449088 | bytes 234881024 | tf_op jit(solution)/shard_map/tail/pallas_call | solution.py:875
  814.2 0.7 add.16
  814.9 0.7 add.17
  815.6 0.9 maximum_reduce_fusion
  816.5 15.9 %psum.39 = f32[2304]{0:T(1024)S(1)} all-reduce(f32[2304]{0:T(1024)S(1)} %maximum_reduce_fusion), channel_id=1, replica_groups=mesh['tp'=2,'dp'=4] {'dp'}, use_global_device_ids=true, to_apply=%region_5.0 | all-reduce | flops 2304 | bytes 18432 | tf_op jit(solution)/shard_map/psum | solution.py:918
  832.3 0.6 slice.14
  832.9 0.5 fusion
  833.5 8.6 copy.23
  842.1 2.1 copy.24
  844.2 1.6 copy-done
  845.8 2.1 copy.25
  847.9 2.1 slice-done.1
  850.0 3.4 copy.26
  (16 shorter events, 0.1 us)
Async XLA Ops:
  7.2 314.5 %all-gather.2.cloned.1.call-start = ((), (), s32[]{:S(2)}) async-start(), calls=%async_computation | async-start | bytes 56623104 | tf_op jit(solution)/shard_map/all_gather | solution.py:907
  17.2 0.7 copy-start.2
  17.2 1.3 copy-start.3
  17.2 1.3 copy-start.4
  17.3 816.2 %all-reduce.3.cloned.1.call-start = ((), (), s32[]{:S(2)}) async-start(), calls=%async_computation.1 | async-start | bytes 50331648 | tf_op jit(solution)/shard_map/psum | solution.py:915
  833.5 8.6 copy-start.1
  842.1 3.7 copy-start
  842.1 5.8 slice-start
  845.8 4.2 slice-start.1
Sparse Core Ops, SparseCore 0:
  17.4 229.3 all-gather.1
  368.8 421.8 all-reduce.2

commit v7 on v6

--- a/solution.py
+++ b/solution.py
@@ -486,6 +486,67 @@
     )(sel, a, *bs, *more)
 
 
+def sum_kernel(n, widths, part_ref, *refs):
+    outs, (slots, local_sem, send_sem, recv_sem) = refs[:-4], refs[-4:]
+    me = lax.axis_index("dp")
+    barrier = pltpu.get_barrier_semaphore()
+    for k in range(1, n):
+        pl.semaphore_signal(barrier, inc=1, device_id={"dp": lax.rem(me + k, n)}, device_id_type=pl.DeviceIdType.MESH)
+    mine = pltpu.make_async_copy(part_ref, slots.at[0], local_sem)
+    mine.start()
+    pl.semaphore_wait(barrier, n - 1)
+    copies = []
+    for k in range(1, n):
+        copies.append(pltpu.make_async_remote_copy(
+            src_ref=part_ref, dst_ref=slots.at[k], send_sem=send_sem.at[k - 1], recv_sem=recv_sem.at[k - 1],
+            device_id={"dp": lax.rem(me + k, n)}, device_id_type=pl.DeviceIdType.MESH))
+    for c in copies:
+        c.start()
+    mine.wait()
+    for c in copies:
+        c.wait()
+    total = slots[lax.rem(me + n, n)]
+    for a in range(1, n):
+        total = total + slots[lax.rem(me + n - a, n)]
+    total = jnp.sum(total, axis=0, keepdims=True)
+    at = 0
+    for out, w in zip(outs, widths):
+        out[...] = total[:, at:at + w]
+        at += w
+
+
+def sum_call(part, widths, n):
+    return pl.pallas_call(
+        functools.partial(sum_kernel, n, widths),
+        in_specs=[pl.BlockSpec(memory_space=pl.ANY)],
+        out_specs=[pl.BlockSpec(memory_space=pltpu.VMEM)] * len(widths),
+        out_shape=[jax.ShapeDtypeStruct((1, w), F32) for w in widths],
+        scratch_shapes=[pltpu.VMEM((n, *part.shape), F32), pltpu.SemaphoreType.DMA, pltpu.SemaphoreType.DMA((n - 1,)), pltpu.SemaphoreType.DMA((n - 1,))],
+        compiler_params=pltpu.CompilerParams(collective_id=0, has_side_effects=True),
+        cost_estimate=pl.CostEstimate(flops=n * part.size, bytes_accessed=8 * n * part.size, transcendentals=0),
+        name="small_sum",
+    )(part)
+
+
+def copy_kernel(n, *refs):
+    for src, dst in zip(refs[:n], refs[n:]):
+        dst[...] = src[...]
+
+
+def copy_call(arrays, steps=8):
+    specs = [pl.BlockSpec((a.shape[0] // steps, a.shape[1]), lambda i: (i, 0)) for a in arrays]
+    return pl.pallas_call(
+        functools.partial(copy_kernel, len(arrays)),
+        grid=(steps,),
+        in_specs=specs,
+        out_specs=specs,
+        out_shape=[jax.ShapeDtypeStruct(a.shape, a.dtype) for a in arrays],
+        compiler_params=pltpu.CompilerParams(dimension_semantics=("arbitrary",), vmem_limit_bytes=60 << 20),
+        cost_estimate=pl.CostEstimate(flops=0, bytes_accessed=8 * sum(a.size for a in arrays), transcendentals=0),
+        name="results",
+    )(*arrays)
+
+
 def attn_stages(seq, n_grp, r):
     half = seq // 2
     scale = HD ** -0.5
@@ -726,10 +787,10 @@
     )
 
 
-def tail_kernel(seq, n_grp, rows, keys, sel_ref, n_in, dy_in, cos_in, sin_in, x_in, dyx_in, gain_ref, qg_ref, kg_ref, *refs):
+def tail_kernel(seq, n_grp, rows, keys, sel_ref, n_in, dy_in, cos_in, sin_in, x_in, dyx_in, gain_ref, qg_ref, kg_ref, dgq_own, dgk_own, *refs):
     own_w, oth_w, own_a = refs[:4], refs[4:8], refs[8:12]
-    y_out, dx_out, dg_out, dgq_out, dgk_out = refs[12:17]
-    r = SimpleNamespace(n=n_in, dy=dy_in, qg=qg_ref, kg=kg_ref, gain=gain_ref, **dict(zip(keys, refs[17:])))
+    y_out, dx_out, sums_out = refs[12:15]
+    r = SimpleNamespace(n=n_in, dy=dy_in, qg=qg_ref, kg=kg_ref, gain=gain_ref, **dict(zip(keys, refs[15:])))
     step = pl.program_id(0)
     me = sel_ref[0]
     oth = 1 - me
@@ -853,12 +914,12 @@
 
     @pl.when(step == rows)
     def _():
-        dg_out[...] = r.dg[...]
-        dgq_out[...] = r.dgq[...]
-        dgk_out[...] = r.dgk[...]
-
-
-def tail_call(sel, n, x, dy, cosd, sind, o, dq, dk, dv, gain, qg, kg, own, oth, seq=256):
+        sums_out[:, 0:D] = r.dg[...]
+        sums_out[:, D:D + HD] = r.dgq[...] + dgq_own[...]
+        sums_out[:, D + HD:] = r.dgk[...] + dgk_own[...]
+
+
+def tail_call(sel, n, x, dy, cosd, sind, o, dq, dk, dv, gain, qg, kg, dgq, dgk, own, oth, seq=256):
     T, D = x.shape
     nq, nk = dq.shape[2], dk.shape[2]
     n_grp = nk // HD
@@ -877,15 +938,15 @@
         grid_spec=pltpu.PrefetchScalarGridSpec(
             num_scalar_prefetch=1,
             grid=(rows + 1,),
-            in_specs=[lag(0, D), lag(0, D), lag(0, HD), lag(0, HD), lag(1, D), lag(1, D), const(1, D), const(1, HD), const(1, HD)] + [hbm] * 12,
-            out_specs=[lag(1, D), lag(1, D), pl.BlockSpec((8, D), lambda i, s: (0, 0))] + [pl.BlockSpec((8, HD), lambda i, s: (0, 0))] * 2,
+            in_specs=[lag(0, D), lag(0, D), lag(0, HD), lag(0, HD), lag(1, D), lag(1, D), const(1, D), const(1, HD), const(1, HD), const(8, HD), const(8, HD)] + [hbm] * 12,
+            out_specs=[lag(1, D), lag(1, D), pl.BlockSpec((8, D + 2 * HD), lambda i, s: (0, 0))],
             scratch_shapes=list(scratch.values()),
         ),
-        out_shape=[jax.ShapeDtypeStruct((T, D), BF16)] * 2 + [jax.ShapeDtypeStruct((8, c), F32) for c in (D, HD, HD)],
+        out_shape=[jax.ShapeDtypeStruct((T, D), BF16)] * 2 + [jax.ShapeDtypeStruct((8, D + 2 * HD), F32)],
         compiler_params=pltpu.CompilerParams(dimension_semantics=("arbitrary",), vmem_limit_bytes=67043328),
         cost_estimate=pl.CostEstimate(flops=flops, bytes_accessed=T * D * 14, transcendentals=T * nq * 2),
         name="tail",
-    )(sel, n, dy, cosd, sind, x, dy, gain, qg, kg, *own, *oth, o, dq, dk, dv)
+    )(sel, n, dy, cosd, sind, x, dy, gain, qg, kg, dgq, dgk, *own, *oth, o, dq, dk, dv)
 
 
 def solution(mesh):
@@ -914,9 +975,9 @@
         dw_o, *theirs = dw_call(own, o, [dy], 1024, gathered=gathered, nk=nk)
         dw_o, dw_q, dw_k, dw_v = lax.psum((dw_o, dw_q, dw_k, dw_v), "dp")
 
-        y, dx, dg, dgq2, dgk2 = tail_call(own, n, x, dy, cosd, sind, o, dq, dk, dv, gain, qg, kg, (w_q, w_k, w_v, w_o), theirs, seq=n_seq)
-        small = lax.psum(jnp.sum(jnp.concatenate([dg, dgq + dgq2, dgk + dgk2], axis=1), axis=0), "dp")
-        g_sum, q_sum, k_sum = small[:D], small[D:D + HD], small[D + HD:]
+        y, dx, sums = tail_call(own, n, x, dy, cosd, sind, o, dq, dk, dv, gain, qg, kg, dgq, dgk, (w_q, w_k, w_v, w_o), theirs, seq=n_seq)
+        g_sum, q_sum, k_sum = (t.reshape(-1) for t in sum_call(sums, (D, HD, HD), n_dp))
+        dw_o, dw_q, dw_k, dw_v = copy_call((dw_o, dw_q, dw_k, dw_v))
         return y.reshape(x_in.shape), dx.reshape(x_in.shape), dw_q, dw_k, dw_v, dw_o, q_sum, k_sum, g_sum
 
     return jax.shard_map(per_device, mesh=mesh, in_specs=(tok_spec, tok_spec, P("dp", None), P(), P(), P(), col_spec, col_spec, col_spec, row_spec), out_specs=(tok_spec, tok_spec, col_spec, col_spec, col_spec, row_spec, P(), P(), P()), check_vma=False)

time: 861 us -> 851 us (0.988)
  Pallas kernels: 804 us -> 833 us
  local copies, waits for them, and re-layouts: 21.6 us -> 2.23 us
  blocking collectives: 15.9 us -> 0 us
    pallas_call x0 -> x2, Pallas kernels: none -> 28.8 us  [the longest x1 18 us: copy_call(): pl.pallas_call(functools.partial(copy_kernel, len(arrays)), grid=(steps,)...]
    unnamed x18 -> x15, local copies, waits for them, and re-layouts: 20.5 us -> 2.23 us
    psum x1 -> x0, blocking collectives: 15.9 us -> none  [per_device(): lax.psum(jnp.sum(jnp.concatenate([dg, dgq + dgq2, dgk + dgk2], axis=1), a...]
  transfers between devices with their start and end apart: 2 -> 2, of which waited for: 0 -> 0; matrix products, arithmetic and copies ran while one was open for 1% -> 0% of each run, Pallas kernels for 87% -> 89%
where the time goes in v7:
time: 851 us
  Pallas kernels  833 us (98%)
  between operations  14.2 us (2%)
    pallas_call x1, Pallas kernels, tail_call(): pl.pallas_call(functools.partial(tail_kernel, seq, n_grp, rows, tuple(scr...  445 us
    pallas_call x1, Pallas kernels, attn_call(): pl.pallas_call(functools.partial(attn_kernel, own, seq, n_grp), grid_spec...  220 us
    pallas_call x2, Pallas kernels, dw_call(): pl.pallas_call(functools.partial(dw_kernel, len(bs), gathered is not None...  130 us
    pallas_call x1, Pallas kernels, copy_call(): pl.pallas_call(functools.partial(copy_kernel, len(arrays)), grid=(steps,)...  18 us
  transfers between devices with their start and end apart: 2, of which 0 were waited for; matrix products, arithmetic and copies ran while one was open for 0% of the time, Pallas kernels for 89%

profile of v7, /device:TPU:0, one launch (start us, length us, event | category | flops | bytes accessed | tf_op | source)
XLA Modules:
  0.0 851.2 jit_solution(16446258702633342300)
XLA Ops:
  7.2 0.0 all-gather.2.cloned.1.call-start
  7.2 0.6 maximum_bitcast_fusion.freq_ref
  7.8 9.4 %pre.1 = (f32[4,192,2048]{2,1,0:T(8,128)}, f32[8192,128]{1,0:T(8,128)}, f32[8192,128]{1,0:T(8,128)}) custom-call(s32[1]{0:T(128)} %bitcast.3.sel_ref, bf16[2048,1024]{1,0:T(8,128)(2,1)} %refs_0_.1, bf16[2048,512]{1,0:T(8,128)(2,1)} %refs_1_.1, bf16[2048,512]{1,0:T(8,128)(2,1)} %refs_2_.1, bf16[1024,2048]{1,0:T(8,128)(2,1)} %refs_3_.1, s32[32,256]{1,0:T(8,128)} %pos_ref.1, ...), custom_call_target="tpu_custom_call" | custom-call | flops 31457280 | bytes 17825792 | tf_op jit(solution)/shard_map/pre/pallas_call | solution.py:395
  17.2 0.0 copy-start.2
  17.2 0.0 copy-start.3
  17.2 0.0 all-gather.2.cloned.1.call-update
  17.3 0.0 all-reduce.3.cloned.1.call-start
  17.3 0.6 copy-done.1
  17.9 0.6 reshape.79
  18.5 0.0 copy-done.2
  18.5 0.0 copy-done.3
  18.5 0.5 bitcast_convert_fusion
  19.0 220.1 %attn_own.1 = (bf16[8192,2048]{1,0:T(8,128)(2,1)}, bf16[2,8192,1024]{2,1,0:T(8,128)(2,1)}, bf16[2,8192,1024]{2,1,0:T(8,128)(2,1)}, bf16[2,8192,512]{2,1,0:T(8,12...) custom-call(s32[1]{0:T(128)} %bitcast.sel_ref, bf16[8192,2048]{1,0:T(8,128)(2,1)} %bitcast.21, ...), custom_call_target="tpu_custom_call" | custom-call | flops 128849018880 | bytes 150994944 | tf_op jit(solution)/shard_map/attn_own/pallas_call | solution.py:325
  239.1 82.6 %shard_map.170 = (f32[2048,1024]{1,0:T(8,128)}, f32[2048,512]{1,0:T(8,128)}, f32[2048,512]{1,0:T(8,128)}) custom-call(s32[1]{0:T(128)} %bitcast.sel_ref, bf16[8192,2048]{1,0:T(8,128)(2,1)} %get-tuple-element.39.n_in.a_ref, bf16[2,8192,1024]{2,1,0:T(8,128)(2,1)} %get-tuple-element.48.refs_9_.refs_0_, ...), custom_call_target="tpu_custom_call" | custom-call | flops 68719476736 | bytes 83886080 | tf_op jit(solution)/shard_map/pallas_call | solution.py:474
  321.7 0.0 all-gather.2.cloned.1.call-done.refs_1_
  321.7 47.0 %shard_map.169 = (f32[1024,2048]{1,0:T(8,128)}, bf16[2048,1024]{1,0:T(8,128)(2,1)}, bf16[2048,512]{1,0:T(8,128)(2,1)}, bf16[2048,512]{1,0:T(8,128)(2,1)}, bf16[1024,2048]{1,0:T(8,128)(2,1)}) custom-call(s32[1]{0:T(128)} %bitcast.sel_ref, bf16[2,8192,1024]{2,1,0:T(8,128)(2,1)} %get-tuple-element.42.a_ref.refs_8_, bf16[8192,2048]{1,0:T(8,128)(2,1)} %bitcast.25, ...), custom_call_target="tpu_custom_call" | custom-call | flops 34359738368 | bytes 58720256 | tf_op jit(solution)/shard_map/pallas_call | solution.py:474
  368.7 0.0 all-reduce.3.cloned.1.call-update
  368.7 445.1 %tail.1 = (bf16[8192,2048]{1,0:T(8,128)(2,1)}, bf16[8192,2048]{1,0:T(8,128)(2,1)}, f32[8,2304]{1,0:T(8,128)}) custom-call(s32[1]{0:T(128)} %bitcast.sel_ref, bf16[8192,2048]{1,0:T(8,128)(2,1)} %get-tuple-element.39.n_in.a_ref, bf16[8192,2048]{1,0:T(8,128)(2,1)} %bitcast.26, f32[8192,128]{1,0:T(8,128)} %get-tuple-element.37.refs_3_.cos_in, ...), custom_call_target="tpu_custom_call" | custom-call | flops 335007449088 | bytes 234881024 | tf_op jit(solution)/shard_map/tail/pallas_call | solution.py:936
  813.8 10.9 %small_sum.1 = (f32[1,2048]{1,0:T(1,128)}, f32[1,128]{1,0:T(1,128)}, f32[1,128]{1,0:T(1,128)}) custom-call(f32[8,2304]{1,0:T(8,128)} %get-tuple-element.61.part_ref), custom_call_target="tpu_custom_call" | custom-call | flops 73728 | bytes 589824 | tf_op jit(solution)/shard_map/small_sum/pallas_call | solution.py:519
  824.7 0.0 all-reduce.3.cloned.1.call-done
  824.7 18.0 %results.1 = (f32[1024,2048]{1,0:T(8,128)}, f32[2048,1024]{1,0:T(8,128)}, f32[2048,512]{1,0:T(8,128)}, f32[2048,512]{1,0:T(8,128)}) custom-call(f32[1024,2048]{1,0:T(8,128)} %get-tuple-element.65.refs_0_, f32[2048,1024]{1,0:T(8,128)} %get-tuple-element.66.refs_1_, f32[2048,512]{1,0:T(8,128)} %get-tuple-element.67.refs_2_, f32[2048,512]{1,0:T(8,128)} %get-tuple-element.68.refs_3_), custom_call_target="tpu_custom_call" | custom-call | bytes 50331648 | tf_op jit(solution)/shard_map/results/pallas_call | solution.py:538
  842.7 0.5 copy.26
  843.2 0.5 copy.27
  843.8 0.6 copy.28
  (8 shorter events, 0.0 us)
Async XLA Ops:
  7.2 314.5 %all-gather.2.cloned.1.call-start = ((), (), s32[]{:S(2)}) async-start(), calls=%async_computation | async-start | bytes 56623104 | tf_op jit(solution)/shard_map/all_gather | solution.py:968
  17.2 0.7 copy-start.1
  17.2 1.3 copy-start.2
  17.2 1.3 copy-start.3
  17.3 807.5 %all-reduce.3.cloned.1.call-start = ((), (), s32[]{:S(2)}) async-start(), calls=%async_computation.1 | async-start | bytes 50331648 | tf_op jit(solution)/shard_map/psum | solution.py:976
  824.7 18.0 %copy-start.5 = (f32[1,128]{1,0:T(1,128)S(1)}, f32[1,128]{1,0:T(1,128)}, u32[]{:S(2)}) copy-start(f32[1,128]{1,0:T(1,128)} %get-tuple-element.62) | copy-start | bytes 1540
  824.7 18.5 %copy-start.4 = (f32[1,128]{1,0:T(1,128)S(1)}, f32[1,128]{1,0:T(1,128)}, u32[]{:S(2)}) copy-start(f32[1,128]{1,0:T(1,128)} %get-tuple-element.63) | copy-start | bytes 1540
  824.7 19.0 %copy-start = (f32[1,2048]{1,0:T(1,128)S(1)}, f32[1,2048]{1,0:T(1,128)}, u32[]{:S(2)}) copy-start(f32[1,2048]{1,0:T(1,128)} %get-tuple-element.64) | copy-start | bytes 24580
Sparse Core Ops, SparseCore 0:
  17.4 229.2 all-gather.1
  368.8 421.8 all-reduce.2

commit v8 on v7

--- a/solution.py
+++ b/solution.py
@@ -275,16 +275,12 @@
     if own:
         norms = norm_rows(xn_ref, nn_ref)
     for g in range(n_grp):
-        vec = soft((g - 3) % n_grp)
         sc = scores((g - 2) % n_grp)
-        vec = vec + rope((g - 1) % n_grp)
-        if own:
-            vec += norms[g * len(norms) // n_grp:(g + 1) * len(norms) // n_grp]
-        vec += back(g)
         gr = grads(g)
+        nm = norms[g * len(norms) // n_grp:(g + 1) * len(norms) // n_grp] if own else []
         for _, f in gr[:2]:
             f()
-        weave(vec, sc + gr[2:] + proj(g))
+        weave(soft((g - 3) % n_grp), rope((g - 1) % n_grp) + nm, back(g), sc + gr[2:] + proj(g))
 
     for dst, src in ((o_out, o_ref), (dq_out, dq_ref), (dk_out, dk_ref), (dv_out, dv_ref)):
         dst[0] = src[...]
@@ -757,12 +753,11 @@
     return SimpleNamespace(norm=norm_rows, proj=proj, rope=rope, scores=scores, soft=soft, grads=grads, back=back)
 
 
-def attn_tick(st, g, n_grp):
-    vec = st.soft((g - 3) % n_grp) + st.rope((g - 1) % n_grp) + st.back(g)
+def attn_tick(st, g, n_grp, more=()):
     gr = st.grads(g)
     for _, f in gr[:2]:
         f()
-    weave(vec, st.scores((g - 2) % n_grp) + gr[2:] + st.proj(g))
+    weave(st.soft((g - 3) % n_grp), st.rope((g - 1) % n_grp), st.back(g), st.scores((g - 2) % n_grp) + gr[2:] + st.proj(g) + list(more))
 
 
 def attn_scratch(seq, n_grp):
@@ -787,6 +782,9 @@
     )
 
 
+EARLY = 4
+
+
 def tail_kernel(seq, n_grp, rows, keys, sel_ref, n_in, dy_in, cos_in, sin_in, x_in, dyx_in, gain_ref, qg_ref, kg_ref, dgq_own, dgk_own, *refs):
     own_w, oth_w, own_a = refs[:4], refs[4:8], refs[8:12]
     y_out, dx_out, sums_out = refs[12:15]
@@ -804,7 +802,10 @@
 
     def fetch(row):
         return [pltpu.make_async_copy(src.at[me, pl.ds(row * seq, seq), :], dst.at[me], r.sem.at[8 + k])
-                for k, (src, dst) in enumerate(zip(own_a, (r.oc, r.dqc, r.dkc, r.dvc)))]
+                for k, (src, dst) in enumerate(zip(own_a[1:], (r.dqc, r.dkc, r.dvc)))]
+
+    def fetch_o(row):
+        return pltpu.make_async_copy(own_a[0].at[me, pl.ds(row * seq, seq), :], r.o_next, r.sem.at[11])
 
     weights = (r.wq_all, r.wk_all, r.wv_all, r.wo_all)
     theirs = [pltpu.make_async_copy(oth_w[k], dst.at[oth], r.sem.at[4 + k]) for k, dst in enumerate(weights)]
@@ -812,16 +813,23 @@
 
     @pl.when(step == 0)
     def _():
-        for c in theirs + mine:
+        for c in theirs + mine[3:] + mine[:3]:
             c.start()
         r.dg[...] = jnp.zeros_like(r.dg)
-        for c in theirs:
+        r.oc[...] = jnp.zeros_like(r.oc)
+        for c in theirs + mine[3:]:
             c.wait()
 
     @pl.when(step > 0)
     def _():
         for c in fetch(step - 1):
             c.start()
+        fetch_o(step - 1).wait()
+        r.oc[me] = r.o_next[...]
+
+    @pl.when(step < rows)
+    def _():
+        fetch_o(step).start()
 
     CR, NC = 32, 256
     nn = D // NC
@@ -853,28 +861,29 @@
     def first(n, c):
         def run():
             cols = slice(n * NC, (n + 1) * NC)
-            w = r.dn[c:c + CR, cols] * (x_in[c:c + CR, cols].astype(F32) * wide(r.xs[0, c:c + CR, :]))
+            inv = wide(r.xs[0, c:c + CR, :])
+            d = r.dn[c:c + CR, cols]
+            w = d * (x_in[c:c + CR, cols].astype(F32) * inv)
             r.dg[:, cols] += jnp.sum(w.reshape(CR // 8, 8, NC), axis=0)
             w = w * gain_ref[0:1, cols]
             r.xs[1, c:c + CR, :] += w[:, :HD] + w[:, HD:]
+            r.dn[c:c + CR, cols] = dyx_in[c:c + CR, cols].astype(F32) + inv * (d * gain_ref[0:1, cols])
 
         return (1, run)
 
     def mean(c):
         def run():
-            r.xs[2, c:c + CR, :] = jnp.broadcast_to(jnp.sum(r.xs[1, c:c + CR, :], axis=-1, keepdims=True) * (1.0 / D), (CR, HD))
+            inv = r.xs[0, c:c + CR, :]
+            r.xs[2, c:c + CR, :] = jnp.sum(r.xs[1, c:c + CR, :], axis=-1, keepdims=True) * (1.0 / D) * (inv * inv)
 
         return (0.2, run)
 
     def second(n, c):
         def run():
             cols = slice(n * NC, (n + 1) * NC)
-            inv = wide(r.xs[0, c:c + CR, :])
-            xh = x_in[c:c + CR, cols].astype(F32) * inv
-            e = r.dn[c:c + CR, cols] * gain_ref[0:1, cols]
-            dx_out[c:c + CR, cols] = (dyx_in[c:c + CR, cols].astype(F32) + inv * (e - xh * wide(r.xs[2, c:c + CR, :]))).astype(BF16)
-
-        return (1.2, run)
+            dx_out[c:c + CR, cols] = (r.dn[c:c + CR, cols] - x_in[c:c + CR, cols].astype(F32) * wide(r.xs[2, c:c + CR, :])).astype(BF16)
+
+        return (1, run)
 
     def y_dot(n):
         def run():
@@ -887,14 +896,15 @@
     r.tab[2:4] = r.tab[0:2]
     r.tab[0] = cos_in[...]
     r.tab[1] = sin_in[...]
+    yd = [y_dot(n) for n in range(nn)]
     for g in range(n_grp):
-        attn_tick(st, g, n_grp)
+        attn_tick(st, g, n_grp, yd[:EARLY] if g == n_grp - 1 else [])
     for acc in (r.dgq, r.dgk):
         acc[...] = jnp.where(step > 0, acc[...], 0.0)
 
     @pl.when(step == 0)
     def _():
-        for c in mine:
+        for c in mine[:3]:
             c.wait()
 
     @pl.when(step > 0)
@@ -902,15 +912,14 @@
         for c in fetch(step - 1):
             c.wait()
         dn = [dn_dot(n) for n in range(nn)]
-        yd = [y_dot(n) for n in range(nn)]
         for _, f in dn[:1]:
             f()
         weave([stat(c) for c in lines], dn[1:2])
         for n in range(2, nn):
             weave([first(n - 2, c) for c in lines], dn[n:n + 1])
-        weave([first(nn - 2, c) for c in lines], yd[:1])
-        weave([first(nn - 1, c) for c in lines] + [mean(c) for c in lines], yd[1:2])
-        weave([second(n, c) for n in range(nn) for c in lines], yd[2:])
+        weave([first(nn - 2, c) for c in lines], yd[EARLY:EARLY + 1])
+        weave([first(nn - 1, c) for c in lines] + [mean(c) for c in lines], yd[EARLY + 1:EARLY + 2])
+        weave([second(n, c) for n in range(nn) for c in lines], yd[EARLY + 2:])
 
     @pl.when(step == rows)
     def _():
@@ -931,7 +940,7 @@
     scratch.update(
         wq_all=pltpu.VMEM((2, D, nq), BF16), wk_all=pltpu.VMEM((2, D, nk), BF16), wv_all=pltpu.VMEM((2, D, nk), BF16), wo_all=pltpu.VMEM((2, nq, D), BF16),
         dn=pltpu.VMEM((seq, D), F32), oc=pltpu.VMEM((2, seq, nq), BF16), dqc=pltpu.VMEM((2, seq, nq), BF16), dkc=pltpu.VMEM((2, seq, nk), BF16), dvc=pltpu.VMEM((2, seq, nk), BF16),
-        xs=pltpu.VMEM((3, seq, HD), F32), dg=pltpu.VMEM((8, D), F32), dgq=pltpu.VMEM((8, HD), F32), dgk=pltpu.VMEM((8, HD), F32), sem=pltpu.SemaphoreType.DMA((12,)))
+        o_next=pltpu.VMEM((seq, nq), BF16), xs=pltpu.VMEM((3, seq, HD), F32), dg=pltpu.VMEM((8, D), F32), dgq=pltpu.VMEM((8, HD), F32), dgk=pltpu.VMEM((8, HD), F32), sem=pltpu.SemaphoreType.DMA((12,)))
     flops = 2 * T * D * (nq + 2 * nk + nq) * 3 + 12 * T * nq * seq
     return pl.pallas_call(
         functools.partial(tail_kernel, seq, n_grp, rows, tuple(scratch)),

time: 851 us -> 833 us (0.979)
  Pallas kernels: 833 us -> 814 us
    pallas_call x1, Pallas kernels: 445 us -> 432 us  [tail_call(): pl.pallas_call(functools.partial(tail_kernel, seq, n_grp, rows, tuple(scr...]
where the time goes in v8:
time: 833 us
  Pallas kernels  814 us (98%)
  between operations  14.2 us (2%)
    pallas_call x1, Pallas kernels, tail_call(): pl.pallas_call(functools.partial(tail_kernel, seq, n_grp, rows, tuple(scr...  432 us
    pallas_call x1, Pallas kernels, attn_call(): pl.pallas_call(functools.partial(attn_kernel, own, seq, n_grp), grid_spec...  216 us
    pallas_call x2, Pallas kernels, dw_call(): pl.pallas_call(functools.partial(dw_kernel, len(bs), gathered is not None...  130 us
    pallas_call x1, Pallas kernels, copy_call(): pl.pallas_call(functools.partial(copy_kernel, len(arrays)), grid=(steps,)...  18 us
  transfers between devices with their start and end apart: 2, of which 0 were waited for; matrix products, arithmetic and copies ran while one was open for 0% of the time, Pallas kernels for 89%

profile of v8, /device:TPU:0, one launch (start us, length us, event | category | flops | bytes accessed | tf_op | source)
XLA Modules:
  0.0 832.6 jit_solution(10455369217165184312)
XLA Ops:
  7.2 0.0 all-gather.2.cloned.1.call-start
  7.2 0.6 maximum_bitcast_fusion.freq_ref
  7.8 9.4 %pre.1 = (f32[4,192,2048]{2,1,0:T(8,128)}, f32[8192,128]{1,0:T(8,128)}, f32[8192,128]{1,0:T(8,128)}) custom-call(s32[1]{0:T(128)} %bitcast.3.sel_ref, bf16[2048,1024]{1,0:T(8,128)(2,1)} %refs_0_.1, bf16[2048,512]{1,0:T(8,128)(2,1)} %refs_1_.1, bf16[2048,512]{1,0:T(8,128)(2,1)} %refs_2_.1, bf16[1024,2048]{1,0:T(8,128)(2,1)} %refs_3_.1, s32[32,256]{1,0:T(8,128)} %pos_ref.1, ...), custom_call_target="tpu_custom_call" | custom-call | flops 31457280 | bytes 17825792 | tf_op jit(solution)/shard_map/pre/pallas_call | solution.py:391
  17.2 0.0 copy-start.2
  17.2 0.0 copy-start.3
  17.2 0.0 all-gather.2.cloned.1.call-update
  17.3 0.0 all-reduce.3.cloned.1.call-start
  17.3 0.6 copy-done.1
  17.9 0.6 reshape.79
  18.5 0.0 copy-done.3
  18.5 0.5 bitcast_convert_fusion
  19.0 215.8 %attn_own.1 = (bf16[8192,2048]{1,0:T(8,128)(2,1)}, bf16[2,8192,1024]{2,1,0:T(8,128)(2,1)}, bf16[2,8192,1024]{2,1,0:T(8,128)(2,1)}, bf16[2,8192,512]{2,1,0:T(8,12...) custom-call(s32[1]{0:T(128)} %bitcast.sel_ref, bf16[8192,2048]{1,0:T(8,128)(2,1)} %bitcast.21, ...), custom_call_target="tpu_custom_call" | custom-call | flops 128849018880 | bytes 150994944 | tf_op jit(solution)/shard_map/attn_own/pallas_call | solution.py:321
  234.8 82.6 %shard_map.170 = (f32[2048,1024]{1,0:T(8,128)}, f32[2048,512]{1,0:T(8,128)}, f32[2048,512]{1,0:T(8,128)}) custom-call(s32[1]{0:T(128)} %bitcast.sel_ref, bf16[8192,2048]{1,0:T(8,128)(2,1)} %get-tuple-element.39.n_in.a_ref, bf16[2,8192,1024]{2,1,0:T(8,128)(2,1)} %get-tuple-element.48.refs_9_.refs_0_, ...), custom_call_target="tpu_custom_call" | custom-call | flops 68719476736 | bytes 83886080 | tf_op jit(solution)/shard_map/pallas_call | solution.py:470
  317.4 0.0 all-gather.2.cloned.1.call-done.refs_1_
  317.4 47.0 %shard_map.169 = (f32[1024,2048]{1,0:T(8,128)}, bf16[2048,1024]{1,0:T(8,128)(2,1)}, bf16[2048,512]{1,0:T(8,128)(2,1)}, bf16[2048,512]{1,0:T(8,128)(2,1)}, bf16[1024,2048]{1,0:T(8,128)(2,1)}) custom-call(s32[1]{0:T(128)} %bitcast.sel_ref, bf16[2,8192,1024]{2,1,0:T(8,128)(2,1)} %get-tuple-element.42.a_ref.refs_8_, bf16[8192,2048]{1,0:T(8,128)(2,1)} %bitcast.25, ...), custom_call_target="tpu_custom_call" | custom-call | flops 34359738368 | bytes 58720256 | tf_op jit(solution)/shard_map/pallas_call | solution.py:470
  364.4 0.0 all-reduce.3.cloned.1.call-update
  364.4 432.1 %tail.1 = (bf16[8192,2048]{1,0:T(8,128)(2,1)}, bf16[8192,2048]{1,0:T(8,128)(2,1)}, f32[8,2304]{1,0:T(8,128)}) custom-call(s32[1]{0:T(128)} %bitcast.sel_ref, bf16[8192,2048]{1,0:T(8,128)(2,1)} %get-tuple-element.39.n_in.a_ref, bf16[8192,2048]{1,0:T(8,128)(2,1)} %bitcast.26, f32[8192,128]{1,0:T(8,128)} %get-tuple-element.37.refs_3_.cos_in, ...), custom_call_target="tpu_custom_call" | custom-call | flops 335007449088 | bytes 234881024 | tf_op jit(solution)/shard_map/tail/pallas_call | solution.py:945
  796.5 9.6 %small_sum.1 = (f32[1,2048]{1,0:T(1,128)}, f32[1,128]{1,0:T(1,128)}, f32[1,128]{1,0:T(1,128)}) custom-call(f32[8,2304]{1,0:T(8,128)} %get-tuple-element.61.part_ref), custom_call_target="tpu_custom_call" | custom-call | flops 73728 | bytes 589824 | tf_op jit(solution)/shard_map/small_sum/pallas_call | solution.py:515
  806.1 0.0 all-reduce.3.cloned.1.call-done
  806.1 18.0 %results.1 = (f32[1024,2048]{1,0:T(8,128)}, f32[2048,1024]{1,0:T(8,128)}, f32[2048,512]{1,0:T(8,128)}, f32[2048,512]{1,0:T(8,128)}) custom-call(f32[1024,2048]{1,0:T(8,128)} %get-tuple-element.65.refs_0_, f32[2048,1024]{1,0:T(8,128)} %get-tuple-element.66.refs_1_, f32[2048,512]{1,0:T(8,128)} %get-tuple-element.67.refs_2_, f32[2048,512]{1,0:T(8,128)} %get-tuple-element.68.refs_3_), custom_call_target="tpu_custom_call" | custom-call | bytes 50331648 | tf_op jit(solution)/shard_map/results/pallas_call | solution.py:534
  824.1 0.5 copy.26
  824.6 0.0 copy-done.4
  824.6 0.5 copy.27
  825.1 0.6 copy.28
  (8 shorter events, 0.0 us)
Async XLA Ops:
  7.2 310.2 %all-gather.2.cloned.1.call-start = ((), (), s32[]{:S(2)}) async-start(), calls=%async_computation | async-start | bytes 56623104 | tf_op jit(solution)/shard_map/all_gather | solution.py:977
  17.2 0.7 copy-start.1
  17.2 1.3 copy-start.2
  17.2 1.3 copy-start.3
  17.3 788.8 %all-reduce.3.cloned.1.call-start = ((), (), s32[]{:S(2)}) async-start(), calls=%async_computation.1 | async-start | bytes 50331648 | tf_op jit(solution)/shard_map/psum | solution.py:985
  806.1 18.0 %copy-start.5 = (f32[1,128]{1,0:T(1,128)S(1)}, f32[1,128]{1,0:T(1,128)}, u32[]{:S(2)}) copy-start(f32[1,128]{1,0:T(1,128)} %get-tuple-element.62) | copy-start | bytes 1540
  806.1 18.5 %copy-start.4 = (f32[1,128]{1,0:T(1,128)S(1)}, f32[1,128]{1,0:T(1,128)}, u32[]{:S(2)}) copy-start(f32[1,128]{1,0:T(1,128)} %get-tuple-element.63) | copy-start | bytes 1540
  806.1 19.0 %copy-start = (f32[1,2048]{1,0:T(1,128)S(1)}, f32[1,2048]{1,0:T(1,128)}, u32[]{:S(2)}) copy-start(f32[1,2048]{1,0:T(1,128)} %get-tuple-element.64) | copy-start | bytes 24580
Sparse Core Ops, SparseCore 0:
  17.4 229.3 all-gather.1
  364.5 421.6 all-reduce.2

commit v9 on v8

--- a/solution.py
+++ b/solution.py
@@ -40,8 +40,8 @@
 def attn_kernel(own, seq, n_grp, sel_ref, *refs):
     if own:
         (x0_ref, xn_ref, dy_ref, cos_ref, sin_ref, gain_ref, qg_ref, kg_ref, wq_ref, wk_ref, wv_ref, wo_ref,
-         n_out, o_out, dq_out, dk_out, dv_out, dgq_out, dgk_out) = refs[:19]
-        refs = refs[19:]
+         n_out, o_out, dq_out, dk_out, dv_out, dgq_out, dgk_out, dwo_out) = refs[:20]
+        refs = refs[20:]
     else:
         nin_ref, dy_ref, cos_ref, sin_ref, qg_ref, kg_ref, wq_ref, wk_ref, wv_ref, wo_ref, _, _, _, _, o_out, dq_out, dk_out, dv_out = refs[:18]
         refs = refs[18:]
@@ -49,7 +49,7 @@
     (wot_ref, qnew_ref, knew_ref, vnew_ref, raw_ref, inv_ref, rot_ref, do_ref, v_ref, s_ref, dp_ref, p_ref, ds_ref, dkf_ref, dqf_ref, st_ref,
      tab_ref, o_ref, dq_ref, dk_ref, dv_ref) = refs[:21]
     if own:
-        n_ref, nn_ref, dgq_ref, dgk_ref = refs[21:]
+        n_ref, nn_ref, dgq_ref, dgk_ref, acc_ref, ot_ref, dyp_ref, sem = refs[21:]
     half = seq // 2
     scale = HD ** -0.5
     log2e = 1.4426950408889634
@@ -257,6 +257,18 @@
             return (0.5, run)
 
         return [f(h, c) for f in (turn, out) for h in (0, 1, 2) for c in range(0, seq, CH)]
+
+    def flip(c):
+        def run():
+            ot_ref[c:c + 256, :] = o_ref[:, c:c + 256].T
+
+        return (0.1, run)
+
+    def dwo(c):
+        def run():
+            acc_ref[:, c:c + 256] += dot(ot_ref[...], dyp_ref[:, c:c + 256])
+
+        return (0.5, run)
 
     @pl.when(step == 0)
     def _():
@@ -280,7 +292,10 @@
         nm = norms[g * len(norms) // n_grp:(g + 1) * len(norms) // n_grp] if own else []
         for _, f in gr[:2]:
             f()
-        weave(soft((g - 3) % n_grp), rope((g - 1) % n_grp) + nm, back(g), sc + gr[2:] + proj(g))
+        late = []
+        if own and g == n_grp - 1:
+            late = [flip(c) for c in range(0, ot_ref.shape[0], 256)], [dwo(c) for c in range(0, acc_ref.shape[1], 256)]
+        weave(soft((g - 3) % n_grp), rope((g - 1) % n_grp) + nm, back(g), sc + gr[2:] + (late[0] + proj(g) + late[1] if late else proj(g)))
 
     for dst, src in ((o_out, o_ref), (dq_out, dq_ref), (dk_out, dk_ref), (dv_out, dv_ref)):
         dst[0] = src[...]
@@ -291,6 +306,19 @@
         for dst, acc in ((dgq_out, dgq_ref), (dgk_out, dgk_ref)):
             acc[...] = jnp.where(keep, acc[...], 0.0)
             dst[...] = acc[...]
+        dyp_ref[...] = dy_ref[...]
+
+        @pl.when(step == 0)
+        def _():
+            @pl.loop(0, acc_ref.shape[0] // 64)
+            def _(j):
+                acc_ref[pl.ds(pl.multiple_of(j * 64, 64), 64), :] = jnp.zeros((64, acc_ref.shape[1]), F32)
+
+        @pl.when(step == pl.num_programs(0) - 1)
+        def _():
+            c = pltpu.make_async_copy(acc_ref, dwo_out, sem)
+            c.start()
+            c.wait()
 
 
 def attn_call(own, sel, x, dy, cosd, sind, gain, qg, kg, wq, wk, wv, wo, prev=None, seq=256):
@@ -310,8 +338,8 @@
     if own:
         in_specs = [const(seq, D), nxt(D)] + mid + [const(1, D)] + tail
         args = [x, x, dy, cosd, sind, gain, qg, kg, wq, wk, wv, wo]
-        shapes = [jax.ShapeDtypeStruct((T, D), BF16)] + shapes + [jax.ShapeDtypeStruct((8, HD), F32)] * 2
-        specs = [now(D)] + specs + [pl.BlockSpec((8, HD), lambda i, s: (0, 0))] * 2
+        shapes = [jax.ShapeDtypeStruct((T, D), BF16)] + shapes + [jax.ShapeDtypeStruct((8, HD), F32)] * 2 + [jax.ShapeDtypeStruct((nq, D), F32)]
+        specs = [now(D)] + specs + [pl.BlockSpec((8, HD), lambda i, s: (0, 0))] * 2 + [pl.BlockSpec(memory_space=pl.ANY)]
     else:
         in_specs = [now(D)] + mid + tail + [pl.BlockSpec(memory_space=pl.ANY)] * 4
         args = [x, dy, cosd, sind, qg, kg, wq, wk, wv, wo]
@@ -344,11 +372,11 @@
                 pltpu.VMEM((6, 2 * seq, HD), F32),
                 pltpu.VMEM((4, seq, HD), F32),
             ] + [pltpu.VMEM((seq, c), BF16) for c in (nq, nq, nk, nk)]
-            + ([pltpu.VMEM((seq, D), BF16)] * 2 + [pltpu.VMEM((8, HD), F32)] * 2 if own else []),
+            + ([pltpu.VMEM((seq, D), BF16)] * 2 + [pltpu.VMEM((8, HD), F32)] * 2 + [pltpu.VMEM((nq, D), F32), pltpu.VMEM((nq, seq), BF16), pltpu.VMEM((seq, D), BF16), pltpu.SemaphoreType.DMA] if own else []),
         ),
         out_shape=shapes,
         input_output_aliases=aliases,
-        compiler_params=pltpu.CompilerParams(dimension_semantics=("arbitrary",), vmem_limit_bytes=56 << 20),
+        compiler_params=pltpu.CompilerParams(dimension_semantics=("arbitrary",), vmem_limit_bytes=62 << 20),
         cost_estimate=pl.CostEstimate(flops=flops, bytes_accessed=T * D * 6 + T * (2 * nq + 2 * nk) * 2, transcendentals=T * nq * 2),
         name="attn_own" if own else "attn_other",
     )(sel, *args)
@@ -504,7 +532,6 @@
     total = slots[lax.rem(me + n, n)]
     for a in range(1, n):
         total = total + slots[lax.rem(me + n - a, n)]
-    total = jnp.sum(total, axis=0, keepdims=True)
     at = 0
     for out, w in zip(outs, widths):
         out[...] = total[:, at:at + w]
@@ -524,20 +551,34 @@
     )(part)
 
 
-def copy_kernel(n, *refs):
-    for src, dst in zip(refs[:n], refs[n:]):
-        dst[...] = src[...]
-
-
-def copy_call(arrays, steps=8):
-    specs = [pl.BlockSpec((a.shape[0] // steps, a.shape[1]), lambda i: (i, 0)) for a in arrays]
+def copy_kernel(n, cuts, *refs):
+    srcs, dsts, bufs, (in_sem, out_sem) = refs[:n], refs[n:2 * n], refs[2 * n:3 * n], refs[3 * n:]
+    ins, outs = [], []
+    for a, (src, dst, buf) in enumerate(zip(srcs, dsts, bufs)):
+        rows = src.shape[0] // cuts
+        for j in range(cuts):
+            part = pl.ds(j * rows, rows)
+            ins.append(pltpu.make_async_copy(src.at[part], buf.at[part], in_sem.at[a, j]))
+            outs.append(pltpu.make_async_copy(buf.at[part], dst.at[part], out_sem.at[a, j]))
+    for c in ins:
+        c.start()
+    for c, d in zip(ins, outs):
+        c.wait()
+        d.start()
+    for d in outs:
+        d.wait()
+
+
+def copy_call(arrays, cuts=4):
+    n = len(arrays)
+    hbm = [pl.BlockSpec(memory_space=pl.ANY)] * n
     return pl.pallas_call(
-        functools.partial(copy_kernel, len(arrays)),
-        grid=(steps,),
-        in_specs=specs,
-        out_specs=specs,
+        functools.partial(copy_kernel, n, cuts),
+        in_specs=hbm,
+        out_specs=hbm,
         out_shape=[jax.ShapeDtypeStruct(a.shape, a.dtype) for a in arrays],
-        compiler_params=pltpu.CompilerParams(dimension_semantics=("arbitrary",), vmem_limit_bytes=60 << 20),
+        scratch_shapes=[pltpu.VMEM(a.shape, a.dtype) for a in arrays] + [pltpu.SemaphoreType.DMA((n, cuts))] * 2,
+        compiler_params=pltpu.CompilerParams(vmem_limit_bytes=60 << 20),
         cost_estimate=pl.CostEstimate(flops=0, bytes_accessed=8 * sum(a.size for a in arrays), transcendentals=0),
         name="results",
     )(*arrays)
@@ -923,9 +964,10 @@
 
     @pl.when(step == rows)
     def _():
-        sums_out[:, 0:D] = r.dg[...]
-        sums_out[:, D:D + HD] = r.dgq[...] + dgq_own[...]
-        sums_out[:, D + HD:] = r.dgk[...] + dgk_own[...]
+        at = 0
+        for part in (r.dg[...], r.dgq[...] + dgq_own[...], r.dgk[...] + dgk_own[...]):
+            sums_out[:, at:at + part.shape[1]] = jnp.sum(part, axis=0, keepdims=True)
+            at += part.shape[1]
 
 
 def tail_call(sel, n, x, dy, cosd, sind, o, dq, dk, dv, gain, qg, kg, dgq, dgk, own, oth, seq=256):
@@ -948,10 +990,10 @@
             num_scalar_prefetch=1,
             grid=(rows + 1,),
             in_specs=[lag(0, D), lag(0, D), lag(0, HD), lag(0, HD), lag(1, D), lag(1, D), const(1, D), const(1, HD), const(1, HD), const(8, HD), const(8, HD)] + [hbm] * 12,
-            out_specs=[lag(1, D), lag(1, D), pl.BlockSpec((8, D + 2 * HD), lambda i, s: (0, 0))],
+            out_specs=[lag(1, D), lag(1, D), pl.BlockSpec((1, D + 2 * HD), lambda i, s: (0, 0))],
             scratch_shapes=list(scratch.values()),
         ),
-        out_shape=[jax.ShapeDtypeStruct((T, D), BF16)] * 2 + [jax.ShapeDtypeStruct((8, D + 2 * HD), F32)],
+        out_shape=[jax.ShapeDtypeStruct((T, D), BF16)] * 2 + [jax.ShapeDtypeStruct((1, D + 2 * HD), F32)],
         compiler_params=pltpu.CompilerParams(dimension_semantics=("arbitrary",), vmem_limit_bytes=67043328),
         cost_estimate=pl.CostEstimate(flops=flops, bytes_accessed=T * D * 14, transcendentals=T * nq * 2),
         name="tail",
@@ -979,9 +1021,8 @@
         gain = g_attn.astype(F32).reshape(1, D)
         qg, kg = q_gain.astype(F32).reshape(1, HD), k_gain.astype(F32).reshape(1, HD)
 
-        n, o, dq, dk, dv, dgq, dgk = attn_call(True, own, x, dy, cosd, sind, gain, qg, kg, w_q, w_k, w_v, w_o, seq=n_seq)
-        dw_q, dw_k, dw_v = dw_call(own, n, [dq, dk, dv], 512)
-        dw_o, *theirs = dw_call(own, o, [dy], 1024, gathered=gathered, nk=nk)
+        n, o, dq, dk, dv, dgq, dgk, dw_o = attn_call(True, own, x, dy, cosd, sind, gain, qg, kg, w_q, w_k, w_v, w_o, seq=n_seq)
+        dw_q, dw_k, dw_v, *theirs = dw_call(own, n, [dq, dk, dv], 512, gathered=gathered, nk=nk)
         dw_o, dw_q, dw_k, dw_v = lax.psum((dw_o, dw_q, dw_k, dw_v), "dp")
 
         y, dx, sums = tail_call(own, n, x, dy, cosd, sind, o, dq, dk, dv, gain, qg, kg, dgq, dgk, (w_q, w_k, w_v, w_o), theirs, seq=n_seq)

time: 833 us -> 830 us (level)
    pallas_call x2 -> x1, Pallas kernels: 130 us -> 84.6 us  [dw_call(): pl.pallas_call(functools.partial(dw_kernel, len(bs), gathered is not None...]
    pallas_call x1, Pallas kernels: 216 us -> 260 us  [attn_call(): pl.pallas_call(functools.partial(attn_kernel, own, seq, n_grp), grid_spec...]
  transfers between devices with their start and end apart: 2 -> 2, of which waited for: 0 -> 0; matrix products, arithmetic and copies ran while one was open for 0% -> 0% of each run, Pallas kernels for 89% -> 84%
where the time goes in v9:
time: 830 us
  Pallas kernels  812 us (98%)
  between operations  14.2 us (2%)
    pallas_call x1, Pallas kernels, tail_call(): pl.pallas_call(functools.partial(tail_kernel, seq, n_grp, rows, tuple(scr...  433 us
    pallas_call x1, Pallas kernels, attn_call(): pl.pallas_call(functools.partial(attn_kernel, own, seq, n_grp), grid_spec...  260 us
    pallas_call x1, Pallas kernels, dw_call(): pl.pallas_call(functools.partial(dw_kernel, len(bs), gathered is not None...  84.6 us
    pallas_call x1, Pallas kernels, copy_call(): pl.pallas_call(functools.partial(copy_kernel, n, cuts), in_specs=hbm, out...  17.2 us
  transfers between devices with their start and end apart: 2, of which 0 were waited for; matrix products, arithmetic and copies ran while one was open for 0% of the time, Pallas kernels for 84%

profile of v9, /device:TPU:0, one launch (start us, length us, event | category | flops | bytes accessed | tf_op | source)
XLA Modules:
  0.0 829.9 jit_solution(6457685300423884769)
XLA Ops:
  7.2 0.0 all-gather.2.cloned.1.call-start
  7.2 0.6 maximum_bitcast_fusion.freq_ref
  7.8 9.4 %pre.1 = (f32[4,192,2048]{2,1,0:T(8,128)}, f32[8192,128]{1,0:T(8,128)}, f32[8192,128]{1,0:T(8,128)}) custom-call(s32[1]{0:T(128)} %bitcast.3.sel_ref, bf16[2048,1024]{1,0:T(8,128)(2,1)} %refs_0_.1, bf16[2048,512]{1,0:T(8,128)(2,1)} %refs_1_.1, bf16[2048,512]{1,0:T(8,128)(2,1)} %refs_2_.1, bf16[1024,2048]{1,0:T(8,128)(2,1)} %refs_3_.1, s32[32,256]{1,0:T(8,128)} %pos_ref.1, ...), custom_call_target="tpu_custom_call" | custom-call | flops 31457280 | bytes 17825792 | tf_op jit(solution)/shard_map/pre/pallas_call | solution.py:419
  17.2 0.0 copy-start.2
  17.2 0.0 copy-start.3
  17.2 0.0 all-gather.2.cloned.1.call-update
  17.3 0.0 all-reduce.3.cloned.1.call-start
  17.3 0.6 copy-done.1
  17.9 0.6 reshape.79
  18.5 0.0 copy-done.2
  18.5 0.0 copy-done.3
  18.5 0.5 bitcast_convert_fusion
  19.0 260.3 %attn_own.1 = (bf16[8192,2048]{1,0:T(8,128)(2,1)}, bf16[2,8192,1024]{2,1,0:T(8,128)(2,1)}, bf16[2,8192,1024]{2,1,0:T(8,128)(2,1)}, bf16[2,8192,512]{2,1,0:T(8,12...) custom-call(s32[1]{0:T(128)} %bitcast.sel_ref, ...), custom_call_target="tpu_custom_call" | custom-call | flops 128849018880 | bytes 150994944 | tf_op jit(solution)/shard_map/attn_own/pallas_call | solution.py:349
  279.3 0.0 all-gather.2.cloned.1.call-done.refs_3_
  279.4 84.6 %shard_map.169 = (f32[2048,1024]{1,0:T(8,128)}, f32[2048,512]{1,0:T(8,128)}, f32[2048,512]{1,0:T(8,128)}, bf16[2048,1024]{1,0:T(8,128)(2,1)}, bf16[2048,512]{1,0...) custom-call(s32[1]{0:T(128)} %bitcast.sel_ref, bf16[8192,2048]{1,0:T(8,128)(2,1)} %get-tuple-element.39.a_ref.n_in, ...), custom_call_target="tpu_custom_call" | custom-call | flops 68719476736 | bytes 83886080 | tf_op jit(solution)/shard_map/pallas_call | solution.py:498
  363.9 0.0 all-reduce.3.cloned.1.call-update
  364.0 432.7 %tail.1 = (bf16[8192,2048]{1,0:T(8,128)(2,1)}, bf16[8192,2048]{1,0:T(8,128)(2,1)}, f32[1,2304]{1,0:T(1,128)}) custom-call(s32[1]{0:T(128)} %bitcast.sel_ref, bf16[8192,2048]{1,0:T(8,128)(2,1)} %get-tuple-element.39.a_ref.n_in, bf16[8192,2048]{1,0:T(8,128)(2,1)} %bitcast.25, f32[8192,128]{1,0:T(8,128)} %get-tuple-element.37.refs_3_.cos_in, ...), custom_call_target="tpu_custom_call" | custom-call | flops 335007449088 | bytes 234881024 | tf_op jit(solution)/shard_map/tail/pallas_call | solution.py:987
  796.7 7.4 small_sum.1
  804.1 0.0 all-reduce.3.cloned.1.call-done
  804.1 0.0 copy-start.5
  804.2 17.2 %results.1 = (f32[1024,2048]{1,0:T(8,128)}, f32[2048,1024]{1,0:T(8,128)}, f32[2048,512]{1,0:T(8,128)}, f32[2048,512]{1,0:T(8,128)}) custom-call(f32[1024,2048]{1,0:T(8,128)} %get-tuple-element.65.refs_0_, f32[2048,1024]{1,0:T(8,128)} %get-tuple-element.66.refs_1_, f32[2048,512]{1,0:T(8,128)} %get-tuple-element.67.refs_2_, f32[2048,512]{1,0:T(8,128)} %get-tuple-element.68.refs_3_), custom_call_target="tpu_custom_call" | custom-call | bytes 50331648 | tf_op jit(solution)/shard_map/results/pallas_call | solution.py:575
  821.4 0.5 copy.26
  821.9 0.5 copy.27
  822.4 0.6 copy.28
  (7 shorter events, 0.0 us)
Async XLA Ops:
  7.2 272.2 %all-gather.2.cloned.1.call-start = ((), (), s32[]{:S(2)}) async-start(), calls=%async_computation | async-start | bytes 56623104 | tf_op jit(solution)/shard_map/all_gather | solution.py:1019
  17.2 0.7 copy-start.1
  17.2 1.3 copy-start.2
  17.2 1.3 copy-start.3
  17.3 786.9 %all-reduce.3.cloned.1.call-start = ((), (), s32[]{:S(2)}) async-start(), calls=%async_computation.1 | async-start | bytes 50331648 | tf_op jit(solution)/shard_map/psum | solution.py:1026
  804.1 17.3 %copy-start.5 = (f32[1,128]{1,0:T(1,128)S(1)}, f32[1,128]{1,0:T(1,128)}, u32[]{:S(2)}) copy-start(f32[1,128]{1,0:T(1,128)} %get-tuple-element.62) | copy-start | bytes 1540
  804.1 17.8 %copy-start.4 = (f32[1,128]{1,0:T(1,128)S(1)}, f32[1,128]{1,0:T(1,128)}, u32[]{:S(2)}) copy-start(f32[1,128]{1,0:T(1,128)} %get-tuple-element.63) | copy-start | bytes 1540
  804.2 18.3 %copy-start = (f32[1,2048]{1,0:T(1,128)S(1)}, f32[1,2048]{1,0:T(1,128)}, u32[]{:S(2)}) copy-start(f32[1,2048]{1,0:T(1,128)} %get-tuple-element.64) | copy-start | bytes 24580
Sparse Core Ops, SparseCore 0:
  17.4 229.2 all-gather.1
  364.1 421.6 all-reduce.2

commit v10 on v9

--- a/solution.py
+++ b/solution.py
@@ -46,10 +46,10 @@
         nin_ref, dy_ref, cos_ref, sin_ref, qg_ref, kg_ref, wq_ref, wk_ref, wv_ref, wo_ref, _, _, _, _, o_out, dq_out, dk_out, dv_out = refs[:18]
         refs = refs[18:]
         n_ref = nin_ref
-    (wot_ref, qnew_ref, knew_ref, vnew_ref, raw_ref, inv_ref, rot_ref, do_ref, v_ref, s_ref, dp_ref, p_ref, ds_ref, dkf_ref, dqf_ref, st_ref,
-     tab_ref, o_ref, dq_ref, dk_ref, dv_ref) = refs[:21]
+    (qnew_ref, knew_ref, vnew_ref, raw_ref, inv_ref, rot_ref, do_ref, v_ref, s_ref, dp_ref, p_ref, ds_ref, dkf_ref, dqf_ref, st_ref,
+     tab_ref, o_ref, dq_ref, dk_ref, dv_ref) = refs[:20]
     if own:
-        n_ref, nn_ref, dgq_ref, dgk_ref, acc_ref, ot_ref, dyp_ref, sem = refs[21:]
+        n_ref, nn_ref, dgq_ref, dgk_ref, acc_ref, ot_ref, dyp_ref, sem = refs[20:]
     half = seq // 2
     scale = HD ** -0.5
     log2e = 1.4426950408889634
@@ -83,7 +83,7 @@
                 vnew_ref[g + h] = t[:, h * HD:(h + 1) * HD].astype(BF16)
 
         def do():
-            t = dot(dy_ref[...], wot_ref[:, g * 2 * HD:(g + 1) * 2 * HD])
+            t = dot(dy_ref[...], wo_ref[g * 2 * HD:(g + 1) * 2 * HD, :], NT)
             for h in range(2):
                 do_ref[g, h * half:(h + 1) * half, :] = t[:half, h * HD:(h + 1) * HD].astype(BF16)
                 do_ref[g, seq + h * half:seq + (h + 1) * half, :] = t[half:, h * HD:(h + 1) * HD].astype(BF16)
@@ -258,26 +258,22 @@
 
         return [f(h, c) for f in (turn, out) for h in (0, 1, 2) for c in range(0, seq, CH)]
 
-    def flip(c):
-        def run():
-            ot_ref[c:c + 256, :] = o_ref[:, c:c + 256].T
-
-        return (0.1, run)
-
-    def dwo(c):
-        def run():
-            acc_ref[:, c:c + 256] += dot(ot_ref[...], dyp_ref[:, c:c + 256])
-
-        return (0.5, run)
+    def dwo(g):
+        rows = slice(g * 2 * HD, (g + 1) * 2 * HD)
+
+        def flip():
+            ot_ref[rows, :] = o_ref[:, rows].T
+
+        def part(c):
+            def run():
+                acc_ref[rows, c:c + 512] += dot(ot_ref[rows, :], dyp_ref[:, c:c + 512])
+
+            return (0.25, run)
+
+        return [(0.1, flip)] + [part(c) for c in range(0, acc_ref.shape[1], 512)]
 
     @pl.when(step == 0)
     def _():
-        @pl.loop(0, wo_ref.shape[0] // 256)
-        def _(j):
-            c = pl.ds(pl.multiple_of(j * 256, 256), 256)
-            for d in range(0, wo_ref.shape[1], 256):
-                wot_ref[d:d + 256, c] = wo_ref[c, d:d + 256].T
-
         if own:
             weave(norm_rows(x0_ref, n_ref))
 
@@ -292,10 +288,7 @@
         nm = norms[g * len(norms) // n_grp:(g + 1) * len(norms) // n_grp] if own else []
         for _, f in gr[:2]:
             f()
-        late = []
-        if own and g == n_grp - 1:
-            late = [flip(c) for c in range(0, ot_ref.shape[0], 256)], [dwo(c) for c in range(0, acc_ref.shape[1], 256)]
-        weave(soft((g - 3) % n_grp), rope((g - 1) % n_grp) + nm, back(g), sc + gr[2:] + (late[0] + proj(g) + late[1] if late else proj(g)))
+        weave(soft((g - 3) % n_grp), rope((g - 1) % n_grp) + nm, back(g), sc + gr[2:] + (dwo(g - 1) if own and g > 0 else []) + proj(g) + (dwo(g) if own and g == n_grp - 1 else []))
 
     for dst, src in ((o_out, o_ref), (dq_out, dq_ref), (dk_out, dk_ref), (dv_out, dv_ref)):
         dst[0] = src[...]
@@ -354,7 +347,6 @@
             in_specs=in_specs,
             out_specs=specs,
             scratch_shapes=[
-                pltpu.VMEM((D, nq), BF16),
                 pltpu.VMEM((2, 2, seq, HD), BF16),
                 pltpu.VMEM((n_grp, seq, HD), BF16),
                 pltpu.VMEM((n_grp, seq, HD), BF16),

time: 830 us -> 825 us (level)
  no operation moved by 1% of the time
where the time goes in v10:
time: 825 us
  Pallas kernels  806 us (98%)
  between operations  14.2 us (2%)
    pallas_call x1, Pallas kernels, tail_call(): pl.pallas_call(functools.partial(tail_kernel, seq, n_grp, rows, tuple(scr...  433 us
    pallas_call x1, Pallas kernels, attn_call(): pl.pallas_call(functools.partial(attn_kernel, own, seq, n_grp), grid_spec...  255 us
    pallas_call x1, Pallas kernels, dw_call(): pl.pallas_call(functools.partial(dw_kernel, len(bs), gathered is not None...  84.4 us
    pallas_call x1, Pallas kernels, copy_call(): pl.pallas_call(functools.partial(copy_kernel, n, cuts), in_specs=hbm, out...  17.2 us
  transfers between devices with their start and end apart: 2, of which 0 were waited for; matrix products, arithmetic and copies ran while one was open for 0% of the time, Pallas kernels for 84%

profile of v10, /device:TPU:0, one launch (start us, length us, event | category | flops | bytes accessed | tf_op | source)
XLA Modules:
  0.0 824.7 jit_solution(3777591360193068997)
XLA Ops:
  7.2 0.0 all-gather.2.cloned.1.call-start
  7.2 0.6 maximum_bitcast_fusion.freq_ref
  7.8 9.4 %pre.1 = (f32[4,192,2048]{2,1,0:T(8,128)}, f32[8192,128]{1,0:T(8,128)}, f32[8192,128]{1,0:T(8,128)}) custom-call(s32[1]{0:T(128)} %bitcast.3.sel_ref, bf16[2048,1024]{1,0:T(8,128)(2,1)} %refs_0_.1, bf16[2048,512]{1,0:T(8,128)(2,1)} %refs_1_.1, bf16[2048,512]{1,0:T(8,128)(2,1)} %refs_2_.1, bf16[1024,2048]{1,0:T(8,128)(2,1)} %refs_3_.1, s32[32,256]{1,0:T(8,128)} %pos_ref.1, ...), custom_call_target="tpu_custom_call" | custom-call | flops 31457280 | bytes 17825792 | tf_op jit(solution)/shard_map/pre/pallas_call | solution.py:411
  17.2 0.0 copy-start.2
  17.2 0.0 copy-start.3
  17.2 0.0 all-gather.2.cloned.1.call-update
  17.3 0.0 all-reduce.3.cloned.1.call-start
  17.3 0.6 copy-done.1
  17.9 0.6 reshape.79
  18.5 0.0 copy-done.3
  18.5 0.5 bitcast_convert_fusion
  19.0 255.3 %attn_own.1 = (bf16[8192,2048]{1,0:T(8,128)(2,1)}, bf16[2,8192,1024]{2,1,0:T(8,128)(2,1)}, bf16[2,8192,1024]{2,1,0:T(8,128)(2,1)}, bf16[2,8192,512]{2,1,0:T(8,12...) custom-call(s32[1]{0:T(128)} %bitcast.sel_ref, ...), custom_call_target="tpu_custom_call" | custom-call | flops 128849018880 | bytes 150994944 | tf_op jit(solution)/shard_map/attn_own/pallas_call | solution.py:342
  274.4 0.0 all-gather.2.cloned.1.call-done.refs_3_
  274.4 84.4 %shard_map.169 = (f32[2048,1024]{1,0:T(8,128)}, f32[2048,512]{1,0:T(8,128)}, f32[2048,512]{1,0:T(8,128)}, bf16[2048,1024]{1,0:T(8,128)(2,1)}, bf16[2048,512]{1,0...) custom-call(s32[1]{0:T(128)} %bitcast.sel_ref, bf16[8192,2048]{1,0:T(8,128)(2,1)} %get-tuple-element.39.a_ref.n_in, ...), custom_call_target="tpu_custom_call" | custom-call | flops 68719476736 | bytes 83886080 | tf_op jit(solution)/shard_map/pallas_call | solution.py:490
  358.8 0.0 all-reduce.3.cloned.1.call-update
  358.8 432.7 %tail.1 = (bf16[8192,2048]{1,0:T(8,128)(2,1)}, bf16[8192,2048]{1,0:T(8,128)(2,1)}, f32[1,2304]{1,0:T(1,128)}) custom-call(s32[1]{0:T(128)} %bitcast.sel_ref, bf16[8192,2048]{1,0:T(8,128)(2,1)} %get-tuple-element.39.a_ref.n_in, bf16[8192,2048]{1,0:T(8,128)(2,1)} %bitcast.25, f32[8192,128]{1,0:T(8,128)} %get-tuple-element.37.refs_3_.cos_in, ...), custom_call_target="tpu_custom_call" | custom-call | flops 335007449088 | bytes 234881024 | tf_op jit(solution)/shard_map/tail/pallas_call | solution.py:979
  791.5 7.5 small_sum.1
  798.9 0.0 all-reduce.3.cloned.1.call-done
  799.0 0.0 copy-start.5
  799.0 0.0 copy-start.4
  799.0 17.2 %results.1 = (f32[1024,2048]{1,0:T(8,128)}, f32[2048,1024]{1,0:T(8,128)}, f32[2048,512]{1,0:T(8,128)}, f32[2048,512]{1,0:T(8,128)}) custom-call(f32[1024,2048]{1,0:T(8,128)} %get-tuple-element.65.refs_0_, f32[2048,1024]{1,0:T(8,128)} %get-tuple-element.66.refs_1_, f32[2048,512]{1,0:T(8,128)} %get-tuple-element.67.refs_2_, f32[2048,512]{1,0:T(8,128)} %get-tuple-element.68.refs_3_), custom_call_target="tpu_custom_call" | custom-call | bytes 50331648 | tf_op jit(solution)/shard_map/results/pallas_call | solution.py:567
  816.3 0.5 copy.26
  816.8 0.5 copy.27
  817.3 0.6 copy.28
  (7 shorter events, 0.0 us)
Async XLA Ops:
  7.2 267.2 %all-gather.2.cloned.1.call-start = ((), (), s32[]{:S(2)}) async-start(), calls=%async_computation | async-start | bytes 56623104 | tf_op jit(solution)/shard_map/all_gather | solution.py:1011
  17.2 0.7 copy-start.1
  17.2 1.3 copy-start.2
  17.2 1.3 copy-start.3
  17.3 781.7 %all-reduce.3.cloned.1.call-start = ((), (), s32[]{:S(2)}) async-start(), calls=%async_computation.1 | async-start | bytes 50331648 | tf_op jit(solution)/shard_map/psum | solution.py:1018
  799.0 17.3 %copy-start.5 = (f32[1,128]{1,0:T(1,128)S(1)}, f32[1,128]{1,0:T(1,128)}, u32[]{:S(2)}) copy-start(f32[1,128]{1,0:T(1,128)} %get-tuple-element.62) | copy-start | bytes 1540
  799.0 17.8 %copy-start.4 = (f32[1,128]{1,0:T(1,128)S(1)}, f32[1,128]{1,0:T(1,128)}, u32[]{:S(2)}) copy-start(f32[1,128]{1,0:T(1,128)} %get-tuple-element.63) | copy-start | bytes 1540
  799.0 18.3 %copy-start = (f32[1,2048]{1,0:T(1,128)S(1)}, f32[1,2048]{1,0:T(1,128)}, u32[]{:S(2)}) copy-start(f32[1,2048]{1,0:T(1,128)} %get-tuple-element.64) | copy-start | bytes 24580
Sparse Core Ops, SparseCore 0:
  17.4 229.3 all-gather.1
  358.9 421.6 all-reduce.2

commit v11 on v10

--- a/solution.py
+++ b/solution.py
@@ -285,7 +285,7 @@
     for g in range(n_grp):
         sc = scores((g - 2) % n_grp)
         gr = grads(g)
-        nm = norms[g * len(norms) // n_grp:(g + 1) * len(norms) // n_grp] if own else []
+        nm = (norms[:4], norms[4:], [], [])[g] if own else []
         for _, f in gr[:2]:
             f()
         weave(soft((g - 3) % n_grp), rope((g - 1) % n_grp) + nm, back(g), sc + gr[2:] + (dwo(g - 1) if own and g > 0 else []) + proj(g) + (dwo(g) if own and g == n_grp - 1 else []))
@@ -380,12 +380,12 @@
     out_ref[0, 0:d, nq:nq + nk] = k_ref[...].astype(F32)
     out_ref[0, 0:d, nq + nk:] = v_ref[...].astype(F32)
     out_ref[0, d:, :] = o_ref[...].astype(F32)
-    n, seq = pos_ref.shape
-    lane = lax.broadcasted_iota(jnp.int32, (HD, HD), 1)
+    n, seq = pos_ref.shape[1:]
+    low = lax.broadcasted_iota(jnp.int32, (HD, HD), 1) < HD // 2
     for r in range(n):
-        for h in range(seq // HD):
-            p = pos_ref[r:r + 1, h * HD:(h + 1) * HD].astype(F32)
-            a = jnp.broadcast_to(p, (HD, HD)).T * freq_ref[0:1, :]
+        for h in range(0, seq // HD, 2):
+            p = [jnp.broadcast_to(pos_ref[0, r:r + 1, (h + b) * HD:(h + b + 1) * HD].astype(F32), (HD, HD)).T for b in range(2)]
+            a = jnp.where(low, p[0], p[1]) * freq_ref[0:1, :]
             k = jnp.round(a * 0.6366197723675814)
             x = ((a - k * 1.5703125) - k * 4.837512969970703125e-4) - k * 7.549789948768648e-8
             z = x * x
@@ -394,12 +394,16 @@
             q = k.astype(jnp.int32)
             odd = (q & 1) == 1
             co, si = jnp.where(odd, s, c), jnp.where(odd, c, s)
-            rows = slice((r * (seq // HD) + h) * HD, (r * (seq // HD) + h + 1) * HD)
-            cos_ref[rows, :] = jnp.where(((q + 1) & 2) == 0, co, -co)
-            sin_ref[rows, :] = jnp.where(((q & 2) == 0) == (lane >= HD // 2), si, -si)
-
-
-def pre_call(part, w_q, w_k, w_v, w_o, positions, parts=2, cuts=4):
+            co = jnp.where(((q + 1) & 2) == 0, co, -co)
+            si = jnp.where((q & 2) == 0, si, -si)
+            cx, sx = pltpu.roll(co, HD // 2, 1), pltpu.roll(si, HD // 2, 1)
+            for b in range(2):
+                at = (r * (seq // HD) + h + b) * HD
+                cos_ref[at:at + HD, :] = jnp.where(low, co, cx) if b == 0 else jnp.where(low, cx, co)
+                sin_ref[at:at + HD, :] = jnp.where(low, -si, sx) if b == 0 else jnp.where(low, -sx, si)
+
+
+def pre_call(part, w_q, w_k, w_v, w_o, positions, parts=2, cuts=8):
     D, nq = w_q.shape
     n, seq = positions.shape
     rows = n // cuts
@@ -413,14 +417,14 @@
         grid_spec=pltpu.PrefetchScalarGridSpec(
             num_scalar_prefetch=1,
             grid=(cuts,),
-            in_specs=[spec(w) for w in (w_q, w_k, w_v, w_o)] + [pl.BlockSpec((rows, seq), lambda i, s: (i, 0)), pl.BlockSpec((1, HD), lambda i, s: (0, 0))],
+            in_specs=[spec(w) for w in (w_q, w_k, w_v, w_o)] + [pl.BlockSpec((1, rows, seq), lambda i, s: (i, 0, 0)), pl.BlockSpec((1, HD), lambda i, s: (0, 0))],
             out_specs=[pl.BlockSpec((1, r, D), lambda i, s: (i, 0, 0)), table, table],
         ),
         out_shape=[jax.ShapeDtypeStruct((cuts, r, D), F32)] + [jax.ShapeDtypeStruct((n * seq, HD), F32)] * 2,
         compiler_params=pltpu.CompilerParams(dimension_semantics=("arbitrary",), vmem_limit_bytes=60 << 20),
         cost_estimate=pl.CostEstimate(flops=n * seq * HD * 30, bytes_accessed=cuts * r * D * 6 + n * seq * HD * 8, transcendentals=0),
         name="pre",
-    )(part, w_q, w_k, w_v, w_o, positions, freq)
+    )(part, w_q, w_k, w_v, w_o, positions.reshape(cuts, rows, seq), freq)
 
 
 def dw_kernel(n_b, unpack, sel_ref, a_ref, *refs):

time: 825 us -> 826 us (level)
  no operation moved by 1% of the time
where the time goes in v11:
time: 826 us
  Pallas kernels  806 us (98%)
  between operations  14.2 us (2%)
    pallas_call x1, Pallas kernels, tail_call(): pl.pallas_call(functools.partial(tail_kernel, seq, n_grp, rows, tuple(scr...  433 us
    pallas_call x1, Pallas kernels, attn_call(): pl.pallas_call(functools.partial(attn_kernel, own, seq, n_grp), grid_spec...  255 us
    pallas_call x1, Pallas kernels, dw_call(): pl.pallas_call(functools.partial(dw_kernel, len(bs), gathered is not None...  84.3 us
    pallas_call x1, Pallas kernels, copy_call(): pl.pallas_call(functools.partial(copy_kernel, n, cuts), in_specs=hbm, out...  17.2 us
  transfers between devices with their start and end apart: 2, of which 0 were waited for; matrix products, arithmetic and copies ran while one was open for 0% of the time, Pallas kernels for 84%

profile of v11, /device:TPU:0, one launch (start us, length us, event | category | flops | bytes accessed | tf_op | source)
XLA Modules:
  0.0 826.0 jit_solution(16564928688065324127)
XLA Ops:
  7.2 0.0 all-gather.2.cloned.1.call-start
  7.2 0.6 maximum_bitcast_fusion.freq_ref
  7.8 1.4 reshape.70.pos_ref
  9.2 10.0 %pre.1 = (f32[8,96,2048]{2,1,0:T(8,128)}, f32[8192,128]{1,0:T(8,128)}, f32[8192,128]{1,0:T(8,128)}) custom-call(s32[1]{0:T(128)} %bitcast.3.sel_ref, bf16[2048,1024]{1,0:T(8,128)(2,1)} %refs_0_.1, bf16[2048,512]{1,0:T(8,128)(2,1)} %refs_1_.1, bf16[2048,512]{1,0:T(8,128)(2,1)} %refs_2_.1, bf16[1024,2048]{1,0:T(8,128)(2,1)} %refs_3_.1, ...), custom_call_target="tpu_custom_call" | custom-call | flops 31457280 | bytes 17825792 | tf_op jit(solution)/shard_map/pre/pallas_call | solution.py:415
  19.2 0.0 copy-start.3
  19.2 0.0 all-gather.2.cloned.1.call-update
  19.3 0.0 all-reduce.3.cloned.1.call-start
  19.3 0.6 copy-done.1
  19.9 0.6 reshape.83
  20.5 0.5 bitcast_convert_fusion
  21.0 254.7 %attn_own.1 = (bf16[8192,2048]{1,0:T(8,128)(2,1)}, bf16[2,8192,1024]{2,1,0:T(8,128)(2,1)}, bf16[2,8192,1024]{2,1,0:T(8,128)(2,1)}, bf16[2,8192,512]{2,1,0:T(8,12...) custom-call(s32[1]{0:T(128)} %bitcast.sel_ref, ...), custom_call_target="tpu_custom_call" | custom-call | flops 128849018880 | bytes 150994944 | tf_op jit(solution)/shard_map/attn_own/pallas_call | solution.py:342
  275.8 0.0 all-gather.2.cloned.1.call-done.refs_3_
  275.8 84.3 %shard_map.169 = (f32[2048,1024]{1,0:T(8,128)}, f32[2048,512]{1,0:T(8,128)}, f32[2048,512]{1,0:T(8,128)}, bf16[2048,1024]{1,0:T(8,128)(2,1)}, bf16[2048,512]{1,0...) custom-call(s32[1]{0:T(128)} %bitcast.sel_ref, bf16[8192,2048]{1,0:T(8,128)(2,1)} %get-tuple-element.39.a_ref.n_in, ...), custom_call_target="tpu_custom_call" | custom-call | flops 68719476736 | bytes 83886080 | tf_op jit(solution)/shard_map/pallas_call | solution.py:494
  360.2 0.0 all-reduce.3.cloned.1.call-update
  360.2 432.7 %tail.1 = (bf16[8192,2048]{1,0:T(8,128)(2,1)}, bf16[8192,2048]{1,0:T(8,128)(2,1)}, f32[1,2304]{1,0:T(1,128)}) custom-call(s32[1]{0:T(128)} %bitcast.sel_ref, bf16[8192,2048]{1,0:T(8,128)(2,1)} %get-tuple-element.39.a_ref.n_in, bf16[8192,2048]{1,0:T(8,128)(2,1)} %bitcast.25, f32[8192,128]{1,0:T(8,128)} %get-tuple-element.37.refs_3_.cos_in, ...), custom_call_target="tpu_custom_call" | custom-call | flops 335007449088 | bytes 234881024 | tf_op jit(solution)/shard_map/tail/pallas_call | solution.py:983
  792.9 7.3 small_sum.1
  800.2 0.0 all-reduce.3.cloned.1.call-done
  800.3 17.2 %results.1 = (f32[1024,2048]{1,0:T(8,128)}, f32[2048,1024]{1,0:T(8,128)}, f32[2048,512]{1,0:T(8,128)}, f32[2048,512]{1,0:T(8,128)}) custom-call(f32[1024,2048]{1,0:T(8,128)} %get-tuple-element.65.refs_0_, f32[2048,1024]{1,0:T(8,128)} %get-tuple-element.66.refs_1_, f32[2048,512]{1,0:T(8,128)} %get-tuple-element.67.refs_2_, f32[2048,512]{1,0:T(8,128)} %get-tuple-element.68.refs_3_), custom_call_target="tpu_custom_call" | custom-call | bytes 50331648 | tf_op jit(solution)/shard_map/results/pallas_call | solution.py:571
  817.5 0.0 copy-done.5
  817.5 0.5 copy.26
  818.0 0.0 copy-done.4
  818.0 0.5 copy.27
  818.5 0.0 copy-done
  818.5 0.6 copy.28
  (8 shorter events, 0.0 us)
Async XLA Ops:
  7.2 268.6 %all-gather.2.cloned.1.call-start = ((), (), s32[]{:S(2)}) async-start(), calls=%async_computation | async-start | bytes 56623104 | tf_op jit(solution)/shard_map/all_gather | solution.py:1015
  19.2 0.7 copy-start.1
  19.2 1.3 copy-start.2
  19.2 1.3 copy-start.3
  19.3 781.0 %all-reduce.3.cloned.1.call-start = ((), (), s32[]{:S(2)}) async-start(), calls=%async_computation.1 | async-start | bytes 50331648 | tf_op jit(solution)/shard_map/psum | solution.py:1022
  800.2 17.3 %copy-start.5 = (f32[1,128]{1,0:T(1,128)S(1)}, f32[1,128]{1,0:T(1,128)}, u32[]{:S(2)}) copy-start(f32[1,128]{1,0:T(1,128)} %get-tuple-element.62) | copy-start | bytes 1540
  800.2 17.8 %copy-start.4 = (f32[1,128]{1,0:T(1,128)S(1)}, f32[1,128]{1,0:T(1,128)}, u32[]{:S(2)}) copy-start(f32[1,128]{1,0:T(1,128)} %get-tuple-element.63) | copy-start | bytes 1540
  800.2 18.3 %copy-start = (f32[1,2048]{1,0:T(1,128)S(1)}, f32[1,2048]{1,0:T(1,128)}, u32[]{:S(2)}) copy-start(f32[1,2048]{1,0:T(1,128)} %get-tuple-element.64) | copy-start | bytes 24580
Sparse Core Ops, SparseCore 0:
  19.4 229.2 all-gather.1
  360.3 421.5 all-reduce.2

commit v12 on v11

--- a/solution.py
+++ b/solution.py
@@ -380,11 +380,11 @@
     out_ref[0, 0:d, nq:nq + nk] = k_ref[...].astype(F32)
     out_ref[0, 0:d, nq + nk:] = v_ref[...].astype(F32)
     out_ref[0, d:, :] = o_ref[...].astype(F32)
-    n, seq = pos_ref.shape[1:]
+    n, seq = pos_ref.shape
     low = lax.broadcasted_iota(jnp.int32, (HD, HD), 1) < HD // 2
     for r in range(n):
         for h in range(0, seq // HD, 2):
-            p = [jnp.broadcast_to(pos_ref[0, r:r + 1, (h + b) * HD:(h + b + 1) * HD].astype(F32), (HD, HD)).T for b in range(2)]
+            p = [jnp.broadcast_to(pos_ref[r:r + 1, (h + b) * HD:(h + b + 1) * HD].astype(F32), (HD, HD)).T for b in range(2)]
             a = jnp.where(low, p[0], p[1]) * freq_ref[0:1, :]
             k = jnp.round(a * 0.6366197723675814)
             x = ((a - k * 1.5703125) - k * 4.837512969970703125e-4) - k * 7.549789948768648e-8
@@ -403,7 +403,7 @@
                 sin_ref[at:at + HD, :] = jnp.where(low, -si, sx) if b == 0 else jnp.where(low, -sx, si)
 
 
-def pre_call(part, w_q, w_k, w_v, w_o, positions, parts=2, cuts=8):
+def pre_call(part, w_q, w_k, w_v, w_o, positions, parts=2, cuts=4):
     D, nq = w_q.shape
     n, seq = positions.shape
     rows = n // cuts
@@ -417,14 +417,14 @@
         grid_spec=pltpu.PrefetchScalarGridSpec(
             num_scalar_prefetch=1,
             grid=(cuts,),
-            in_specs=[spec(w) for w in (w_q, w_k, w_v, w_o)] + [pl.BlockSpec((1, rows, seq), lambda i, s: (i, 0, 0)), pl.BlockSpec((1, HD), lambda i, s: (0, 0))],
+            in_specs=[spec(w) for w in (w_q, w_k, w_v, w_o)] + [pl.BlockSpec((rows, seq), lambda i, s: (i, 0)), pl.BlockSpec((1, HD), lambda i, s: (0, 0))],
             out_specs=[pl.BlockSpec((1, r, D), lambda i, s: (i, 0, 0)), table, table],
         ),
         out_shape=[jax.ShapeDtypeStruct((cuts, r, D), F32)] + [jax.ShapeDtypeStruct((n * seq, HD), F32)] * 2,
         compiler_params=pltpu.CompilerParams(dimension_semantics=("arbitrary",), vmem_limit_bytes=60 << 20),
         cost_estimate=pl.CostEstimate(flops=n * seq * HD * 30, bytes_accessed=cuts * r * D * 6 + n * seq * HD * 8, transcendentals=0),
         name="pre",
-    )(part, w_q, w_k, w_v, w_o, positions.reshape(cuts, rows, seq), freq)
+    )(part, w_q, w_k, w_v, w_o, positions, freq)
 
 
 def dw_kernel(n_b, unpack, sel_ref, a_ref, *refs):

time: 826 us -> 823 us (level)
  no operation moved by 1% of the time
where the time goes in v12:
time: 823 us
  Pallas kernels  805 us (98%)
  between operations  14.2 us (2%)
    pallas_call x1, Pallas kernels, tail_call(): pl.pallas_call(functools.partial(tail_kernel, seq, n_grp, rows, tuple(scr...  433 us
    pallas_call x1, Pallas kernels, attn_call(): pl.pallas_call(functools.partial(attn_kernel, own, seq, n_grp), grid_spec...  255 us
    pallas_call x1, Pallas kernels, dw_call(): pl.pallas_call(functools.partial(dw_kernel, len(bs), gathered is not None...  84.3 us
    pallas_call x1, Pallas kernels, copy_call(): pl.pallas_call(functools.partial(copy_kernel, n, cuts), in_specs=hbm, out...  17.2 us
  transfers between devices with their start and end apart: 2, of which 0 were waited for; matrix products, arithmetic and copies ran while one was open for 0% of the time, Pallas kernels for 84%

profile of v12, /device:TPU:0, one launch (start us, length us, event | category | flops | bytes accessed | tf_op | source)
XLA Modules:
  0.0 823.2 jit_solution(4130657915644913271)
XLA Ops:
  7.2 0.0 all-gather.2.cloned.1.call-start
  7.2 0.6 maximum_bitcast_fusion.freq_ref
  7.8 8.6 %pre.1 = (f32[4,192,2048]{2,1,0:T(8,128)}, f32[8192,128]{1,0:T(8,128)}, f32[8192,128]{1,0:T(8,128)}) custom-call(s32[1]{0:T(128)} %bitcast.3.sel_ref, bf16[2048,1024]{1,0:T(8,128)(2,1)} %refs_0_.1, bf16[2048,512]{1,0:T(8,128)(2,1)} %refs_1_.1, bf16[2048,512]{1,0:T(8,128)(2,1)} %refs_2_.1, bf16[1024,2048]{1,0:T(8,128)(2,1)} %refs_3_.1, s32[32,256]{1,0:T(8,128)} %pos_ref.1, ...), custom_call_target="tpu_custom_call" | custom-call | flops 31457280 | bytes 17825792 | tf_op jit(solution)/shard_map/pre/pallas_call | solution.py:415
  16.4 0.0 copy-start.2
  16.4 0.0 copy-start.3
  16.4 0.0 all-gather.2.cloned.1.call-update
  16.5 0.0 all-reduce.3.cloned.1.call-start
  16.5 0.6 copy-done.1
  17.1 0.6 reshape.79
  17.7 0.0 copy-done.2
  17.7 0.0 copy-done.3
  17.7 0.5 bitcast_convert_fusion
  18.2 254.7 %attn_own.1 = (bf16[8192,2048]{1,0:T(8,128)(2,1)}, bf16[2,8192,1024]{2,1,0:T(8,128)(2,1)}, bf16[2,8192,1024]{2,1,0:T(8,128)(2,1)}, bf16[2,8192,512]{2,1,0:T(8,12...) custom-call(s32[1]{0:T(128)} %bitcast.sel_ref, ...), custom_call_target="tpu_custom_call" | custom-call | flops 128849018880 | bytes 150994944 | tf_op jit(solution)/shard_map/attn_own/pallas_call | solution.py:342
  273.0 0.0 all-gather.2.cloned.1.call-done.refs_3_
  273.0 84.3 %shard_map.169 = (f32[2048,1024]{1,0:T(8,128)}, f32[2048,512]{1,0:T(8,128)}, f32[2048,512]{1,0:T(8,128)}, bf16[2048,1024]{1,0:T(8,128)(2,1)}, bf16[2048,512]{1,0...) custom-call(s32[1]{0:T(128)} %bitcast.sel_ref, bf16[8192,2048]{1,0:T(8,128)(2,1)} %get-tuple-element.39.a_ref.n_in, ...), custom_call_target="tpu_custom_call" | custom-call | flops 68719476736 | bytes 83886080 | tf_op jit(solution)/shard_map/pallas_call | solution.py:494
  357.3 0.0 all-reduce.3.cloned.1.call-update
  357.4 432.7 %tail.1 = (bf16[8192,2048]{1,0:T(8,128)(2,1)}, bf16[8192,2048]{1,0:T(8,128)(2,1)}, f32[1,2304]{1,0:T(1,128)}) custom-call(s32[1]{0:T(128)} %bitcast.sel_ref, bf16[8192,2048]{1,0:T(8,128)(2,1)} %get-tuple-element.39.a_ref.n_in, bf16[8192,2048]{1,0:T(8,128)(2,1)} %bitcast.25, f32[8192,128]{1,0:T(8,128)} %get-tuple-element.37.refs_3_.cos_in, ...), custom_call_target="tpu_custom_call" | custom-call | flops 335007449088 | bytes 234881024 | tf_op jit(solution)/shard_map/tail/pallas_call | solution.py:983
  790.1 7.3 small_sum.1
  797.4 0.0 all-reduce.3.cloned.1.call-done
  797.4 0.0 copy-start.5
  797.4 17.2 %results.1 = (f32[1024,2048]{1,0:T(8,128)}, f32[2048,1024]{1,0:T(8,128)}, f32[2048,512]{1,0:T(8,128)}, f32[2048,512]{1,0:T(8,128)}) custom-call(f32[1024,2048]{1,0:T(8,128)} %get-tuple-element.65.refs_0_, f32[2048,1024]{1,0:T(8,128)} %get-tuple-element.66.refs_1_, f32[2048,512]{1,0:T(8,128)} %get-tuple-element.67.refs_2_, f32[2048,512]{1,0:T(8,128)} %get-tuple-element.68.refs_3_), custom_call_target="tpu_custom_call" | custom-call | bytes 50331648 | tf_op jit(solution)/shard_map/results/pallas_call | solution.py:571
  814.7 0.5 copy.26
  815.2 0.5 copy.27
  815.7 0.6 copy.28
  (7 shorter events, 0.0 us)
Async XLA Ops:
  7.2 265.8 %all-gather.2.cloned.1.call-start = ((), (), s32[]{:S(2)}) async-start(), calls=%async_computation | async-start | bytes 56623104 | tf_op jit(solution)/shard_map/all_gather | solution.py:1015
  16.4 0.7 copy-start.1
  16.4 1.3 copy-start.2
  16.4 1.3 copy-start.3
  16.5 780.9 %all-reduce.3.cloned.1.call-start = ((), (), s32[]{:S(2)}) async-start(), calls=%async_computation.1 | async-start | bytes 50331648 | tf_op jit(solution)/shard_map/psum | solution.py:1022
  797.4 17.3 %copy-start.5 = (f32[1,128]{1,0:T(1,128)S(1)}, f32[1,128]{1,0:T(1,128)}, u32[]{:S(2)}) copy-start(f32[1,128]{1,0:T(1,128)} %get-tuple-element.62) | copy-start | bytes 1540
  797.4 17.8 %copy-start.4 = (f32[1,128]{1,0:T(1,128)S(1)}, f32[1,128]{1,0:T(1,128)}, u32[]{:S(2)}) copy-start(f32[1,128]{1,0:T(1,128)} %get-tuple-element.63) | copy-start | bytes 1540
  797.4 18.3 %copy-start = (f32[1,2048]{1,0:T(1,128)S(1)}, f32[1,2048]{1,0:T(1,128)}, u32[]{:S(2)}) copy-start(f32[1,2048]{1,0:T(1,128)} %get-tuple-element.64) | copy-start | bytes 24580
Sparse Core Ops, SparseCore 0:
  16.6 229.3 all-gather.1
  357.5 421.6 all-reduce.2
